TPU v7x, 128 devices: a whole 4x4x4 slice. The times are simulated.
128 devices in a mesh: dp: 64 (over y, x, z_hi, core), mp: 2 (over z_lo).
Axes of the slice: x: 4, y: 4, z: 4 (z_hi: 2, z_lo: 2; z = z_hi * 2 + z_lo), core: 2. Of those that a mesh axis runs over, the one named last changes fastest.
Arguments:
- pooled_grad: bfloat16 [16384, 128, 128], P(('dp', 'mp')), may hold values from -6 to 6
- bag_lengths: int32 [16384, 128], P(('dp', 'mp')), may hold values from 1 to 4
- bag_rows: int32 [16384, 128, 4], P(('dp', 'mp')), may hold values from 0 to 2047
- table_rows: float32 [128, 2048, 128], P('dp', 'mp'), may hold values from -6 to 6
- row_accum: float32 [128, 2048], P('dp', 'mp'), may hold values from 0.01 to 1
- dense_input: bfloat16 [16384, 1024], P(('dp', 'mp')), may hold values from -6 to 6
- dense_cotangent: bfloat16 [16384, 1024], P(('dp', 'mp')), may hold values from -0.046875 to 0.046875
Outputs:
- new_rows: float32 [128, 2048, 128], P('dp', 'mp')
- new_accum: float32 [128, 2048], P('dp', 'mp')
- dense_grad: float32 [1024, 1024], replicated
Inputs may be any that keep to these rules, and one draw needn't show every extreme that they name: `bag_rows`: a row number of the whole table.
All inputs are finite; a program needn't handle non-finite values.
Results may differ from a plain program's by a relative error of at most 0.0003.
Values may be sent and summed in bfloat16 or wider, within the bound.
No kernel may reach another device: no remote copies, remote signals or barrier semaphores. Data moves between devices by JAX's collectives and lax.ppermute only.
A program may use at most 128 MiB of HBM per device.

v0:
```python
import math

import jax
import jax.numpy as jnp
from jax import lax
from jax.sharding import PartitionSpec as P

learn_rate = 0.5


def in_one_piece(arrays, axis, split_dim, concat_dim, along):
    widths = [math.prod(a.shape[along:]) for a in arrays]
    both = jnp.concatenate(
        [a.reshape(*a.shape[:along], w) for a, w in zip(arrays, widths)], axis=along
    )
    whole = lax.all_to_all(both, axis, split_axis=split_dim, concat_axis=concat_dim, tiled=True)
    blocks = jnp.split(whole, [sum(widths[:k]) for k in range(1, len(widths))], axis=along)
    return tuple(
        (b.reshape(*whole.shape[:along], *a.shape[along:]) for a, b in zip(arrays, blocks))
    )


def in_blocks(value, dim, peers):
    before, after = (value.shape[:dim], value.shape[dim + 1 :])
    return jnp.moveaxis(value.reshape(*before, peers, -1, *after), dim, 0)


def sent_and_summed(value, axis, dim):
    blocks = in_blocks(value, dim, lax.axis_size(axis))
    arrived = lax.all_to_all(blocks, axis, split_axis=0, concat_axis=0, tiled=True)
    return arrived.sum(axis=0)


def grads_by_row(grads, lengths, looked, base_row, row_count):
    sample_count = grads.shape[0]
    tab_local = grads.shape[1]
    feat_width = grads.shape[2]
    slot_count = looked.shape[2]
    step = math.gcd(sample_count, max(8, (1 << 21) // row_count))
    turns = sample_count // step
    slot_iota = jnp.arange(slot_count, dtype=jnp.int32)
    target = jnp.where(slot_iota[None, None, :] < lengths[..., None], looked - base_row, -1)
    row_iota = jnp.arange(row_count, dtype=jnp.int32)
    results = []
    for table in range(tab_local):

        def add_block(turn, total):
            start = turn * step
            piece = lax.dynamic_slice_in_dim(grads, start, step, 0)[:, table, :]
            wanted = lax.dynamic_slice_in_dim(target, start, step, 0)[:, table, :]
            onehot = (wanted[:, 0, None] == row_iota[None, :]).astype(jnp.bfloat16)
            for slot in range(1, slot_count):
                onehot = onehot + (wanted[:, slot, None] == row_iota[None, :]).astype(jnp.bfloat16)
            return total + lax.dot_general(
                onehot, piece, (((0,), (0,)), ((), ())), preferred_element_type=jnp.float32
            )

        empty = jnp.zeros((row_count, feat_width), jnp.float32)
        results.append(lax.fori_loop(0, turns, add_block, empty))
    return jnp.stack(results, axis=0)


def per_device(
    pooled_grad, bag_lengths, bag_rows, table_rows, row_accum, dense_input, dense_cotangent
):
    local_dense = lax.dot_general(
        dense_input, dense_cotangent, (((0,), (0,)), ((), ())), preferred_element_type=jnp.float32
    )
    dense_grad = lax.psum(local_dense, ("dp", "mp"))
    mp_count = lax.axis_size("mp")
    rows_local = table_rows.shape[1]
    owned_grad, owned_lengths, owned_rows = (
        lax.all_to_all(pooled_grad, "dp", split_axis=1, concat_axis=0, tiled=True),
        *in_one_piece((bag_lengths, bag_rows), "dp", 1, 0, 2),
    )
    full_rows = rows_local * mp_count
    partial_value = grads_by_row(
        owned_grad, owned_lengths, owned_rows, jnp.zeros((), jnp.int32), full_rows
    )
    row_grad = sent_and_summed(partial_value, "mp", 1)
    new_accum = row_accum + jnp.mean(row_grad * row_grad, axis=-1)
    new_rows = table_rows - learn_rate * row_grad / jnp.sqrt(new_accum)[..., None]
    return (new_rows, new_accum, dense_grad)


def solution(mesh):
    in_specs = (
        P(("dp", "mp"), None, None),
        P(("dp", "mp"), None),
        P(("dp", "mp"), None, None),
        P("dp", "mp", None),
        P("dp", "mp"),
        P(("dp", "mp"), None),
        P(("dp", "mp"), None),
    )
    out_specs = (P("dp", "mp", None), P("dp", "mp"), P())
    return jax.shard_map(
        per_device, mesh=mesh, in_specs=in_specs, out_specs=out_specs, check_vma=False
    )
```

profile of v0, /device:TPU:1, one launch (start us, length us, event | category | flops | bytes accessed | tf_op | source)
XLA Modules:
  0.0 244.6 jit_solution(2633486620304057127)
XLA Ops:
  7.2 0.0 copy-start
  7.2 1.1 copy.21
  8.3 0.9 copy.20
  9.3 0.9 pad_add_fusion
  10.2 12.3 %all-to-all-start = ((s32[128,128,5]{0,2,1:T(8,128)}), s32[128,128,5]{0,2,1:T(8,128)S(1)}, u32[]{:S(2)}, u32[]{:S(2)}) async-start(s32[128,128,5]{0,2,1:T(8,128)} %pad_add_fusion), calls=%async_computation | async-start | bytes 1048576 | tf_op jit(solution)/shard_map/all_to_all | solution.py:16
  22.5 6.9 %copy.23 = bf16[128,128,128]{2,0,1:T(8,128)(2,1)} copy(bf16[128,128,128]{2,1,0:T(8,128)(2,1)} %param.11) | data formatting | bytes 8388608 | tf_op args[0]
  29.4 0.0 copy-start.1
  29.4 6.9 %all-to-all-done = s32[128,128,5]{0,2,1:T(8,128)S(1)} async-done(((s32[128,128,5]{0,2,1:T(8,128)}), s32[128,128,5]{0,2,1:T(8,128)S(1)}, u32[]{:S(2)}, u32[]{:S(2)}) %all-to-all-start) | async-done | bytes 327712 | tf_op jit(solution)/shard_map/all_to_all | solution.py:16
  36.3 5.8 %all-to-all-start.1 = ((bf16[128,128,128]{2,0,1:T(8,128)(2,1)}), bf16[128,128,128]{2,0,1:T(8,128)(2,1)}, u32[]{:S(2)}, u32[]{:S(2)}) async-start(bf16[128,128,128]{2,0,1:T(8,128)(2,1)} %copy.23), calls=%async_computation.1 | async-start | bytes 8388608 | tf_op jit(solution)/shard_map/all_to_all | solution.py:73
  42.1 0.2 all-reduce.2.cloned.1.call-start
  42.3 0.0 copy-done
  42.3 0.0 copy-done.1
  42.3 2.7 %fusion.47 = f32[1024,1024]{1,0:T(8,128)} fusion(bf16[128,1024]{1,0:T(8,128)(2,1)S(1)} %copy-done, bf16[128,1024]{1,0:T(8,128)(2,1)S(1)} %copy-done.1), kind=kOutput, calls=%fused_computation.52 | convolution fusion | flops 268435456 | bytes 4718592 | tf_op jit(solution)/shard_map/dot_general | solution.py:66
  45.0 0.0 all-reduce.2.cloned.1.call-update
  45.1 0.1 copy.22
  45.2 0.2 compare_select_fusion
  45.3 0.2 copy.25
  45.5 51.9 %all-to-all-done.1 = bf16[128,128,128]{2,0,1:T(8,128)(2,1)} async-done(((bf16[128,128,128]{2,0,1:T(8,128)(2,1)}), bf16[128,128,128]{2,0,1:T(8,128)(2,1)}, u32[]{:S(2)}, u32[]{:S(2)}) %all-to-all-start.1) | async-done | bytes 4194336 | tf_op jit(solution)/shard_map/all_to_all | solution.py:73
  97.4 4.8 %copy.24 = bf16[64,128,2,128]{3,1,0,2:T(8,128)(2,1)} copy(bf16[64,128,2,128]{3,1,2,0:T(8,128)(2,1)} %bitcast.8) | data formatting | bytes 8388608 | tf_op jit(solution)/shard_map/all_to_all | solution.py:73
  102.3 45.8 %while.31 = (s32[]{:T(128)}, f32[2048,128]{1,0:T(8,128)S(1)}, s32[8192,2,4]{0,2,1:T(4,128)S(1)}, bf16[8192,2,128]{2,0,1:T(8,128)(2,1)}, s32[]{:T(128)}, /*index=5*/s32[]{:T(128)}, s32[]{:T(128)}, s32[]{:T(128)}, s32[]{}) while((s32[]{:T(128)}, f32[2048,128]{1,0:T(8,128)S(1)}, s32[8192,2,4]{0,2,1:T(4,128)S(1)}, ...), condition=%wide.region_3.4_spmd.clone.clone, body=%wide.region_2.3_spmd.clone.clone.sunk | while | flops 570949632 | bytes 2441393 | solution.py:59
  102.3 5.7 %fusion.61 = f32[2048,128]{1,0:T(8,128)S(1)} fusion(s32[1024]{0:T(1024)S(1)} %bitcast.67, s32[1024]{0:T(1024)S(1)} %bitcast.68, s32[1024]{0:T(1024)S(1)} %bitcast.69, s32[1024]{0:T(1024)S(1)} %bitcast.66, f32[2048,128]{1,0:T(8,128)S(1)} %get-tuple-element.395, pred[]{:T(512)S(6)} %compare.7, bf16[8192,2,128]{2,0,1:T(8,128)(2,1)} %get-tuple-element.406, ...), kind=kOutput, calls=%fused_computation.38.clone.1 | convolution fusion | flops 570949632 | bytes 2375689 | tf_op jit(solution)/shard_map/while/body/eval_jaxpr/dot_general | solution.py:54
  108.0 5.6 %fusion.61 = f32[2048,128]{1,0:T(8,128)S(1)} fusion(s32[1024]{0:T(1024)S(1)} %bitcast.67, s32[1024]{0:T(1024)S(1)} %bitcast.68, s32[1024]{0:T(1024)S(1)} %bitcast.69, s32[1024]{0:T(1024)S(1)} %bitcast.66, f32[2048,128]{1,0:T(8,128)S(1)} %get-tuple-element.395, pred[]{:T(512)S(6)} %compare.7, bf16[8192,2,128]{2,0,1:T(8,128)(2,1)} %get-tuple-element.406, ...), kind=kOutput, calls=%fused_computation.38.clone.1 | convolution fusion | flops 570949632 | bytes 2375689 | tf_op jit(solution)/shard_map/while/body/eval_jaxpr/dot_general | solution.py:54
  113.7 5.7 %fusion.61 = f32[2048,128]{1,0:T(8,128)S(1)} fusion(s32[1024]{0:T(1024)S(1)} %bitcast.67, s32[1024]{0:T(1024)S(1)} %bitcast.68, s32[1024]{0:T(1024)S(1)} %bitcast.69, s32[1024]{0:T(1024)S(1)} %bitcast.66, f32[2048,128]{1,0:T(8,128)S(1)} %get-tuple-element.395, pred[]{:T(512)S(6)} %compare.7, bf16[8192,2,128]{2,0,1:T(8,128)(2,1)} %get-tuple-element.406, ...), kind=kOutput, calls=%fused_computation.38.clone.1 | convolution fusion | flops 570949632 | bytes 2375689 | tf_op jit(solution)/shard_map/while/body/eval_jaxpr/dot_general | solution.py:54
  119.5 5.7 %fusion.61 = f32[2048,128]{1,0:T(8,128)S(1)} fusion(s32[1024]{0:T(1024)S(1)} %bitcast.67, s32[1024]{0:T(1024)S(1)} %bitcast.68, s32[1024]{0:T(1024)S(1)} %bitcast.69, s32[1024]{0:T(1024)S(1)} %bitcast.66, f32[2048,128]{1,0:T(8,128)S(1)} %get-tuple-element.395, pred[]{:T(512)S(6)} %compare.7, bf16[8192,2,128]{2,0,1:T(8,128)(2,1)} %get-tuple-element.406, ...), kind=kOutput, calls=%fused_computation.38.clone.1 | convolution fusion | flops 570949632 | bytes 2375689 | tf_op jit(solution)/shard_map/while/body/eval_jaxpr/dot_general | solution.py:54
  125.2 5.7 %fusion.61 = f32[2048,128]{1,0:T(8,128)S(1)} fusion(s32[1024]{0:T(1024)S(1)} %bitcast.67, s32[1024]{0:T(1024)S(1)} %bitcast.68, s32[1024]{0:T(1024)S(1)} %bitcast.69, s32[1024]{0:T(1024)S(1)} %bitcast.66, f32[2048,128]{1,0:T(8,128)S(1)} %get-tuple-element.395, pred[]{:T(512)S(6)} %compare.7, bf16[8192,2,128]{2,0,1:T(8,128)(2,1)} %get-tuple-element.406, ...), kind=kOutput, calls=%fused_computation.38.clone.1 | convolution fusion | flops 570949632 | bytes 2375689 | tf_op jit(solution)/shard_map/while/body/eval_jaxpr/dot_general | solution.py:54
  130.9 5.7 %fusion.61 = f32[2048,128]{1,0:T(8,128)S(1)} fusion(s32[1024]{0:T(1024)S(1)} %bitcast.67, s32[1024]{0:T(1024)S(1)} %bitcast.68, s32[1024]{0:T(1024)S(1)} %bitcast.69, s32[1024]{0:T(1024)S(1)} %bitcast.66, f32[2048,128]{1,0:T(8,128)S(1)} %get-tuple-element.395, pred[]{:T(512)S(6)} %compare.7, bf16[8192,2,128]{2,0,1:T(8,128)(2,1)} %get-tuple-element.406, ...), kind=kOutput, calls=%fused_computation.38.clone.1 | convolution fusion | flops 570949632 | bytes 2375689 | tf_op jit(solution)/shard_map/while/body/eval_jaxpr/dot_general | solution.py:54
  136.6 5.6 %fusion.61 = f32[2048,128]{1,0:T(8,128)S(1)} fusion(s32[1024]{0:T(1024)S(1)} %bitcast.67, s32[1024]{0:T(1024)S(1)} %bitcast.68, s32[1024]{0:T(1024)S(1)} %bitcast.69, s32[1024]{0:T(1024)S(1)} %bitcast.66, f32[2048,128]{1,0:T(8,128)S(1)} %get-tuple-element.395, pred[]{:T(512)S(6)} %compare.7, bf16[8192,2,128]{2,0,1:T(8,128)(2,1)} %get-tuple-element.406, ...), kind=kOutput, calls=%fused_computation.38.clone.1 | convolution fusion | flops 570949632 | bytes 2375689 | tf_op jit(solution)/shard_map/while/body/eval_jaxpr/dot_general | solution.py:54
  142.4 5.6 %fusion.61 = f32[2048,128]{1,0:T(8,128)S(1)} fusion(s32[1024]{0:T(1024)S(1)} %bitcast.67, s32[1024]{0:T(1024)S(1)} %bitcast.68, s32[1024]{0:T(1024)S(1)} %bitcast.69, s32[1024]{0:T(1024)S(1)} %bitcast.66, f32[2048,128]{1,0:T(8,128)S(1)} %get-tuple-element.395, pred[]{:T(512)S(6)} %compare.7, bf16[8192,2,128]{2,0,1:T(8,128)(2,1)} %get-tuple-element.406, ...), kind=kOutput, calls=%fused_computation.38.clone.1 | convolution fusion | flops 570949632 | bytes 2375689 | tf_op jit(solution)/shard_map/while/body/eval_jaxpr/dot_general | solution.py:54
  148.0 45.8 %while.30 = (s32[]{:T(128)}, f32[2048,128]{1,0:T(8,128)S(1)}, s32[8192,2,4]{0,2,1:T(4,128)S(1)}, bf16[8192,2,128]{2,0,1:T(8,128)(2,1)}, s32[]{:T(128)}, /*index=5*/s32[]{:T(128)}, s32[]{:T(128)}, s32[]{:T(128)}) while((s32[]{:T(128)}, f32[2048,128]{1,0:T(8,128)S(1)}, s32[8192,2,4]{0,2,1:T(4,128)S(1)}, ...), condition=%wide.region_1.2_spmd.clone.clone, body=%wide.region_0.0_spmd.clone.clone.sunk | while | flops 570949632 | bytes 2441365 | solution.py:59
  148.1 5.6 %fusion.58 = f32[2048,128]{1,0:T(8,128)S(1)} fusion(s32[1024]{0:T(1024)S(1)} %bitcast.71, s32[1024]{0:T(1024)S(1)} %bitcast.72, s32[1024]{0:T(1024)S(1)} %bitcast.73, s32[1024]{0:T(1024)S(1)} %bitcast.70, f32[2048,128]{1,0:T(8,128)S(1)} %get-tuple-element.421, pred[]{:T(512)S(6)} %compare.6, bf16[8192,2,128]{2,0,1:T(8,128)(2,1)} %get-tuple-element.431, ...), kind=kOutput, calls=%fused_computation.18.clone.1 | convolution fusion | flops 570949632 | bytes 2375685 | tf_op jit(solution)/shard_map/while/body/eval_jaxpr/dot_general | solution.py:54
  153.8 5.6 %fusion.58 = f32[2048,128]{1,0:T(8,128)S(1)} fusion(s32[1024]{0:T(1024)S(1)} %bitcast.71, s32[1024]{0:T(1024)S(1)} %bitcast.72, s32[1024]{0:T(1024)S(1)} %bitcast.73, s32[1024]{0:T(1024)S(1)} %bitcast.70, f32[2048,128]{1,0:T(8,128)S(1)} %get-tuple-element.421, pred[]{:T(512)S(6)} %compare.6, bf16[8192,2,128]{2,0,1:T(8,128)(2,1)} %get-tuple-element.431, ...), kind=kOutput, calls=%fused_computation.18.clone.1 | convolution fusion | flops 570949632 | bytes 2375685 | tf_op jit(solution)/shard_map/while/body/eval_jaxpr/dot_general | solution.py:54
  159.5 5.6 %fusion.58 = f32[2048,128]{1,0:T(8,128)S(1)} fusion(s32[1024]{0:T(1024)S(1)} %bitcast.71, s32[1024]{0:T(1024)S(1)} %bitcast.72, s32[1024]{0:T(1024)S(1)} %bitcast.73, s32[1024]{0:T(1024)S(1)} %bitcast.70, f32[2048,128]{1,0:T(8,128)S(1)} %get-tuple-element.421, pred[]{:T(512)S(6)} %compare.6, bf16[8192,2,128]{2,0,1:T(8,128)(2,1)} %get-tuple-element.431, ...), kind=kOutput, calls=%fused_computation.18.clone.1 | convolution fusion | flops 570949632 | bytes 2375685 | tf_op jit(solution)/shard_map/while/body/eval_jaxpr/dot_general | solution.py:54
  165.3 5.6 %fusion.58 = f32[2048,128]{1,0:T(8,128)S(1)} fusion(s32[1024]{0:T(1024)S(1)} %bitcast.71, s32[1024]{0:T(1024)S(1)} %bitcast.72, s32[1024]{0:T(1024)S(1)} %bitcast.73, s32[1024]{0:T(1024)S(1)} %bitcast.70, f32[2048,128]{1,0:T(8,128)S(1)} %get-tuple-element.421, pred[]{:T(512)S(6)} %compare.6, bf16[8192,2,128]{2,0,1:T(8,128)(2,1)} %get-tuple-element.431, ...), kind=kOutput, calls=%fused_computation.18.clone.1 | convolution fusion | flops 570949632 | bytes 2375685 | tf_op jit(solution)/shard_map/while/body/eval_jaxpr/dot_general | solution.py:54
  171.0 5.6 %fusion.58 = f32[2048,128]{1,0:T(8,128)S(1)} fusion(s32[1024]{0:T(1024)S(1)} %bitcast.71, s32[1024]{0:T(1024)S(1)} %bitcast.72, s32[1024]{0:T(1024)S(1)} %bitcast.73, s32[1024]{0:T(1024)S(1)} %bitcast.70, f32[2048,128]{1,0:T(8,128)S(1)} %get-tuple-element.421, pred[]{:T(512)S(6)} %compare.6, bf16[8192,2,128]{2,0,1:T(8,128)(2,1)} %get-tuple-element.431, ...), kind=kOutput, calls=%fused_computation.18.clone.1 | convolution fusion | flops 570949632 | bytes 2375685 | tf_op jit(solution)/shard_map/while/body/eval_jaxpr/dot_general | solution.py:54
  176.7 5.6 %fusion.58 = f32[2048,128]{1,0:T(8,128)S(1)} fusion(s32[1024]{0:T(1024)S(1)} %bitcast.71, s32[1024]{0:T(1024)S(1)} %bitcast.72, s32[1024]{0:T(1024)S(1)} %bitcast.73, s32[1024]{0:T(1024)S(1)} %bitcast.70, f32[2048,128]{1,0:T(8,128)S(1)} %get-tuple-element.421, pred[]{:T(512)S(6)} %compare.6, bf16[8192,2,128]{2,0,1:T(8,128)(2,1)} %get-tuple-element.431, ...), kind=kOutput, calls=%fused_computation.18.clone.1 | convolution fusion | flops 570949632 | bytes 2375685 | tf_op jit(solution)/shard_map/while/body/eval_jaxpr/dot_general | solution.py:54
  182.4 5.7 %fusion.58 = f32[2048,128]{1,0:T(8,128)S(1)} fusion(s32[1024]{0:T(1024)S(1)} %bitcast.71, s32[1024]{0:T(1024)S(1)} %bitcast.72, s32[1024]{0:T(1024)S(1)} %bitcast.73, s32[1024]{0:T(1024)S(1)} %bitcast.70, f32[2048,128]{1,0:T(8,128)S(1)} %get-tuple-element.421, pred[]{:T(512)S(6)} %compare.6, bf16[8192,2,128]{2,0,1:T(8,128)(2,1)} %get-tuple-element.431, ...), kind=kOutput, calls=%fused_computation.18.clone.1 | convolution fusion | flops 570949632 | bytes 2375685 | tf_op jit(solution)/shard_map/while/body/eval_jaxpr/dot_general | solution.py:54
  188.1 5.7 %fusion.58 = f32[2048,128]{1,0:T(8,128)S(1)} fusion(s32[1024]{0:T(1024)S(1)} %bitcast.71, s32[1024]{0:T(1024)S(1)} %bitcast.72, s32[1024]{0:T(1024)S(1)} %bitcast.73, s32[1024]{0:T(1024)S(1)} %bitcast.70, f32[2048,128]{1,0:T(8,128)S(1)} %get-tuple-element.421, pred[]{:T(512)S(6)} %compare.6, bf16[8192,2,128]{2,0,1:T(8,128)(2,1)} %get-tuple-element.431, ...), kind=kOutput, calls=%fused_computation.18.clone.1 | convolution fusion | flops 570949632 | bytes 2375685 | tf_op jit(solution)/shard_map/while/body/eval_jaxpr/dot_general | solution.py:54
  193.8 0.1 maximum_bitcast_fusion
  193.9 0.0 copy-start.2
  194.0 33.0 %all_to_all.41 = f32[2,2,1024,128]{3,2,1,0:T(8,128)S(1)} all-to-all(f32[2,2,1024,128]{3,2,1,0:T(8,128)S(1)} %maximum_bitcast_fusion), channel_id=1, replica_groups=mesh['dp'=64,'mp'=2] {'mp'}, dimensions={0} | all-to-all | bytes 4194304 | tf_op jit(solution)/shard_map/all_to_all | solution.py:30
  227.0 0.2 reduce_sum.18
  227.2 0.4 multiply_reduce_fusion
  227.6 0.0 copy-done.2
  227.6 0.6 fusion.44
  228.2 2.5 %divide_subtract_fusion = f32[2,1024,128]{2,1,0:T(8,128)} fusion(f32[2,1024,128]{2,1,0:T(8,128)} %param.14, f32[2,1024,128]{2,1,0:T(8,128)S(1)} %reduce_sum.18, f32[2,1024]{1,0:T(2,128)S(1)} %get-tuple-element.309), kind=kLoop, calls=%fused_computation.43 | loop fusion | flops 786432 | bytes 3153920 | tf_op jit(solution)/shard_map/sub | solution.py:82
  230.7 2.2 all-reduce.2.cloned.1.call-done
  232.9 4.8 %copy.40 = f32[1024,1024]{1,0:T(8,128)} copy(f32[1024,1024]{1,0:T(8,128)} %all-reduce.2.cloned.1.call-done) | data formatting | bytes 8388608
  (35 shorter events, 0.4 us)
Async XLA Ops:
  7.2 35.1 %copy-start = (bf16[128,1024]{1,0:T(8,128)(2,1)S(1)}, bf16[128,1024]{1,0:T(8,128)(2,1)}, u32[]{:S(2)}) copy-start(bf16[128,1024]{1,0:T(8,128)(2,1)} %param.16) | copy-start | bytes 786436
  10.2 26.1 %all-to-all-start = ((s32[128,128,5]{0,2,1:T(8,128)}), s32[128,128,5]{0,2,1:T(8,128)S(1)}, u32[]{:S(2)}, u32[]{:S(2)}) async-start(s32[128,128,5]{0,2,1:T(8,128)} %pad_add_fusion), calls=%async_computation | async-start | bytes 1048576 | tf_op jit(solution)/shard_map/all_to_all | solution.py:16
  29.4 13.0 %copy-start.1 = (bf16[128,1024]{1,0:T(8,128)(2,1)S(1)}, bf16[128,1024]{1,0:T(8,128)(2,1)}, u32[]{:S(2)}) copy-start(bf16[128,1024]{1,0:T(8,128)(2,1)} %param.17) | copy-start | bytes 786436
  36.3 61.1 %all-to-all-start.1 = ((bf16[128,128,128]{2,0,1:T(8,128)(2,1)}), bf16[128,128,128]{2,0,1:T(8,128)(2,1)}, u32[]{:S(2)}, u32[]{:S(2)}) async-start(bf16[128,128,128]{2,0,1:T(8,128)(2,1)} %copy.23), calls=%async_computation.1 | async-start | bytes 8388608 | tf_op jit(solution)/shard_map/all_to_all | solution.py:73
  42.1 190.9 %all-reduce.2.cloned.1.call-start = ((), (), s32[]{:S(2)}) async-start(), calls=%async_computation.3 | async-start | bytes 8388608 | tf_op jit(solution)/shard_map/psum | solution.py:69
  193.9 33.6 %copy-start.2 = (f32[2,1024]{1,0:T(2,128)S(1)}, f32[2,1024]{1,0:T(2,128)}, u32[]{:S(2)}) copy-start(f32[2,1024]{1,0:T(2,128)} %param.15) | copy-start | bytes 24580
Sparse Core Ops, SparseCore 0:
  47.8 185.0 all-reduce.1
where the time goes:
time: 246 us; the launch traced here: 245 us
  matrix products  93.1 us (38%)
  waiting for transfers between devices  61 us (25%)
  blocking collectives  33 us (13%)
  local copies, waits for them, and re-layouts  19.2 us (8%)
  starting transfers between devices  18.3 us (7%)
  between operations  14.2 us (6%)
  other arithmetic  4.93 us (2%)
    dot_general x16, matrix products, add_block(): lax.dot_general(onehot, piece, (((0,), (0,)), ((), ())), preferred_elemen...  90.4 us
    all_to_all x1, waiting for transfers between devices, per_device(): lax.all_to_all(pooled_grad, 'dp', split_axis=1, concat_axis=0, tiled=True)  51.9 us
    all_to_all x1, blocking collectives, sent_and_summed(): lax.all_to_all(blocks, axis, split_axis=0, concat_axis=0, tiled=True)  33 us
    unnamed x11, local copies, waits for them, and re-layouts  13.9 us
    all_to_all x1, starting transfers between devices, in_one_piece(): lax.all_to_all(both, axis, split_axis=split_dim, concat_axis=concat_dim,...  12.3 us
    all_to_all x1, waiting for transfers between devices, in_one_piece(): lax.all_to_all(both, axis, split_axis=split_dim, concat_axis=concat_dim,...  6.93 us
    all_to_all x1, starting transfers between devices, per_device(): lax.all_to_all(pooled_grad, 'dp', split_axis=1, concat_axis=0, tiled=True)  5.78 us
  transfers between devices with their start and end apart: 3, of which 3 were waited for; matrix products, arithmetic and copies ran while one was open for 45% of the time, Pallas kernels for 0%

commit v1 on v0

v1 whole, which is shorter than its diff:
```python
import functools

import jax
import jax.numpy as jnp
from jax import lax
from jax.experimental import pallas as pl
from jax.experimental.pallas import tpu as pltpu
from jax.sharding import Mesh, PartitionSpec as P

learn_rate = 0.5
ring = 4
every = ("y", "x", "zh", "c", "zl")
deep = ("zh", "zl")
f32 = jnp.float32
bf16 = jnp.bfloat16


def coded(row):
    size = (128 + (row & 127)) << ((row >> 7) & 7)
    return jnp.where(row >= 1024, -size, size).astype(f32).astype(bf16)


def slot_codes(lengths, looked):
    rows = jnp.transpose(looked, (1, 2, 0))
    count = jnp.transpose(lengths, (1, 0))
    slots = rows.shape[1]
    active = [count > j for j in range(slots)]
    row = [rows[:, j, :] for j in range(slots)]
    codes, weights = [], []
    for j in range(slots):
        first = active[j]
        for i in range(j):
            first = first & (row[i] != row[j])
        weight = jnp.ones_like(count)
        for i in range(j + 1, slots):
            weight = weight + (active[i] & (row[i] == row[j])).astype(jnp.int32)
        codes.append(jnp.where(first, coded(row[j]), jnp.zeros((), bf16)))
        weights.append(weight.astype(f32).astype(bf16))
    return jnp.stack(codes + weights, axis=1)


def pack_kernel(swap_ref, grad_ref, code_ref, out_ref):
    samples = grad_ref.shape[0]
    tables, _, width = code_ref.shape
    for first in range(0, samples, 16):
        block = grad_ref[first : first + 16].reshape(16 * tables, width)
        turned = jnp.dot(swap_ref[...], block, preferred_element_type=f32)
        out_ref[:, first : first + 16, :] = turned.astype(bf16).reshape(tables, 16, width)
    out_ref[:, samples : samples + 8, :] = code_ref[...]


def packed(grads, codes):
    samples, tables, width = grads.shape
    index = jnp.arange(256, dtype=jnp.int32)
    swap = ((index[:, None] % 16 == index[None, :] // 16) & (index[:, None] // 16 == index[None, :] % 16)).astype(bf16)
    return pl.pallas_call(
        pack_kernel,
        grid=(tables // 16,),
        in_specs=[
            pl.BlockSpec((256, 256), lambda i: (0, 0)),
            pl.BlockSpec((samples, 16, width), lambda i: (0, i, 0)),
            pl.BlockSpec((16, 8, width), lambda i: (i, 0, 0)),
        ],
        out_specs=pl.BlockSpec((16, samples + 8, width), lambda i: (i, 0, 0)),
        out_shape=jax.ShapeDtypeStruct((tables, samples + 8, width), bf16),
        cost_estimate=pl.CostEstimate(flops=2 * 256 * samples * tables * width, bytes_accessed=8 << 20, transcendentals=0),
        name="pack",
    )(swap, grads, codes)


group = 4


def sum_kernel(base_ref, code_ref, data_ref, out_ref):
    senders, height, width = data_ref.shape
    samples = height - 8
    rows = out_ref.shape[0]
    base = base_ref[0]

    @pl.when(pl.program_id(0) == 0)
    def _():
        out_ref[...] = jnp.zeros_like(out_ref)

    mine = code_ref[pl.ds(pl.multiple_of(base, rows), rows), :]
    zero = jnp.zeros((), bf16)
    for first in range(0, senders, group):
        hots = []
        values = []
        for k in range(first, first + group):
            info = data_ref[k, samples:height, :]
            hot = jnp.where(mine == info[3:4], info[7:8], zero)
            for j in (2, 1, 0):
                hot = jnp.where(mine == info[j : j + 1], info[4 + j : 5 + j], hot)
            hots.append(hot)
            values.append(data_ref[k, 0:samples, :])
        out_ref[...] += jnp.dot(
            jnp.concatenate(hots, axis=1), jnp.concatenate(values, axis=0), preferred_element_type=f32
        )


def summed(data, codes, base, rows):
    senders, height, width = data.shape
    step = 8
    return pl.pallas_call(
        sum_kernel,
        grid_spec=pltpu.PrefetchScalarGridSpec(
            num_scalar_prefetch=1,
            grid=(senders // step,),
            in_specs=[
                pl.BlockSpec(codes.shape, lambda i, b: (0, 0)),
                pl.BlockSpec((step, height, width), lambda i, b: (i, 0, 0)),
            ],
            out_specs=pl.BlockSpec((rows, width), lambda i, b: (0, 0)),
        ),
        out_shape=jax.ShapeDtypeStruct((rows, width), f32),
        cost_estimate=pl.CostEstimate(flops=2 * senders * 128 * rows * width, bytes_accessed=5 << 20, transcendentals=0),
        name="sum_by_row",
    )(base, codes, data)


def to_next(value, axis, step):
    return lax.ppermute(value, axis, [(i, (i + step) % ring) for i in range(ring)])


def scattered(value, axis, here):
    arrived = [
        to_next(lax.dynamic_index_in_dim(value, (here + step) % ring, 0, keepdims=False), axis, step)
        for step in range(1, ring)
    ]
    own = lax.dynamic_index_in_dim(value, here, 0, keepdims=False)
    return own + arrived[0] + arrived[1] + arrived[2]


def place_kernel(at_ref, *refs):
    out_ref = refs[-1]
    here_y, here_x, here_z, here_c = (at_ref[k] for k in range(4))
    for core in range(2):
        c = here_c if core == 0 else 1 - here_c
        for dy in range(ring):
            y = (here_y + ring - dy) % ring
            piece = refs[core * ring + dy]
            for dx in range(ring):
                x = (here_x + ring - dx) % ring
                left = pl.multiple_of((x % 2) * 512, 512)
                for dz in range(ring):
                    z = (here_z + ring - dz) % ring
                    top = pl.multiple_of((x // 2) * 512 + c * 256 + y * 64 + z * 16, 16)
                    out_ref[pl.ds(top, 16), pl.ds(left, 512)] = piece[dx, dz]


def placed(at, pieces):
    return pl.pallas_call(
        place_kernel,
        in_specs=[pl.BlockSpec(memory_space=pltpu.SMEM)] + [pl.BlockSpec(memory_space=pltpu.VMEM)] * len(pieces),
        out_specs=pl.BlockSpec(memory_space=pltpu.VMEM),
        out_shape=jax.ShapeDtypeStruct((1024, 1024), f32),
        cost_estimate=pl.CostEstimate(flops=3 << 20, bytes_accessed=8 << 20, transcendentals=0),
        name="place",
    )(at, *pieces)


def dense_sum(inputs, cotangents):
    y, x, c = (lax.axis_index(a) for a in ("y", "x", "c"))
    z = lax.axis_index(deep)

    def share(of):
        one = jnp.where(of // 2 == 0, inputs[:, :512], inputs[:, 512:])
        two = jnp.where(of % 2 == 0, cotangents[:, :512], cotangents[:, 512:])
        return jnp.concatenate([one, two], axis=1)

    parts = [share(x)] + [to_next(share((x + step) % ring), "x", step) for step in range(1, ring)]
    both = jnp.concatenate(parts, axis=0)
    local = lax.dot_general(both[:, :512], both[:, 512:], (((0,), (0,)), ((), ())), preferred_element_type=f32)
    halves = local.reshape(2, 256, 512)
    swap = [(0, 1), (1, 0)]
    other = lax.ppermute(lax.dynamic_index_in_dim(halves, 1 - c, 0, keepdims=False), "c", swap)
    total = lax.dynamic_index_in_dim(halves, c, 0, keepdims=False) + other
    total = scattered(total.reshape(ring, 64, 512), "y", y)
    total = scattered(total.reshape(ring, 16, 512), deep, z)
    total = jnp.stack([total] + [to_next(total, deep, step) for step in range(1, ring)])
    total = jnp.stack([total] + [to_next(total, "x", step) for step in range(1, ring)])
    mine = [total] + [to_next(total, "y", step) for step in range(1, ring)]
    theirs = [lax.ppermute(p, "c", swap) for p in mine]
    return placed(jnp.stack([y, x, z, c]).astype(jnp.int32), mine + theirs)


def per_device(
    pooled_grad, bag_lengths, bag_rows, table_rows, row_accum, dense_input, dense_cotangent
):
    tables, rows = row_accum.shape
    dense_grad = dense_sum(dense_input, dense_cotangent)
    outgoing = packed(pooled_grad, slot_codes(bag_lengths, bag_rows))
    data = lax.all_to_all(outgoing, every, split_axis=0, concat_axis=0, tiled=True)
    codes = jnp.broadcast_to(coded(jnp.arange(tables * rows, dtype=jnp.int32))[:, None], (tables * rows, 128))
    half = lax.axis_index("zl").astype(jnp.int32)
    theirs = summed(data, codes, ((1 - half) * rows)[None], rows)
    arrived = lax.ppermute(theirs, "zl", [(0, 1), (1, 0)])
    own = summed(data, codes, (half * rows)[None], rows)
    row_grad = jnp.where(half == 0, jnp.stack([own, arrived]), jnp.stack([arrived, own]))
    new_accum = row_accum + jnp.mean(row_grad * row_grad, axis=-1)
    new_rows = table_rows - learn_rate * row_grad / jnp.sqrt(new_accum)[..., None]
    return (new_rows, new_accum, dense_grad)


def solution(mesh):
    fine = Mesh(mesh.devices.reshape(4, 4, 2, 2, 2), every)
    samples = P(every)
    owned = P(("y", "x", "zh", "c"), "zl")
    return jax.shard_map(
        per_device,
        mesh=fine,
        in_specs=(samples, samples, samples, owned, owned, samples, samples),
        out_specs=(owned, owned, P()),
        check_vma=False,
    )
```

time: 246 us -> 211 us (0.86)
  matrix products: 93.1 us -> 0.46 us
  Pallas kernels: 0 us -> 59.7 us
  blocking collectives: 33 us -> 0 us
  starting transfers between devices: 18.3 us -> 49.3 us
  waiting for transfers between devices: 61 us -> 87.3 us
  local copies, waits for them, and re-layouts: 19.2 us -> 5.9 us
  between operations: 14.2 us -> 1.09 us
    dot_general x17 -> x1, matrix products: 93.1 us -> 0.46 us  [dense_sum(): lax.dot_general(both[:, :512], both[:, 512:], (((0,), (0,)), ((), ())), p...]
    ppermute x0 -> x24, waiting for transfers between devices: none -> 87.3 us  [the longest x18 85.8 us: to_next(): lax.ppermute(value, axis, [(i, (i + step) % ring) for i in range(ring)])]
    pallas_call x0 -> x4, Pallas kernels: none -> 59.7 us  [the longest x2 46.9 us: summed(): pl.pallas_call(sum_kernel, grid_spec=pltpu.PrefetchScalarGridSpec(num_sca...]
    all_to_all x2 -> x1, waiting for transfers between devices: 58.8 us -> 0.01 us  [per_device(): lax.all_to_all(outgoing, every, split_axis=0, concat_axis=0, tiled=True)]
    ppermute x0 -> x24, starting transfers between devices: none -> 37.4 us  [the longest x18 19.5 us: to_next(): lax.ppermute(value, axis, [(i, (i + step) % ring) for i in range(ring)])]
    all_to_all x1 -> x0, blocking collectives: 33 us -> none  [sent_and_summed(): lax.all_to_all(blocks, axis, split_axis=0, concat_axis=0, tiled=True)]
    unnamed x11 -> x20, local copies, waits for them, and re-layouts: 13.9 us -> 2.81 us
    all_to_all x2 -> x1, starting transfers between devices: 18.1 us -> 11.9 us  [per_device(): lax.all_to_all(outgoing, every, split_axis=0, concat_axis=0, tiled=True)]
  transfers between devices with their start and end apart: 3 -> 25, of which waited for: 3 -> 16; matrix products, arithmetic and copies ran while one was open for 45% -> 1% of each run, Pallas kernels for 0% -> 24%
where the time goes in v1:
time: 211 us
  waiting for transfers between devices  87.3 us (41%)
  Pallas kernels  59.7 us (28%)
  starting transfers between devices  49.3 us (23%)
  other arithmetic  6.83 us (3%)
  local copies, waits for them, and re-layouts  5.9 us (3%)
    ppermute x18, waiting for transfers between devices, to_next(): lax.ppermute(value, axis, [(i, (i + step) % ring) for i in range(ring)])  85.8 us
    pallas_call x2, Pallas kernels, summed(): pl.pallas_call(sum_kernel, grid_spec=pltpu.PrefetchScalarGridSpec(num_sca...  46.9 us
    ppermute x18, starting transfers between devices, to_next(): lax.ppermute(value, axis, [(i, (i + step) % ring) for i in range(ring)])  19.5 us
    ppermute x4, starting transfers between devices, dense_sum(): theirs = [lax.ppermute(p, 'c', swap) for p in mine]  16.8 us
    all_to_all x1, starting transfers between devices, per_device(): lax.all_to_all(outgoing, every, split_axis=0, concat_axis=0, tiled=True)  11.9 us
    pallas_call x1, Pallas kernels, packed(): pl.pallas_call(pack_kernel, grid=(tables // 16,), in_specs=[pl.BlockSpec(...  8.17 us
    pallas_call x1, Pallas kernels, placed(): pl.pallas_call(place_kernel, in_specs=[pl.BlockSpec(memory_space=pltpu.SM...  4.63 us
  transfers between devices with their start and end apart: 25, of which 16 were waited for; matrix products, arithmetic and copies ran while one was open for 1% of the time, Pallas kernels for 24%

profile of v1, /device:TPU:1, one launch (start us, length us, event | category | flops | bytes accessed | tf_op | source)
XLA Modules:
  0.0 210.6 jit_solution(13274506697282336279)
XLA Ops:
  0.6 1.1 copy.95
  1.7 0.9 copy.94
  2.8 0.2 fusion.24
  3.0 0.1 copy.100
  3.0 0.1 copy.101
  3.1 0.1 copy.102
  3.1 0.1 copy.103
  3.2 0.1 copy.104
  3.3 0.1 copy.105
  3.4 0.8 and_convert_fusion.swap_ref
  4.2 1.5 stack.94.code_ref
  5.7 8.2 %pack.1 = bf16[128,136,128]{2,1,0:T(8,128)(2,1)} custom-call(bf16[256,256]{1,0:T(8,128)(2,1)} %and_convert_fusion.swap_ref, bf16[128,128,128]{2,1,0:T(8,128)(2,1)} %grad_ref.1, bf16[128,8,128]{2,1,0:T(8,128)(2,1)} %stack.94.code_ref), custom_call_target="tpu_custom_call" | custom-call | flops 1073741824 | bytes 8388608 | tf_op jit(solution)/shard_map/pack/pallas_call | solution.py:56
  13.8 11.9 %all-to-all-start = ((bf16[128,136,128]{2,1,0:T(8,128)(2,1)}), bf16[128,136,128]{2,1,0:T(8,128)(2,1)}, u32[]{:S(2)}, u32[]{:S(2)}) async-start(bf16[128,136,128]{2,1,0:T(8,128)(2,1)} %pack.1), calls=%async_computation | async-start | bytes 8912896 | tf_op jit(solution)/shard_map/all_to_all | solution.py:193
  26.0 2.6 %collective-permute-start.3 = (bf16[128,1024]{1,0:T(8,128)(2,1)S(1)}, bf16[128,1024]{1,0:T(8,128)(2,1)S(1)}, u32[]{:S(2)}, u32[]{:S(2)}) collective-permute-start(bf16[128,1024]{1,0:T(8,128)(2,1)S(1)} %pad_maximum_fusion.4), channel_id=1, source_target_pairs={{0,24},{8,0},{16,8},{24,16},{1,25},{9,1},{17,9},{25,17},{2,26},{10... | collective-permute-start | bytes 786440 | tf_op jit(solution)/shard_map/ppermute | solution.py:122
  28.7 0.7 collective-permute-start.2
  29.4 0.6 collective-permute-start.1
  30.0 50.2 %collective-permute-done.3 = bf16[128,1024]{1,0:T(8,128)(2,1)S(1)} collective-permute-done((bf16[128,1024]{1,0:T(8,128)(2,1)S(1)}, bf16[128,1024]{1,0:T(8,128)(2,1)S(1)}, u32[]{:S(2)}, u32[]{:S(2)}) %collective-permute-start.3) | collective-permute-done | bytes 262176 | tf_op jit(solution)/shard_map/ppermute | solution.py:122
  80.2 1.5 collective-permute-done.2
  81.7 5.4 %collective-permute-done.1 = bf16[128,1024]{1,0:T(8,128)(2,1)S(1)} collective-permute-done((bf16[128,1024]{1,0:T(8,128)(2,1)S(1)}, bf16[128,1024]{1,0:T(8,128)(2,1)S(1)}, u32[]{:S(2)}, u32[]{:S(2)}) %collective-permute-start.1) | collective-permute-done | bytes 262176 | tf_op jit(solution)/shard_map/ppermute | solution.py:122
  87.1 0.1 pad_maximum_fusion
  87.2 0.5 fusion
  87.7 0.9 collective-permute-start.4
  88.5 1.5 collective-permute-done.4
  90.1 0.1 bitcast_add_fusion
  90.2 2.6 %collective-permute-start.7 = (f32[64,512]{1,0:T(8,128)S(1)}, f32[64,512]{1,0:T(8,128)S(1)}, u32[]{:S(2)}, u32[]{:S(2)}) collective-permute-start(f32[64,512]{1,0:T(8,128)S(1)} %get-tuple-element.12), channel_id=1, source_target_pairs={{0,96},{32,0},{64,32},{96,64},{1,97},{33,1},{65,33},{97,65},{2,98}... | collective-permute-start | bytes 393224 | tf_op jit(solution)/shard_map/ppermute | solution.py:122
  92.8 0.5 collective-permute-start.6
  93.3 0.6 collective-permute-start.5
  93.9 4.1 %collective-permute-done.7 = f32[64,512]{1,0:T(8,128)S(1)} collective-permute-done((f32[64,512]{1,0:T(8,128)S(1)}, f32[64,512]{1,0:T(8,128)S(1)}, u32[]{:S(2)}, u32[]{:S(2)}) %collective-permute-start.7) | collective-permute-done | bytes 131104 | tf_op jit(solution)/shard_map/ppermute | solution.py:122
  98.0 0.7 collective-permute-done.6
  98.7 3.8 %collective-permute-done.5 = f32[64,512]{1,0:T(8,128)S(1)} collective-permute-done((f32[64,512]{1,0:T(8,128)S(1)}, f32[64,512]{1,0:T(8,128)S(1)}, u32[]{:S(2)}, u32[]{:S(2)}) %collective-permute-start.5) | collective-permute-done | bytes 131104 | tf_op jit(solution)/shard_map/ppermute | solution.py:122
  102.6 3.3 %collective-permute-start.10 = (f32[16,512]{1,0:T(8,128)S(1)}, f32[16,512]{1,0:T(8,128)S(1)}, u32[]{:S(2)}, u32[]{:S(2)}) collective-permute-start(f32[16,512]{1,0:T(8,128)S(1)} %get-tuple-element.29), channel_id=1, source_target_pairs={{0,5},{1,0},{4,1},{5,4},{2,7},{3,2},{6,3},{7,6},{8,13},{9,8},{12,9... | collective-permute-start | bytes 98312 | tf_op jit(solution)/shard_map/ppermute | solution.py:122
  105.9 0.1 collective-permute-start.9
  105.9 0.8 collective-permute-start.8
  106.7 0.2 collective-permute-done.10
  106.9 3.3 %collective-permute-done.9 = f32[16,512]{1,0:T(8,128)S(1)} collective-permute-done((f32[16,512]{1,0:T(8,128)S(1)}, f32[16,512]{1,0:T(8,128)S(1)}, u32[]{:S(2)}, u32[]{:S(2)}) %collective-permute-start.9) | collective-permute-done | bytes 32800 | tf_op jit(solution)/shard_map/ppermute | solution.py:122
  110.3 0.9 collective-permute-start.13
  111.1 0.8 collective-permute-start.12
  111.9 0.8 collective-permute-start.11
  112.7 0.4 collective-permute-done.13
  113.1 2.3 %collective-permute-done.12 = f32[16,512]{1,0:T(8,128)S(1)} collective-permute-done((f32[16,512]{1,0:T(8,128)S(1)}, f32[16,512]{1,0:T(8,128)S(1)}, u32[]{:S(2)}, u32[]{:S(2)}) %collective-permute-start.12) | collective-permute-done | bytes 32800 | tf_op jit(solution)/shard_map/ppermute | solution.py:122
  115.4 0.5 collective-permute-done.11
  115.9 1.2 collective-permute-start.16
  117.1 1.4 collective-permute-start.15
  118.5 1.3 collective-permute-done.16
  119.8 2.7 %collective-permute-done.15 = f32[4,16,512]{2,1,0:T(8,128)S(1)} collective-permute-done((f32[4,16,512]{2,1,0:T(8,128)S(1)}, f32[4,16,512]{2,1,0:T(8,128)S(1)}, u32[]{:S(2)}, u32[]{:S(2)}) %collective-permute-start.15) | collective-permute-done | bytes 131104 | tf_op jit(solution)/shard_map/ppermute | solution.py:122
  122.5 1.4 collective-permute-done.14
  123.9 0.1 collective-permute-start.17
  124.0 0.4 collective-permute-start.18
  124.4 2.3 %collective-permute-start.19 = (f32[4,4,16,512]{3,2,1,0:T(8,128)S(1)}, f32[4,4,16,512]{3,2,1,0:T(8,128)S(1)}, u32[]{:S(2)}, u32[]{:S(2)}) collective-permute-start(f32[4,4,16,512]{3,2,1,0:T(8,128)S(1)} %pad_maximum_fusion.1.refs_0_), channel_id=1, source_target_pairs={{0,96},{32,0},{64,32},{96,64},{1,97},{33,1},{65,33},{97,65},{2,98}... | collective-permute-start | bytes 1572872 | tf_op jit(solution)/shard_map/ppermute | solution.py:122
  126.7 5.6 %collective-permute-start.20 = (f32[4,4,16,512]{3,2,1,0:T(8,128)S(1)}, f32[4,4,16,512]{3,2,1,0:T(8,128)S(1)}, u32[]{:S(2)}, u32[]{:S(2)}) collective-permute-start(f32[4,4,16,512]{3,2,1,0:T(8,128)S(1)} %pad_maximum_fusion.1.refs_0_), channel_id=1, source_target_pairs={{0,2},{2,0},{1,3},{3,1},{4,6},{6,4},{5,7},{7,5},{8,10},{10,8},{9,1... | collective-permute-start | bytes 1572872 | tf_op jit(solution)/shard_map/ppermute | solution.py:183
  132.3 7.9 %collective-permute-done.17.refs_1_ = f32[4,4,16,512]{3,2,1,0:T(8,128)S(1)} collective-permute-done((f32[4,4,16,512]{3,2,1,0:T(8,128)S(1)}, f32[4,4,16,512]{3,2,1,0:T(8,128)S(1)}, u32[]{:S(2)}, u32[]{:S(2)}) %collective-permute-start.17) | collective-permute-done | bytes 524320 | tf_op jit(solution)/shard_map/ppermute | solution.py:122
  140.2 10.5 %collective-permute-start.21 = (f32[4,4,16,512]{3,2,1,0:T(8,128)S(1)}, f32[4,4,16,512]{3,2,1,0:T(8,128)}, u32[]{:S(2)}, u32[]{:S(2)}) collective-permute-start(f32[4,4,16,512]{3,2,1,0:T(8,128)S(1)} %collective-permute-done.17.refs_1_), channel_id=1, source_target_pairs={{0,2},{2,0},{1,3},{3,1},{4,6},{6,4},{5,7},{7,5},{8,10},{10,8},{9,1... | collective-permute-start | bytes 1572872 | tf_op jit(solution)/shard_map/ppermute | solution.py:183
  150.8 0.1 collective-permute-start.22
  150.9 0.5 collective-permute-start.23
  151.4 1.1 broadcast_in_dim.27.code_ref
  152.6 23.4 %sum_by_row.3 = f32[1024,128]{1,0:T(8,128)} custom-call(s32[1]{0:T(128)} %bitcast.34.base_ref, bf16[2048,128]{1,0:T(8,128)(2,1)} %broadcast_in_dim.27.code_ref, bf16[128,136,128]{2,1,0:T(8,128)(2,1)} %all-to-all-done.data_ref), custom_call_target="tpu_custom_call" | custom-call | flops 4294967296 | bytes 5242880 | tf_op jit(solution)/shard_map/sum_by_row/pallas_call | solution.py:104
  176.0 0.3 collective-permute-start
  176.3 0.6 pad_add_fusion.at_ref
  176.9 0.8 copy-done.5
  177.7 4.6 %place.1 = f32[1024,1024]{1,0:T(8,128)} custom-call(s32[4]{0:T(128)} %pad_add_fusion.at_ref, f32[4,4,16,512]{3,2,1,0:T(8,128)} %copy-done, f32[4,4,16,512]{3,2,1,0:T(8,128)} %copy-done.2, f32[4,4,16,512]{3,2,1,0:T(8,128)} %copy-done.3, f32[4,4,16,512]{3,2,1,0:T(8,128)} %copy-done.4, f32[4,4,16,512]{3,2,1,0:T(8,128)} %copy-done.5, ...), custom_call_target="tpu_custom_call" | custom-call | flops 3145728 | bytes 8388608 | tf_op jit(solution)/shard_map/place/pallas_call | solution.py:152
  182.4 23.5 %sum_by_row.2 = f32[1024,128]{1,0:T(8,128)} custom-call(s32[1]{0:T(128)} %bitcast.base_ref, bf16[2048,128]{1,0:T(8,128)(2,1)} %broadcast_in_dim.27.code_ref, bf16[128,136,128]{2,1,0:T(8,128)(2,1)} %all-to-all-done.data_ref), custom_call_target="tpu_custom_call" | custom-call | flops 4294967296 | bytes 5242880 | tf_op jit(solution)/shard_map/sum_by_row/pallas_call | solution.py:104
  205.9 1.6 multiply_reduce_fusion
  207.5 0.6 fusion.32
  208.1 2.6 %divide_subtract_fusion = f32[2,1024,128]{2,1,0:T(8,128)} fusion(f32[2,1024,128]{2,1,0:T(8,128)S(1)} %copy-done.1, f32[1,1024,128]{2,1,0:T(8,128)} %bitcast.214, f32[1,1024,128]{2,1,0:T(8,128)S(1)} %bitcast.212, f32[2,1024]{1,0:T(2,128)S(1)} %get-tuple-element.3, pred[]{:T(512)S(6)} %eq.107), kind=kLoop, calls=%fused_computation.2 | loop fusion | flops 1572864 | bytes 3153921 | tf_op jit(solution)/shard_map/sub | solution.py:201
  (46 shorter events, 0.7 us)
Async XLA Ops:
  13.8 12.0 %copy-start.6 = (bf16[128,1024]{1,0:T(8,128)(2,1)S(1)}, bf16[128,1024]{1,0:T(8,128)(2,1)}, u32[]{:S(2)}) copy-start(bf16[128,1024]{1,0:T(8,128)(2,1)} %param.13) | copy-start | bytes 786436
  13.8 12.1 %copy-start.7 = (bf16[128,1024]{1,0:T(8,128)(2,1)S(1)}, bf16[128,1024]{1,0:T(8,128)(2,1)}, u32[]{:S(2)}) copy-start(bf16[128,1024]{1,0:T(8,128)(2,1)} %param.12) | copy-start | bytes 786436
  13.8 137.6 %all-to-all-start = ((bf16[128,136,128]{2,1,0:T(8,128)(2,1)}), bf16[128,136,128]{2,1,0:T(8,128)(2,1)}, u32[]{:S(2)}, u32[]{:S(2)}) async-start(bf16[128,136,128]{2,1,0:T(8,128)(2,1)} %pack.1), calls=%async_computation | async-start | bytes 8912896 | tf_op jit(solution)/shard_map/all_to_all | solution.py:193
  26.0 54.1 %collective-permute-start.3 = (bf16[128,1024]{1,0:T(8,128)(2,1)S(1)}, bf16[128,1024]{1,0:T(8,128)(2,1)S(1)}, u32[]{:S(2)}, u32[]{:S(2)}) collective-permute-start(bf16[128,1024]{1,0:T(8,128)(2,1)S(1)} %pad_maximum_fusion.4), channel_id=1, source_target_pairs={{0,24},{8,0},{16,8},{24,16},{1,25},{9,1},{17,9},{25,17},{2,26},{10... | collective-permute-start | bytes 786440 | tf_op jit(solution)/shard_map/ppermute | solution.py:122
  28.7 53.0 %collective-permute-start.2 = (bf16[128,1024]{1,0:T(8,128)(2,1)S(1)}, bf16[128,1024]{1,0:T(8,128)(2,1)S(1)}, u32[]{:S(2)}, u32[]{:S(2)}) collective-permute-start(bf16[128,1024]{1,0:T(8,128)(2,1)S(1)} %pad_maximum_fusion.3), channel_id=1, source_target_pairs={{0,16},{8,24},{16,0},{24,8},{1,17},{9,25},{17,1},{25,9},{2,18},{10... | collective-permute-start | bytes 786440 | tf_op jit(solution)/shard_map/ppermute | solution.py:122
  29.4 57.7 %collective-permute-start.1 = (bf16[128,1024]{1,0:T(8,128)(2,1)S(1)}, bf16[128,1024]{1,0:T(8,128)(2,1)S(1)}, u32[]{:S(2)}, u32[]{:S(2)}) collective-permute-start(bf16[128,1024]{1,0:T(8,128)(2,1)S(1)} %pad_maximum_fusion.2), channel_id=1, source_target_pairs={{0,8},{8,16},{16,24},{24,0},{1,9},{9,17},{17,25},{25,1},{2,10},{10... | collective-permute-start | bytes 786440 | tf_op jit(solution)/shard_map/ppermute | solution.py:122
  87.7 2.4 %collective-permute-start.4 = (f32[256,512]{1,0:T(8,128)S(1)}, f32[256,512]{1,0:T(8,128)S(1)}, u32[]{:S(2)}, u32[]{:S(2)}) collective-permute-start(f32[256,512]{1,0:T(8,128)S(1)} %dynamic-slice_bitcast_fusion), channel_id=1, source_target_pairs={{0,2},{2,0},{1,3},{3,1},{4,6},{6,4},{5,7},{7,5},{8,10},{10,8},{9,1... | collective-permute-start | bytes 1572872 | tf_op jit(solution)/shard_map/ppermute | solution.py:176
  90.2 7.7 %collective-permute-start.7 = (f32[64,512]{1,0:T(8,128)S(1)}, f32[64,512]{1,0:T(8,128)S(1)}, u32[]{:S(2)}, u32[]{:S(2)}) collective-permute-start(f32[64,512]{1,0:T(8,128)S(1)} %get-tuple-element.12), channel_id=1, source_target_pairs={{0,96},{32,0},{64,32},{96,64},{1,97},{33,1},{65,33},{97,65},{2,98}... | collective-permute-start | bytes 393224 | tf_op jit(solution)/shard_map/ppermute | solution.py:122
  92.8 5.9 %collective-permute-start.6 = (f32[64,512]{1,0:T(8,128)S(1)}, f32[64,512]{1,0:T(8,128)S(1)}, u32[]{:S(2)}, u32[]{:S(2)}) collective-permute-start(f32[64,512]{1,0:T(8,128)S(1)} %get-tuple-element.13), channel_id=1, source_target_pairs={{0,64},{32,96},{64,0},{96,32},{1,65},{33,97},{65,1},{97,33},{2,66}... | collective-permute-start | bytes 393224 | tf_op jit(solution)/shard_map/ppermute | solution.py:122
  93.3 9.3 %collective-permute-start.5 = (f32[64,512]{1,0:T(8,128)S(1)}, f32[64,512]{1,0:T(8,128)S(1)}, u32[]{:S(2)}, u32[]{:S(2)}) collective-permute-start(f32[64,512]{1,0:T(8,128)S(1)} %get-tuple-element.11), channel_id=1, source_target_pairs={{0,32},{32,64},{64,96},{96,0},{1,33},{33,65},{65,97},{97,1},{2,34}... | collective-permute-start | bytes 393224 | tf_op jit(solution)/shard_map/ppermute | solution.py:122
  102.6 4.3 %collective-permute-start.10 = (f32[16,512]{1,0:T(8,128)S(1)}, f32[16,512]{1,0:T(8,128)S(1)}, u32[]{:S(2)}, u32[]{:S(2)}) collective-permute-start(f32[16,512]{1,0:T(8,128)S(1)} %get-tuple-element.29), channel_id=1, source_target_pairs={{0,5},{1,0},{4,1},{5,4},{2,7},{3,2},{6,3},{7,6},{8,13},{9,8},{12,9... | collective-permute-start | bytes 98312 | tf_op jit(solution)/shard_map/ppermute | solution.py:122
  105.9 4.4 %collective-permute-start.9 = (f32[16,512]{1,0:T(8,128)S(1)}, f32[16,512]{1,0:T(8,128)S(1)}, u32[]{:S(2)}, u32[]{:S(2)}) collective-permute-start(f32[16,512]{1,0:T(8,128)S(1)} %get-tuple-element.30), channel_id=1, source_target_pairs={{0,4},{1,5},{4,0},{5,1},{2,6},{3,7},{6,2},{7,3},{8,12},{9,13},{12,... | collective-permute-start | bytes 98312 | tf_op jit(solution)/shard_map/ppermute | solution.py:122
  105.9 4.3 %collective-permute-start.8 = (f32[16,512]{1,0:T(8,128)S(1)}, f32[16,512]{1,0:T(8,128)S(1)}, u32[]{:S(2)}, u32[]{:S(2)}) collective-permute-start(f32[16,512]{1,0:T(8,128)S(1)} %get-tuple-element.28), channel_id=1, source_target_pairs={{0,1},{1,4},{4,5},{5,0},{2,3},{3,6},{6,7},{7,2},{8,9},{9,12},{12,1... | collective-permute-start | bytes 98312 | tf_op jit(solution)/shard_map/ppermute | solution.py:122
  110.3 2.8 %collective-permute-start.13 = (f32[16,512]{1,0:T(8,128)S(1)}, f32[16,512]{1,0:T(8,128)S(1)}, u32[]{:S(2)}, u32[]{:S(2)}) collective-permute-start(f32[16,512]{1,0:T(8,128)S(1)} %fusion.21), channel_id=1, source_target_pairs={{0,5},{1,0},{4,1},{5,4},{2,7},{3,2},{6,3},{7,6},{8,13},{9,8},{12,9... | collective-permute-start | bytes 98312 | tf_op jit(solution)/shard_map/ppermute | solution.py:122
  111.1 4.3 %collective-permute-start.12 = (f32[16,512]{1,0:T(8,128)S(1)}, f32[16,512]{1,0:T(8,128)S(1)}, u32[]{:S(2)}, u32[]{:S(2)}) collective-permute-start(f32[16,512]{1,0:T(8,128)S(1)} %fusion.21), channel_id=1, source_target_pairs={{0,4},{1,5},{4,0},{5,1},{2,6},{3,7},{6,2},{7,3},{8,12},{9,13},{12,... | collective-permute-start | bytes 98312 | tf_op jit(solution)/shard_map/ppermute | solution.py:122
  111.9 4.0 %collective-permute-start.11 = (f32[16,512]{1,0:T(8,128)S(1)}, f32[16,512]{1,0:T(8,128)S(1)}, u32[]{:S(2)}, u32[]{:S(2)}) collective-permute-start(f32[16,512]{1,0:T(8,128)S(1)} %fusion.21), channel_id=1, source_target_pairs={{0,1},{1,4},{4,5},{5,0},{2,3},{3,6},{6,7},{7,2},{8,9},{9,12},{12,1... | collective-permute-start | bytes 98312 | tf_op jit(solution)/shard_map/ppermute | solution.py:122
  115.9 3.9 %collective-permute-start.16 = (f32[4,16,512]{2,1,0:T(8,128)S(1)}, f32[4,16,512]{2,1,0:T(8,128)S(1)}, u32[]{:S(2)}, u32[]{:S(2)}) collective-permute-start(f32[4,16,512]{2,1,0:T(8,128)S(1)} %get-tuple-element.27), channel_id=1, source_target_pairs={{0,24},{8,0},{16,8},{24,16},{1,25},{9,1},{17,9},{25,17},{2,26},{10... | collective-permute-start | bytes 393224 | tf_op jit(solution)/shard_map/ppermute | solution.py:122
  117.1 5.4 %collective-permute-start.15 = (f32[4,16,512]{2,1,0:T(8,128)S(1)}, f32[4,16,512]{2,1,0:T(8,128)S(1)}, u32[]{:S(2)}, u32[]{:S(2)}) collective-permute-start(f32[4,16,512]{2,1,0:T(8,128)S(1)} %get-tuple-element.27), channel_id=1, source_target_pairs={{0,16},{8,24},{16,0},{24,8},{1,17},{9,25},{17,1},{25,9},{2,18},{10... | collective-permute-start | bytes 393224 | tf_op jit(solution)/shard_map/ppermute | solution.py:122
  118.5 5.4 %collective-permute-start.14 = (f32[4,16,512]{2,1,0:T(8,128)S(1)}, f32[4,16,512]{2,1,0:T(8,128)S(1)}, u32[]{:S(2)}, u32[]{:S(2)}) collective-permute-start(f32[4,16,512]{2,1,0:T(8,128)S(1)} %get-tuple-element.27), channel_id=1, source_target_pairs={{0,8},{8,16},{16,24},{24,0},{1,9},{9,17},{17,25},{25,1},{2,10},{10... | collective-permute-start | bytes 393224 | tf_op jit(solution)/shard_map/ppermute | solution.py:122
  123.9 52.1 %copy-start = (f32[4,4,16,512]{3,2,1,0:T(8,128)}, f32[4,4,16,512]{3,2,1,0:T(8,128)S(1)}, u32[]{:S(2)}) copy-start(f32[4,4,16,512]{3,2,1,0:T(8,128)S(1)} %pad_maximum_fusion.1.refs_0_) | copy-start | bytes 1572868
  123.9 16.3 %collective-permute-start.17 = (f32[4,4,16,512]{3,2,1,0:T(8,128)S(1)}, f32[4,4,16,512]{3,2,1,0:T(8,128)S(1)}, u32[]{:S(2)}, u32[]{:S(2)}) collective-permute-start(f32[4,4,16,512]{3,2,1,0:T(8,128)S(1)} %pad_maximum_fusion.1.refs_0_), channel_id=1, source_target_pairs={{0,32},{32,64},{64,96},{96,0},{1,33},{33,65},{65,97},{97,1},{2,34}... | collective-permute-start | bytes 1572872 | tf_op jit(solution)/shard_map/ppermute | solution.py:122
  124.0 26.8 %collective-permute-start.18 = (f32[4,4,16,512]{3,2,1,0:T(8,128)S(1)}, f32[4,4,16,512]{3,2,1,0:T(8,128)S(1)}, u32[]{:S(2)}, u32[]{:S(2)}) collective-permute-start(f32[4,4,16,512]{3,2,1,0:T(8,128)S(1)} %pad_maximum_fusion.1.refs_0_), channel_id=1, source_target_pairs={{0,64},{32,96},{64,0},{96,32},{1,65},{33,97},{65,1},{97,33},{2,66}... | collective-permute-start | bytes 1572872 | tf_op jit(solution)/shard_map/ppermute | solution.py:122
  124.4 26.5 %collective-permute-start.19 = (f32[4,4,16,512]{3,2,1,0:T(8,128)S(1)}, f32[4,4,16,512]{3,2,1,0:T(8,128)S(1)}, u32[]{:S(2)}, u32[]{:S(2)}) collective-permute-start(f32[4,4,16,512]{3,2,1,0:T(8,128)S(1)} %pad_maximum_fusion.1.refs_0_), channel_id=1, source_target_pairs={{0,96},{32,0},{64,32},{96,64},{1,97},{33,1},{65,33},{97,65},{2,98}... | collective-permute-start | bytes 1572872 | tf_op jit(solution)/shard_map/ppermute | solution.py:122
  126.7 50.2 %collective-permute-start.20 = (f32[4,4,16,512]{3,2,1,0:T(8,128)S(1)}, f32[4,4,16,512]{3,2,1,0:T(8,128)S(1)}, u32[]{:S(2)}, u32[]{:S(2)}) collective-permute-start(f32[4,4,16,512]{3,2,1,0:T(8,128)S(1)} %pad_maximum_fusion.1.refs_0_), channel_id=1, source_target_pairs={{0,2},{2,0},{1,3},{3,1},{4,6},{6,4},{5,7},{7,5},{8,10},{10,8},{9,1... | collective-permute-start | bytes 1572872 | tf_op jit(solution)/shard_map/ppermute | solution.py:183
  140.2 35.7 %copy-start.2 = (f32[4,4,16,512]{3,2,1,0:T(8,128)}, f32[4,4,16,512]{3,2,1,0:T(8,128)S(1)}, u32[]{:S(2)}) copy-start(f32[4,4,16,512]{3,2,1,0:T(8,128)S(1)} %collective-permute-done.17.refs_1_) | copy-start | bytes 1572868
  140.2 36.7 %collective-permute-start.21 = (f32[4,4,16,512]{3,2,1,0:T(8,128)S(1)}, f32[4,4,16,512]{3,2,1,0:T(8,128)}, u32[]{:S(2)}, u32[]{:S(2)}) collective-permute-start(f32[4,4,16,512]{3,2,1,0:T(8,128)S(1)} %collective-permute-done.17.refs_1_), channel_id=1, source_target_pairs={{0,2},{2,0},{1,3},{3,1},{4,6},{6,4},{5,7},{7,5},{8,10},{10,8},{9,1... | collective-permute-start | bytes 1572872 | tf_op jit(solution)/shard_map/ppermute | solution.py:183
  150.8 25.2 %copy-start.3 = (f32[4,4,16,512]{3,2,1,0:T(8,128)}, f32[4,4,16,512]{3,2,1,0:T(8,128)S(1)}, u32[]{:S(2)}) copy-start(f32[4,4,16,512]{3,2,1,0:T(8,128)S(1)} %collective-permute-done.18.refs_2_) | copy-start | bytes 1572868
  150.8 26.1 %collective-permute-start.22 = (f32[4,4,16,512]{3,2,1,0:T(8,128)S(1)}, f32[4,4,16,512]{3,2,1,0:T(8,128)}, u32[]{:S(2)}, u32[]{:S(2)}) collective-permute-start(f32[4,4,16,512]{3,2,1,0:T(8,128)S(1)} %collective-permute-done.18.refs_2_), channel_id=1, source_target_pairs={{0,2},{2,0},{1,3},{3,1},{4,6},{6,4},{5,7},{7,5},{8,10},{10,8},{9,1... | collective-permute-start | bytes 1572872 | tf_op jit(solution)/shard_map/ppermute | solution.py:183
  150.9 25.1 %copy-start.4 = (f32[4,4,16,512]{3,2,1,0:T(8,128)}, f32[4,4,16,512]{3,2,1,0:T(8,128)S(1)}, u32[]{:S(2)}) copy-start(f32[4,4,16,512]{3,2,1,0:T(8,128)S(1)} %collective-permute-done.19.refs_3_) | copy-start | bytes 1572868
  150.9 26.0 %collective-permute-start.23 = (f32[4,4,16,512]{3,2,1,0:T(8,128)S(1)}, f32[4,4,16,512]{3,2,1,0:T(8,128)}, u32[]{:S(2)}, u32[]{:S(2)}) collective-permute-start(f32[4,4,16,512]{3,2,1,0:T(8,128)S(1)} %collective-permute-done.19.refs_3_), channel_id=1, source_target_pairs={{0,2},{2,0},{1,3},{3,1},{4,6},{6,4},{5,7},{7,5},{8,10},{10,8},{9,1... | collective-permute-start | bytes 1572872 | tf_op jit(solution)/shard_map/ppermute | solution.py:183
  176.0 29.9 %collective-permute-start = (f32[1024,128]{1,0:T(8,128)}, f32[1024,128]{1,0:T(8,128)S(1)}, u32[]{:S(2)}, u32[]{:S(2)}) collective-permute-start(f32[1024,128]{1,0:T(8,128)} %sum_by_row.3), channel_id=1, source_target_pairs={{0,1},{1,0},{2,3},{3,2},{4,5},{5,4},{6,7},{7,6},{8,9},{9,8},{10,11... | collective-permute-start | bytes 1572872 | tf_op jit(solution)/shard_map/ppermute | solution.py:197
  176.9 0.8 copy-start.5
  182.3 25.1 %copy-start.8 = (f32[2,1024]{1,0:T(2,128)S(1)}, f32[2,1024]{1,0:T(2,128)}, u32[]{:S(2)}) copy-start(f32[2,1024]{1,0:T(2,128)} %param.11) | copy-start | bytes 24580
  182.3 25.7 %copy-start.1 = (f32[2,1024,128]{2,1,0:T(8,128)S(1)}, f32[2,1024,128]{2,1,0:T(8,128)}, u32[]{:S(2)}) copy-start(f32[2,1024,128]{2,1,0:T(8,128)} %param.10) | copy-start | bytes 3145732

commit v2 on v1

v2 whole, which is shorter than its diff:
```python
import functools

import jax
import jax.numpy as jnp
from jax import lax
from jax.experimental import pallas as pl
from jax.experimental.pallas import tpu as pltpu
from jax.sharding import Mesh, PartitionSpec as P


learn_rate = 0.5
ring = 4
every = ("y", "x", "zh", "c", "zl")
deep = ("zh", "zl")
f32 = jnp.float32
bf16 = jnp.bfloat16


def sized(row):
    size = (128 + (row & 127)) << ((row >> 7) & 7)
    return jnp.where(row >= 1024, -size, size)


def coded(row):
    return sized(row).astype(f32).astype(bf16)


def slot_codes(lengths, looked):
    rows = jnp.transpose(looked, (1, 2, 0))
    count = jnp.transpose(lengths, (1, 0))
    slots = rows.shape[1]
    active = [count > j for j in range(slots)]
    row = [rows[:, j, :] for j in range(slots)]
    codes, weights = [], []
    for j in range(slots):
        first = active[j]
        for i in range(j):
            first = first & (row[i] != row[j])
        weight = jnp.ones_like(count)
        for i in range(j + 1, slots):
            weight = weight + (active[i] & (row[i] == row[j])).astype(jnp.int32)
        codes.append(jnp.where(first, coded(row[j]), jnp.zeros((), bf16)))
        weights.append(weight.astype(f32).astype(bf16))
    return jnp.stack(codes + weights, axis=1)


def pack_kernel(*refs):
    grad_ref, out_ref, swap_ref = refs[0], refs[-2], refs[-1]
    samples, tables, width = grad_ref.shape

    @pl.when(pl.program_id(0) == 0)
    def _():
        to = lax.broadcasted_iota(jnp.int32, swap_ref.shape, 0)
        of = lax.broadcasted_iota(jnp.int32, swap_ref.shape, 1)
        hit = ((to & 15) == (of >> 4)) & ((to >> 4) == (of & 15))
        swap_ref[...] = jnp.where(hit, 1.0, 0.0).astype(bf16)

    for first in range(0, samples, 16):
        block = grad_ref[first : first + 16].reshape(16 * tables, width)
        turned = jnp.dot(swap_ref[...], block, preferred_element_type=f32)
        out_ref[:, first : first + 16, :] = turned.astype(bf16).reshape(tables, 16, width)
    if len(refs) == 4:
        out_ref[:, samples : samples + 8, :] = refs[1][...]


def packed(grads, part, codes=()):
    samples, tables, width = grads.shape
    count = samples // parts
    height = count + 8 * len(codes)
    return pl.pallas_call(
        pack_kernel,
        grid=(tables // 16,),
        in_specs=[pl.BlockSpec((count, 16, width), lambda i: (part, i, 0))]
        + [pl.BlockSpec((16, 8, width), lambda i: (i, 0, 0))] * len(codes),
        out_specs=pl.BlockSpec((16, height, width), lambda i: (i, 0, 0)),
        out_shape=jax.ShapeDtypeStruct((tables, height, width), bf16),
        scratch_shapes=[pltpu.VMEM((256, 256), bf16)],
        cost_estimate=pl.CostEstimate(flops=2 * 256 * count * tables * width, bytes_accessed=4 << 20, transcendentals=0),
        name="pack",
    )(grads, *codes)


parts = 2
group = 8
stripe = 256


def sum_kernel(part, base_ref, info_ref, data_ref, *refs):
    out_ref, mine_ref = refs[-2], refs[-1]
    senders, samples, _ = data_ref.shape
    rows = out_ref.shape[0]

    @pl.when(pl.program_id(0) == 0)
    def _():
        out_ref[...] = refs[0][...] if len(refs) == 3 else jnp.zeros_like(out_ref)
        mine_ref[...] = sized(base_ref[0] + lax.broadcasted_iota(jnp.int32, mine_ref.shape, 0)).astype(f32)

    zero = jnp.zeros((), bf16)
    here = slice(part * samples, (part + 1) * samples)
    for first in range(0, senders, group):
        pairs = [
            jnp.concatenate([info_ref[k][:, here], info_ref[k + 1][:, here]], axis=1)
            for k in range(first, first + group, 2)
        ]
        values = jnp.concatenate([data_ref[k, 0:samples, :] for k in range(first, first + group)], axis=0)
        for top in range(0, rows, stripe):
            mine = mine_ref[top : top + stripe, :].astype(bf16)
            hots = []
            for info in pairs:
                hot = jnp.where(mine == info[3:4], info[7:8], zero)
                for j in (2, 1, 0):
                    hot = jnp.where(mine == info[j : j + 1], info[4 + j : 5 + j], hot)
                hots.append(hot)
            out_ref[top : top + stripe, :] += jnp.dot(
                jnp.concatenate(hots, axis=1), values, preferred_element_type=f32
            )


def summed(part, first, data, base, rows, before=()):
    senders, _, width = data.shape
    samples = width // parts
    step = 16
    return pl.pallas_call(
        functools.partial(sum_kernel, part),
        grid_spec=pltpu.PrefetchScalarGridSpec(
            num_scalar_prefetch=1,
            grid=(senders // step,),
            in_specs=[
                pl.BlockSpec((step, 8, width), lambda i, b: (i, samples // 8, 0)),
                pl.BlockSpec((step, samples, width), lambda i, b: (i, 0, 0)),
            ]
            + [pl.BlockSpec((rows, width), lambda i, b: (b[0] // rows, 0))] * len(before),
            out_specs=pl.BlockSpec((rows, width), lambda i, b: (0, 0)),
            scratch_shapes=[pltpu.VMEM((rows, width), f32)],
        ),
        out_shape=jax.ShapeDtypeStruct((rows, width), f32),
        cost_estimate=pl.CostEstimate(flops=2 * senders * samples * rows * width, bytes_accessed=3 << 20, transcendentals=0),
        name="sum_by_row",
    )(base, first, data, *before)


def to_next(value, axis, step):
    return lax.ppermute(value, axis, [(i, (i + step) % ring) for i in range(ring)])


def scattered(value, axis, here):
    arrived = [
        to_next(lax.dynamic_index_in_dim(value, (here + step) & 3, 0, keepdims=False), axis, step)
        for step in range(1, ring)
    ]
    own = lax.dynamic_index_in_dim(value, here, 0, keepdims=False)
    return own + arrived[0] + arrived[1] + arrived[2]


def place_kernel(at_ref, *refs):
    out_ref = refs[-1]
    here_y, here_x, here_z, here_c = (at_ref[k] for k in range(4))
    for number, piece in enumerate(refs[:-1]):
        core, stream, far = number // 8, number // 4 % 2, number % 4
        c = here_c if core == 0 else 1 - here_c
        for near in range(ring):
            dy, dx = (far, near) if stream == 0 else (near, far)
            y = (here_y + ring - dy) % ring
            x = (here_x + ring - dx) % ring
            left = pl.multiple_of((x % 2) * 512 + stream * 256, 256)
            for dz in range(ring):
                z = (here_z + ring - dz) % ring
                top = pl.multiple_of((x // 2) * 512 + c * 256 + y * 64 + z * 16, 16)
                out_ref[pl.ds(top, 16), pl.ds(left, 256)] = piece[near, dz]


def placed(at, pieces):
    return pl.pallas_call(
        place_kernel,
        in_specs=[pl.BlockSpec(memory_space=pltpu.SMEM)] + [pl.BlockSpec(memory_space=pltpu.VMEM)] * len(pieces),
        out_specs=pl.BlockSpec(memory_space=pltpu.VMEM),
        out_shape=jax.ShapeDtypeStruct((1024, 1024), f32),
        cost_estimate=pl.CostEstimate(flops=3 << 20, bytes_accessed=8 << 20, transcendentals=0),
        name="place",
    )(at, *pieces)


def gathered(value, axis):
    return [value] + [to_next(value, axis, step) for step in range(1, ring)]


def dense_sum(inputs, cotangents):
    y, x, c = (lax.axis_index(a) for a in ("y", "x", "c"))
    z = lax.axis_index(deep)

    def share(of):
        one = jnp.where((of & 2) == 0, inputs[:, :512], inputs[:, 512:])
        two = jnp.where((of & 1) == 0, cotangents[:, :512], cotangents[:, 512:])
        return jnp.concatenate([one, two], axis=1)

    parts = [share(x)] + [to_next(share((x + step) & 3), "x", step) for step in range(1, ring)]
    both = jnp.concatenate(parts, axis=0)
    local = lax.dot_general(both[:, :512], both[:, 512:], (((0,), (0,)), ((), ())), preferred_element_type=f32)
    halves = local.reshape(2, 256, 512)
    swap = [(0, 1), (1, 0)]
    other = lax.ppermute(lax.dynamic_index_in_dim(halves, 1 - c, 0, keepdims=False), "c", swap)
    total = lax.dynamic_index_in_dim(halves, c, 0, keepdims=False) + other
    total = scattered(total.reshape(ring, 64, 512), "y", y)
    total = scattered(total.reshape(ring, 16, 512), deep, z)
    total = jnp.stack(gathered(total, deep))
    left, right = (total[..., :256], total[..., 256:])
    left = gathered(jnp.stack(gathered(left, "x")), "y")
    right = gathered(jnp.stack(gathered(right, "y")), "x")
    mine = left + right
    theirs = [lax.ppermute(p, "c", swap) for p in mine]
    return placed(jnp.stack([y, x, z, c]).astype(jnp.int32), mine + theirs)


def per_device(
    pooled_grad, bag_lengths, bag_rows, table_rows, row_accum, dense_input, dense_cotangent
):
    tables, rows = row_accum.shape
    dense_grad = dense_sum(dense_input, dense_cotangent)
    codes = slot_codes(bag_lengths, bag_rows)

    def exchanged(value):
        return lax.all_to_all(value, every, split_axis=0, concat_axis=0, tiled=True)

    first = exchanged(packed(pooled_grad, 0, (codes,)))
    second = exchanged(packed(pooled_grad, 1))
    half = lax.axis_index("zl").astype(jnp.int32)
    early = summed(0, first, first, jnp.zeros((1,), jnp.int32), tables * rows)
    theirs = summed(1, first, second, ((1 - half) * rows)[None], rows, (early,))
    arrived = lax.ppermute(theirs, "zl", [(0, 1), (1, 0)])
    own = summed(1, first, second, (half * rows)[None], rows, (early,))
    row_grad = jnp.where(half == 0, jnp.stack([own, arrived]), jnp.stack([arrived, own]))
    new_accum = row_accum + jnp.mean(row_grad * row_grad, axis=-1)
    new_rows = table_rows - learn_rate * row_grad / jnp.sqrt(new_accum)[..., None]
    return (new_rows, new_accum, dense_grad)


def solution(mesh):
    fine = Mesh(mesh.devices.reshape(4, 4, 2, 2, 2), every)
    samples = P(every)
    owned = P(("y", "x", "zh", "c"), "zl")
    return jax.shard_map(
        per_device,
        mesh=fine,
        in_specs=(samples, samples, samples, owned, owned, samples, samples),
        out_specs=(owned, owned, P()),
        check_vma=False,
    )
```

time: 211 us -> 202 us (0.957)
  waiting for transfers between devices: 87.3 us -> 62.9 us
  starting transfers between devices: 49.3 us -> 66.5 us
  Pallas kernels: 59.7 us -> 53.6 us
  other arithmetic: 6.83 us -> 9.11 us
    ppermute x18 -> x24, waiting for transfers between devices: 85.8 us -> 60.4 us  [to_next(): lax.ppermute(value, axis, [(i, (i + step) % ring) for i in range(ring)])]
    ppermute x18 -> x24, starting transfers between devices: 19.5 us -> 37.9 us  [to_next(): lax.ppermute(value, axis, [(i, (i + step) % ring) for i in range(ring)])]
    pallas_call x2 -> x3, Pallas kernels: 46.9 us -> 35.3 us  [summed(): pl.pallas_call(functools.partial(sum_kernel, part), grid_spec=pltpu.Prefe...]
    ppermute x4 -> x8, starting transfers between devices: 16.8 us -> 7.59 us  [dense_sum(): theirs = [lax.ppermute(p, 'c', swap) for p in mine]]
    all_to_all x1 -> x2, starting transfers between devices: 11.9 us -> 20.1 us  [exchanged(): return lax.all_to_all(value, every, split_axis=0, concat_axis=0, tiled=True)]
    pallas_call x1 -> x2, Pallas kernels: 8.17 us -> 13.5 us  [packed(): pl.pallas_call(pack_kernel, grid=(tables // 16,), in_specs=[pl.BlockSpec(...]
    unnamed x20 -> x44, local copies, waits for them, and re-layouts: 2.81 us -> 5.44 us
  transfers between devices with their start and end apart: 25 -> 36, of which waited for: 16 -> 14; matrix products, arithmetic and copies ran while one was open for 1% -> 2% of each run, Pallas kernels for 24% -> 23%
where the time goes in v2:
time: 202 us; the launch traced here: 201 us
  starting transfers between devices  66.5 us (33%)
  waiting for transfers between devices  62.9 us (31%)
  Pallas kernels  53.6 us (27%)
  other arithmetic  9.11 us (5%)
  local copies, waits for them, and re-layouts  7.41 us (4%)
    ppermute x24, waiting for transfers between devices, to_next(): lax.ppermute(value, axis, [(i, (i + step) % ring) for i in range(ring)])  60.4 us
    ppermute x24, starting transfers between devices, to_next(): lax.ppermute(value, axis, [(i, (i + step) % ring) for i in range(ring)])  37.9 us
    pallas_call x3, Pallas kernels, summed(): pl.pallas_call(functools.partial(sum_kernel, part), grid_spec=pltpu.Prefe...  35.3 us
    all_to_all x2, starting transfers between devices, exchanged(): return lax.all_to_all(value, every, split_axis=0, concat_axis=0, tiled=True)  20.1 us
    pallas_call x2, Pallas kernels, packed(): pl.pallas_call(pack_kernel, grid=(tables // 16,), in_specs=[pl.BlockSpec(...  13.5 us
    ppermute x8, starting transfers between devices, dense_sum(): theirs = [lax.ppermute(p, 'c', swap) for p in mine]  7.59 us
    unnamed x44, local copies, waits for them, and re-layouts  5.44 us
    pallas_call x1, Pallas kernels, placed(): pl.pallas_call(place_kernel, in_specs=[pl.BlockSpec(memory_space=pltpu.SM...  4.79 us
  transfers between devices with their start and end apart: 36, of which 14 were waited for; matrix products, arithmetic and copies ran while one was open for 2% of the time, Pallas kernels for 23%

profile of v2, /device:TPU:1, one launch (start us, length us, event | category | flops | bytes accessed | tf_op | source)
XLA Modules:
  0.0 201.1 jit_solution(14068945019732403948)
XLA Ops:
  0.6 1.1 copy.95
  1.7 0.9 copy.94
  3.4 1.5 stack.109.refs_1_
  4.9 6.8 %pack.2 = bf16[128,72,128]{2,1,0:T(8,128)(2,1)} custom-call(bf16[128,128,128]{2,1,0:T(8,128)(2,1)} %refs_0_.3, bf16[128,8,128]{2,1,0:T(8,128)(2,1)} %stack.109.refs_1_), custom_call_target="tpu_custom_call" | custom-call | flops 536870912 | bytes 4194304 | tf_op jit(solution)/shard_map/pack/pallas_call | solution.py:70
  11.6 11.5 %all-to-all-start = ((bf16[128,72,128]{2,1,0:T(8,128)(2,1)}), bf16[128,72,128]{2,1,0:T(8,128)(2,1)S(1)}, u32[]{:S(2)}, u32[]{:S(2)}) async-start(bf16[128,72,128]{2,1,0:T(8,128)(2,1)} %pack.2), calls=%async_computation | async-start | bytes 4718592 | tf_op jit(solution)/shard_map/all_to_all | solution.py:222
  23.3 2.6 %collective-permute-start.3 = (bf16[128,1024]{1,0:T(8,128)(2,1)S(1)}, bf16[128,1024]{1,0:T(8,128)(2,1)}, u32[]{:S(2)}, u32[]{:S(2)}) collective-permute-start(bf16[128,1024]{1,0:T(8,128)(2,1)S(1)} %pad_maximum_fusion.3), channel_id=1, source_target_pairs={{0,24},{8,0},{16,8},{24,16},{1,25},{9,1},{17,9},{25,17},{2,26},{10... | collective-permute-start | bytes 786440 | tf_op jit(solution)/shard_map/ppermute | solution.py:143
  26.0 0.7 collective-permute-start.2
  26.7 0.6 collective-permute-start.1
  27.3 28.2 %collective-permute-done.3 = bf16[128,1024]{1,0:T(8,128)(2,1)} collective-permute-done((bf16[128,1024]{1,0:T(8,128)(2,1)S(1)}, bf16[128,1024]{1,0:T(8,128)(2,1)}, u32[]{:S(2)}, u32[]{:S(2)}) %collective-permute-start.3) | collective-permute-done | bytes 262176 | tf_op jit(solution)/shard_map/ppermute | solution.py:143
  55.5 1.5 collective-permute-done.2
  57.0 5.5 %collective-permute-done.1 = bf16[128,1024]{1,0:T(8,128)(2,1)} collective-permute-done((bf16[128,1024]{1,0:T(8,128)(2,1)S(1)}, bf16[128,1024]{1,0:T(8,128)(2,1)}, u32[]{:S(2)}, u32[]{:S(2)}) %collective-permute-start.1) | collective-permute-done | bytes 262176 | tf_op jit(solution)/shard_map/ppermute | solution.py:143
  62.5 1.2 pad_maximum_fusion
  63.7 0.5 fusion
  64.2 1.0 copy-done.4
  65.2 0.9 collective-permute-start.4
  66.1 1.5 collective-permute-done.4
  67.6 1.1 bitcast_add_fusion
  68.8 2.6 %collective-permute-start.7 = (f32[64,512]{1,0:T(8,128)S(1)}, f32[64,512]{1,0:T(8,128)S(1)}, u32[]{:S(2)}, u32[]{:S(2)}) collective-permute-start(f32[64,512]{1,0:T(8,128)S(1)} %get-tuple-element.12), channel_id=1, source_target_pairs={{0,96},{32,0},{64,32},{96,64},{1,97},{33,1},{65,33},{97,65},{2,98}... | collective-permute-start | bytes 393224 | tf_op jit(solution)/shard_map/ppermute | solution.py:143
  71.3 0.5 collective-permute-start.6
  71.8 0.6 collective-permute-start.5
  72.4 6.8 %pack.3 = bf16[128,64,128]{2,1,0:T(8,128)(2,1)} custom-call(bf16[128,128,128]{2,1,0:T(8,128)(2,1)} %refs_0_.3), custom_call_target="tpu_custom_call" | custom-call | flops 536870912 | bytes 4194304 | tf_op jit(solution)/shard_map/pack/pallas_call | solution.py:70
  79.2 1.4 copy-done
  80.6 8.7 %all-to-all-start.1 = ((bf16[128,64,128]{2,1,0:T(8,128)(2,1)}), bf16[128,64,128]{2,1,0:T(8,128)(2,1)}, u32[]{:S(2)}, u32[]{:S(2)}) async-start(bf16[128,64,128]{2,1,0:T(8,128)(2,1)} %pack.3), calls=%async_computation.1 | async-start | bytes 4194304 | tf_op jit(solution)/shard_map/all_to_all | solution.py:222
  89.3 0.9 fusion.4
  90.3 3.3 %collective-permute-start.10 = (f32[16,512]{1,0:T(8,128)S(1)}, f32[16,512]{1,0:T(8,128)S(1)}, u32[]{:S(2)}, u32[]{:S(2)}) collective-permute-start(f32[16,512]{1,0:T(8,128)S(1)} %get-tuple-element.31), channel_id=1, source_target_pairs={{0,5},{1,0},{4,1},{5,4},{2,7},{3,2},{6,3},{7,6},{8,13},{9,8},{12,9... | collective-permute-start | bytes 98312 | tf_op jit(solution)/shard_map/ppermute | solution.py:143
  93.7 0.8 collective-permute-start.8
  94.5 13.0 %collective-permute-done.10 = f32[16,512]{1,0:T(8,128)S(1)} collective-permute-done((f32[16,512]{1,0:T(8,128)S(1)}, f32[16,512]{1,0:T(8,128)S(1)}, u32[]{:S(2)}, u32[]{:S(2)}) %collective-permute-start.10) | collective-permute-done | bytes 32800 | tf_op jit(solution)/shard_map/ppermute | solution.py:143
  107.5 0.9 collective-permute-done.9
  108.4 3.7 %collective-permute-done.8 = f32[16,512]{1,0:T(8,128)S(1)} collective-permute-done((f32[16,512]{1,0:T(8,128)S(1)}, f32[16,512]{1,0:T(8,128)S(1)}, u32[]{:S(2)}, u32[]{:S(2)}) %collective-permute-start.8) | collective-permute-done | bytes 32800 | tf_op jit(solution)/shard_map/ppermute | solution.py:143
  112.1 3.0 %collective-permute-start.13 = (f32[16,512]{1,0:T(8,128)S(1)}, f32[16,512]{1,0:T(8,128)S(1)}, u32[]{:S(2)}, u32[]{:S(2)}) collective-permute-start(f32[16,512]{1,0:T(8,128)S(1)} %fusion.21), channel_id=1, source_target_pairs={{0,5},{1,0},{4,1},{5,4},{2,7},{3,2},{6,3},{7,6},{8,13},{9,8},{12,9... | collective-permute-start | bytes 98312 | tf_op jit(solution)/shard_map/ppermute | solution.py:143
  115.1 2.0 collective-permute-start.12
  117.1 0.8 collective-permute-start.11
  117.9 1.8 collective-permute-done.12
  119.7 1.4 collective-permute-done.11
  121.1 3.6 %collective-permute-start.16 = (f32[4,16,256]{2,1,0:T(8,128)S(1)}, f32[4,16,256]{2,1,0:T(8,128)S(1)}, u32[]{:S(2)}, u32[]{:S(2)}) collective-permute-start(f32[4,16,256]{2,1,0:T(8,128)S(1)} %get-tuple-element.29), channel_id=1, source_target_pairs={{0,24},{8,0},{16,8},{24,16},{1,25},{9,1},{17,9},{25,17},{2,26},{10... | collective-permute-start | bytes 196616 | tf_op jit(solution)/shard_map/ppermute | solution.py:143
  124.7 0.8 collective-permute-start.15
  125.5 0.8 collective-permute-start.14
  126.3 3.0 %collective-permute-start.22 = (f32[4,16,256]{2,1,0:T(8,128)S(1)}, f32[4,16,256]{2,1,0:T(8,128)S(1)}, u32[]{:S(2)}, u32[]{:S(2)}) collective-permute-start(f32[4,16,256]{2,1,0:T(8,128)S(1)} %get-tuple-element.28), channel_id=1, source_target_pairs={{0,96},{32,0},{64,32},{96,64},{1,97},{33,1},{65,33},{97,65},{2,98}... | collective-permute-start | bytes 196616 | tf_op jit(solution)/shard_map/ppermute | solution.py:143
  129.2 0.6 collective-permute-start.21
  129.9 0.9 collective-permute-start.20
  130.8 1.2 collective-permute-start.17
  132.0 2.6 %collective-permute-start.18 = (f32[4,4,16,256]{3,2,1,0:T(8,128)S(1)}, f32[4,4,16,256]{3,2,1,0:T(8,128)S(1)}, u32[]{:S(2)}, u32[]{:S(2)}) collective-permute-start(f32[4,4,16,256]{3,2,1,0:T(8,128)S(1)} %pad_maximum_fusion.4.refs_0_), channel_id=1, source_target_pairs={{0,64},{32,96},{64,0},{96,32},{1,65},{33,97},{65,1},{97,33},{2,66}... | collective-permute-start | bytes 786440 | tf_op jit(solution)/shard_map/ppermute | solution.py:143
  134.6 1.6 collective-permute-start.19
  136.3 0.3 collective-permute-start.23
  136.5 1.8 collective-permute-start.24
  138.4 0.3 collective-permute-done.17.refs_1_
  138.7 3.2 %collective-permute-start.25 = (f32[4,4,16,256]{3,2,1,0:T(8,128)S(1)}, f32[4,4,16,256]{3,2,1,0:T(8,128)S(1)}, u32[]{:S(2)}, u32[]{:S(2)}) collective-permute-start(f32[4,4,16,256]{3,2,1,0:T(8,128)S(1)} %pad_maximum_fusion.5.refs_4_), channel_id=1, source_target_pairs={{0,24},{8,0},{16,8},{24,16},{1,25},{9,1},{17,9},{25,17},{2,26},{10... | collective-permute-start | bytes 786440 | tf_op jit(solution)/shard_map/ppermute | solution.py:143
  141.9 4.0 %collective-permute-done.18.refs_2_ = f32[4,4,16,256]{3,2,1,0:T(8,128)S(1)} collective-permute-done((f32[4,4,16,256]{3,2,1,0:T(8,128)S(1)}, f32[4,4,16,256]{3,2,1,0:T(8,128)S(1)}, u32[]{:S(2)}, u32[]{:S(2)}) %collective-permute-start.18) | collective-permute-done | bytes 262176 | tf_op jit(solution)/shard_map/ppermute | solution.py:143
  145.9 3.0 %collective-permute-start.26 = (f32[4,4,16,256]{3,2,1,0:T(8,128)S(1)}, f32[4,4,16,256]{3,2,1,0:T(8,128)S(1)}, u32[]{:S(2)}, u32[]{:S(2)}) collective-permute-start(f32[4,4,16,256]{3,2,1,0:T(8,128)S(1)} %pad_maximum_fusion.4.refs_0_), channel_id=1, source_target_pairs={{0,2},{2,0},{1,3},{3,1},{4,6},{6,4},{5,7},{7,5},{8,10},{10,8},{9,1... | collective-permute-start | bytes 786440 | tf_op jit(solution)/shard_map/ppermute | solution.py:210
  149.0 3.1 %collective-permute-start.27 = (f32[4,4,16,256]{3,2,1,0:T(8,128)S(1)}, f32[4,4,16,256]{3,2,1,0:T(8,128)S(1)}, u32[]{:S(2)}, u32[]{:S(2)}) collective-permute-start(f32[4,4,16,256]{3,2,1,0:T(8,128)S(1)} %collective-permute-done.17.refs_1_), channel_id=1, source_target_pairs={{0,2},{2,0},{1,3},{3,1},{4,6},{6,4},{5,7},{7,5},{8,10},{10,8},{9,1... | collective-permute-start | bytes 786440 | tf_op jit(solution)/shard_map/ppermute | solution.py:210
  152.2 15.7 %sum_by_row.3.refs_0_ = f32[2048,128]{1,0:T(8,128)} custom-call(s32[1]{0:T(128)} %constant.72.clone.1.base_ref, bf16[128,72,128]{2,1,0:T(8,128)(2,1)} %copy-done, bf16[128,72,128]{2,1,0:T(8,128)(2,1)} %copy-done), custom_call_target="tpu_custom_call" | custom-call | flops 4294967296 | bytes 3145728 | tf_op jit(solution)/shard_map/sum_by_row/pallas_call | solution.py:123
  167.9 9.8 %sum_by_row.5 = f32[1024,128]{1,0:T(8,128)} custom-call(s32[1]{0:T(128)} %bitcast.34.base_ref, bf16[128,72,128]{2,1,0:T(8,128)(2,1)} %copy-done, bf16[128,64,128]{2,1,0:T(8,128)(2,1)} %all-to-all-done.1.data_ref, f32[2048,128]{1,0:T(8,128)} %sum_by_row.3.refs_0_), custom_call_target="tpu_custom_call" | custom-call | flops 2147483648 | bytes 3145728 | tf_op jit(solution)/shard_map/sum_by_row/pallas_call | solution.py:123
  177.8 0.5 collective-permute-start.29
  178.5 0.5 collective-permute-start.32
  179.1 0.7 pad_add_fusion.at_ref
  180.0 0.4 collective-permute-done.32.refs_14_
  180.3 0.4 collective-permute-done.33.refs_15_
  180.7 0.3 copy-done.18
  181.0 0.7 copy-done.19
  181.7 4.8 %place.1 = f32[1024,1024]{1,0:T(8,128)} custom-call(s32[4]{0:T(128)} %pad_add_fusion.at_ref, f32[4,4,16,256]{3,2,1,0:T(8,128)} %copy-done.1, f32[4,4,16,256]{3,2,1,0:T(8,128)} %copy-done.7, f32[4,4,16,256]{3,2,1,0:T(8,128)} %copy-done.8, f32[4,4,16,256]{3,2,1,0:T(8,128)} %copy-done.9, f32[4,4,16,256]{3,2,1,0:T(8,128)} %copy-done.2, ...), custom_call_target="tpu_custom_call" | custom-call | flops 3145728 | bytes 8388608 | tf_op jit(solution)/shard_map/place/pallas_call | solution.py:173
  186.5 9.8 %sum_by_row.4 = f32[1024,128]{1,0:T(8,128)} custom-call(s32[1]{0:T(128)} %bitcast.base_ref, bf16[128,72,128]{2,1,0:T(8,128)(2,1)} %copy-done, bf16[128,64,128]{2,1,0:T(8,128)(2,1)} %all-to-all-done.1.data_ref, f32[2048,128]{1,0:T(8,128)} %sum_by_row.3.refs_0_), custom_call_target="tpu_custom_call" | custom-call | flops 2147483648 | bytes 3145728 | tf_op jit(solution)/shard_map/sum_by_row/pallas_call | solution.py:123
  196.4 1.6 multiply_reduce_fusion
  198.0 0.6 fusion.25
  198.6 2.5 %divide_subtract_fusion = f32[2,1024,128]{2,1,0:T(8,128)} fusion(f32[2,1024,128]{2,1,0:T(8,128)S(1)} %copy-done.3, f32[1,1024,128]{2,1,0:T(8,128)} %bitcast.219, f32[1,1024,128]{2,1,0:T(8,128)S(1)} %bitcast.217, f32[2,1024]{1,0:T(2,128)S(1)} %get-tuple-element.3, pred[]{:T(512)S(6)} %eq.63), kind=kLoop, calls=%fused_computation.2 | loop fusion | flops 1572864 | bytes 3153921 | tf_op jit(solution)/shard_map/sub | solution.py:233
  (92 shorter events, 1.9 us)
Async XLA Ops:
  11.6 11.5 %copy-start.5 = (bf16[128,1024]{1,0:T(8,128)(2,1)S(1)}, bf16[128,1024]{1,0:T(8,128)(2,1)}, u32[]{:S(2)}) copy-start(bf16[128,1024]{1,0:T(8,128)(2,1)} %param.13) | copy-start | bytes 786436
  11.6 11.6 %copy-start.6 = (bf16[128,1024]{1,0:T(8,128)(2,1)S(1)}, bf16[128,1024]{1,0:T(8,128)(2,1)}, u32[]{:S(2)}) copy-start(bf16[128,1024]{1,0:T(8,128)(2,1)} %param.12) | copy-start | bytes 786436
  11.6 67.5 %all-to-all-start = ((bf16[128,72,128]{2,1,0:T(8,128)(2,1)}), bf16[128,72,128]{2,1,0:T(8,128)(2,1)S(1)}, u32[]{:S(2)}, u32[]{:S(2)}) async-start(bf16[128,72,128]{2,1,0:T(8,128)(2,1)} %pack.2), calls=%async_computation | async-start | bytes 4718592 | tf_op jit(solution)/shard_map/all_to_all | solution.py:222
  23.3 32.2 %collective-permute-start.3 = (bf16[128,1024]{1,0:T(8,128)(2,1)S(1)}, bf16[128,1024]{1,0:T(8,128)(2,1)}, u32[]{:S(2)}, u32[]{:S(2)}) collective-permute-start(bf16[128,1024]{1,0:T(8,128)(2,1)S(1)} %pad_maximum_fusion.3), channel_id=1, source_target_pairs={{0,24},{8,0},{16,8},{24,16},{1,25},{9,1},{17,9},{25,17},{2,26},{10... | collective-permute-start | bytes 786440 | tf_op jit(solution)/shard_map/ppermute | solution.py:143
  26.0 31.0 %collective-permute-start.2 = (bf16[128,1024]{1,0:T(8,128)(2,1)S(1)}, bf16[128,1024]{1,0:T(8,128)(2,1)}, u32[]{:S(2)}, u32[]{:S(2)}) collective-permute-start(bf16[128,1024]{1,0:T(8,128)(2,1)S(1)} %pad_maximum_fusion.2), channel_id=1, source_target_pairs={{0,16},{8,24},{16,0},{24,8},{1,17},{9,25},{17,1},{25,9},{2,18},{10... | collective-permute-start | bytes 786440 | tf_op jit(solution)/shard_map/ppermute | solution.py:143
  26.7 35.9 %collective-permute-start.1 = (bf16[128,1024]{1,0:T(8,128)(2,1)S(1)}, bf16[128,1024]{1,0:T(8,128)(2,1)}, u32[]{:S(2)}, u32[]{:S(2)}) collective-permute-start(bf16[128,1024]{1,0:T(8,128)(2,1)S(1)} %pad_maximum_fusion.1), channel_id=1, source_target_pairs={{0,8},{8,16},{16,24},{24,0},{1,9},{9,17},{17,25},{25,1},{2,10},{10... | collective-permute-start | bytes 786440 | tf_op jit(solution)/shard_map/ppermute | solution.py:143
  64.2 1.0 copy-start.4
  65.2 2.4 %collective-permute-start.4 = (f32[256,512]{1,0:T(8,128)S(1)}, f32[256,512]{1,0:T(8,128)S(1)}, u32[]{:S(2)}, u32[]{:S(2)}) collective-permute-start(f32[256,512]{1,0:T(8,128)S(1)} %dynamic-slice_bitcast_fusion), channel_id=1, source_target_pairs={{0,2},{2,0},{1,3},{3,1},{4,6},{6,4},{5,7},{7,5},{8,10},{10,8},{9,1... | collective-permute-start | bytes 1572872 | tf_op jit(solution)/shard_map/ppermute | solution.py:201
  68.8 20.5 %collective-permute-start.7 = (f32[64,512]{1,0:T(8,128)S(1)}, f32[64,512]{1,0:T(8,128)S(1)}, u32[]{:S(2)}, u32[]{:S(2)}) collective-permute-start(f32[64,512]{1,0:T(8,128)S(1)} %get-tuple-element.12), channel_id=1, source_target_pairs={{0,96},{32,0},{64,32},{96,64},{1,97},{33,1},{65,33},{97,65},{2,98}... | collective-permute-start | bytes 393224 | tf_op jit(solution)/shard_map/ppermute | solution.py:143
  71.3 17.9 %collective-permute-start.6 = (f32[64,512]{1,0:T(8,128)S(1)}, f32[64,512]{1,0:T(8,128)S(1)}, u32[]{:S(2)}, u32[]{:S(2)}) collective-permute-start(f32[64,512]{1,0:T(8,128)S(1)} %get-tuple-element.13), channel_id=1, source_target_pairs={{0,64},{32,96},{64,0},{96,32},{1,65},{33,97},{65,1},{97,33},{2,66}... | collective-permute-start | bytes 393224 | tf_op jit(solution)/shard_map/ppermute | solution.py:143
  71.8 17.5 %collective-permute-start.5 = (f32[64,512]{1,0:T(8,128)S(1)}, f32[64,512]{1,0:T(8,128)}, u32[]{:S(2)}, u32[]{:S(2)}) collective-permute-start(f32[64,512]{1,0:T(8,128)S(1)} %get-tuple-element.11), channel_id=1, source_target_pairs={{0,32},{32,64},{64,96},{96,0},{1,33},{33,65},{65,97},{97,1},{2,34}... | collective-permute-start | bytes 393224 | tf_op jit(solution)/shard_map/ppermute | solution.py:143
  79.2 1.4 copy-start
  80.6 87.3 %all-to-all-start.1 = ((bf16[128,64,128]{2,1,0:T(8,128)(2,1)}), bf16[128,64,128]{2,1,0:T(8,128)(2,1)}, u32[]{:S(2)}, u32[]{:S(2)}) async-start(bf16[128,64,128]{2,1,0:T(8,128)(2,1)} %pack.3), calls=%async_computation.1 | async-start | bytes 4194304 | tf_op jit(solution)/shard_map/all_to_all | solution.py:222
  90.3 17.2 %collective-permute-start.10 = (f32[16,512]{1,0:T(8,128)S(1)}, f32[16,512]{1,0:T(8,128)S(1)}, u32[]{:S(2)}, u32[]{:S(2)}) collective-permute-start(f32[16,512]{1,0:T(8,128)S(1)} %get-tuple-element.31), channel_id=1, source_target_pairs={{0,5},{1,0},{4,1},{5,4},{2,7},{3,2},{6,3},{7,6},{8,13},{9,8},{12,9... | collective-permute-start | bytes 98312 | tf_op jit(solution)/shard_map/ppermute | solution.py:143
  93.6 14.8 %collective-permute-start.9 = (f32[16,512]{1,0:T(8,128)S(1)}, f32[16,512]{1,0:T(8,128)S(1)}, u32[]{:S(2)}, u32[]{:S(2)}) collective-permute-start(f32[16,512]{1,0:T(8,128)S(1)} %get-tuple-element.32), channel_id=1, source_target_pairs={{0,4},{1,5},{4,0},{5,1},{2,6},{3,7},{6,2},{7,3},{8,12},{9,13},{12,... | collective-permute-start | bytes 98312 | tf_op jit(solution)/shard_map/ppermute | solution.py:143
  93.7 18.4 %collective-permute-start.8 = (f32[16,512]{1,0:T(8,128)S(1)}, f32[16,512]{1,0:T(8,128)S(1)}, u32[]{:S(2)}, u32[]{:S(2)}) collective-permute-start(f32[16,512]{1,0:T(8,128)S(1)} %get-tuple-element.30), channel_id=1, source_target_pairs={{0,1},{1,4},{4,5},{5,0},{2,3},{3,6},{6,7},{7,2},{8,9},{9,12},{12,1... | collective-permute-start | bytes 98312 | tf_op jit(solution)/shard_map/ppermute | solution.py:143
  112.1 5.7 %collective-permute-start.13 = (f32[16,512]{1,0:T(8,128)S(1)}, f32[16,512]{1,0:T(8,128)S(1)}, u32[]{:S(2)}, u32[]{:S(2)}) collective-permute-start(f32[16,512]{1,0:T(8,128)S(1)} %fusion.21), channel_id=1, source_target_pairs={{0,5},{1,0},{4,1},{5,4},{2,7},{3,2},{6,3},{7,6},{8,13},{9,8},{12,9... | collective-permute-start | bytes 98312 | tf_op jit(solution)/shard_map/ppermute | solution.py:143
  115.1 4.6 %collective-permute-start.12 = (f32[16,512]{1,0:T(8,128)S(1)}, f32[16,512]{1,0:T(8,128)S(1)}, u32[]{:S(2)}, u32[]{:S(2)}) collective-permute-start(f32[16,512]{1,0:T(8,128)S(1)} %fusion.21), channel_id=1, source_target_pairs={{0,4},{1,5},{4,0},{5,1},{2,6},{3,7},{6,2},{7,3},{8,12},{9,13},{12,... | collective-permute-start | bytes 98312 | tf_op jit(solution)/shard_map/ppermute | solution.py:143
  117.1 4.0 %collective-permute-start.11 = (f32[16,512]{1,0:T(8,128)S(1)}, f32[16,512]{1,0:T(8,128)S(1)}, u32[]{:S(2)}, u32[]{:S(2)}) collective-permute-start(f32[16,512]{1,0:T(8,128)S(1)} %fusion.21), channel_id=1, source_target_pairs={{0,1},{1,4},{4,5},{5,0},{2,3},{3,6},{6,7},{7,2},{8,9},{9,12},{12,1... | collective-permute-start | bytes 98312 | tf_op jit(solution)/shard_map/ppermute | solution.py:143
  121.1 8.8 %collective-permute-start.16 = (f32[4,16,256]{2,1,0:T(8,128)S(1)}, f32[4,16,256]{2,1,0:T(8,128)S(1)}, u32[]{:S(2)}, u32[]{:S(2)}) collective-permute-start(f32[4,16,256]{2,1,0:T(8,128)S(1)} %get-tuple-element.29), channel_id=1, source_target_pairs={{0,24},{8,0},{16,8},{24,16},{1,25},{9,1},{17,9},{25,17},{2,26},{10... | collective-permute-start | bytes 196616 | tf_op jit(solution)/shard_map/ppermute | solution.py:143
  124.7 6.0 %collective-permute-start.15 = (f32[4,16,256]{2,1,0:T(8,128)S(1)}, f32[4,16,256]{2,1,0:T(8,128)S(1)}, u32[]{:S(2)}, u32[]{:S(2)}) collective-permute-start(f32[4,16,256]{2,1,0:T(8,128)S(1)} %get-tuple-element.29), channel_id=1, source_target_pairs={{0,16},{8,24},{16,0},{24,8},{1,17},{9,25},{17,1},{25,9},{2,18},{10... | collective-permute-start | bytes 196616 | tf_op jit(solution)/shard_map/ppermute | solution.py:143
  125.5 5.2 %collective-permute-start.14 = (f32[4,16,256]{2,1,0:T(8,128)S(1)}, f32[4,16,256]{2,1,0:T(8,128)S(1)}, u32[]{:S(2)}, u32[]{:S(2)}) collective-permute-start(f32[4,16,256]{2,1,0:T(8,128)S(1)} %get-tuple-element.29), channel_id=1, source_target_pairs={{0,8},{8,16},{16,24},{24,0},{1,9},{9,17},{17,25},{25,1},{2,10},{10... | collective-permute-start | bytes 196616 | tf_op jit(solution)/shard_map/ppermute | solution.py:143
  126.3 8.4 %collective-permute-start.22 = (f32[4,16,256]{2,1,0:T(8,128)S(1)}, f32[4,16,256]{2,1,0:T(8,128)S(1)}, u32[]{:S(2)}, u32[]{:S(2)}) collective-permute-start(f32[4,16,256]{2,1,0:T(8,128)S(1)} %get-tuple-element.28), channel_id=1, source_target_pairs={{0,96},{32,0},{64,32},{96,64},{1,97},{33,1},{65,33},{97,65},{2,98}... | collective-permute-start | bytes 196616 | tf_op jit(solution)/shard_map/ppermute | solution.py:143
  129.2 7.0 %collective-permute-start.21 = (f32[4,16,256]{2,1,0:T(8,128)S(1)}, f32[4,16,256]{2,1,0:T(8,128)S(1)}, u32[]{:S(2)}, u32[]{:S(2)}) collective-permute-start(f32[4,16,256]{2,1,0:T(8,128)S(1)} %get-tuple-element.28), channel_id=1, source_target_pairs={{0,64},{32,96},{64,0},{96,32},{1,65},{33,97},{65,1},{97,33},{2,66}... | collective-permute-start | bytes 196616 | tf_op jit(solution)/shard_map/ppermute | solution.py:143
  129.9 6.4 %collective-permute-start.20 = (f32[4,16,256]{2,1,0:T(8,128)S(1)}, f32[4,16,256]{2,1,0:T(8,128)S(1)}, u32[]{:S(2)}, u32[]{:S(2)}) collective-permute-start(f32[4,16,256]{2,1,0:T(8,128)S(1)} %get-tuple-element.28), channel_id=1, source_target_pairs={{0,32},{32,64},{64,96},{96,0},{1,33},{33,65},{65,97},{97,1},{2,34}... | collective-permute-start | bytes 196616 | tf_op jit(solution)/shard_map/ppermute | solution.py:143
  130.8 37.1 %copy-start.1 = (f32[4,4,16,256]{3,2,1,0:T(8,128)}, f32[4,4,16,256]{3,2,1,0:T(8,128)S(1)}, u32[]{:S(2)}) copy-start(f32[4,4,16,256]{3,2,1,0:T(8,128)S(1)} %pad_maximum_fusion.4.refs_0_) | copy-start | bytes 786436
  130.8 7.9 %collective-permute-start.17 = (f32[4,4,16,256]{3,2,1,0:T(8,128)S(1)}, f32[4,4,16,256]{3,2,1,0:T(8,128)S(1)}, u32[]{:S(2)}, u32[]{:S(2)}) collective-permute-start(f32[4,4,16,256]{3,2,1,0:T(8,128)S(1)} %pad_maximum_fusion.4.refs_0_), channel_id=1, source_target_pairs={{0,32},{32,64},{64,96},{96,0},{1,33},{33,65},{65,97},{97,1},{2,34}... | collective-permute-start | bytes 786440 | tf_op jit(solution)/shard_map/ppermute | solution.py:143
  132.0 13.9 %collective-permute-start.18 = (f32[4,4,16,256]{3,2,1,0:T(8,128)S(1)}, f32[4,4,16,256]{3,2,1,0:T(8,128)S(1)}, u32[]{:S(2)}, u32[]{:S(2)}) collective-permute-start(f32[4,4,16,256]{3,2,1,0:T(8,128)S(1)} %pad_maximum_fusion.4.refs_0_), channel_id=1, source_target_pairs={{0,64},{32,96},{64,0},{96,32},{1,65},{33,97},{65,1},{97,33},{2,66}... | collective-permute-start | bytes 786440 | tf_op jit(solution)/shard_map/ppermute | solution.py:143
  134.6 14.3 %collective-permute-start.19 = (f32[4,4,16,256]{3,2,1,0:T(8,128)S(1)}, f32[4,4,16,256]{3,2,1,0:T(8,128)S(1)}, u32[]{:S(2)}, u32[]{:S(2)}) collective-permute-start(f32[4,4,16,256]{3,2,1,0:T(8,128)S(1)} %pad_maximum_fusion.4.refs_0_), channel_id=1, source_target_pairs={{0,96},{32,0},{64,32},{96,64},{1,97},{33,1},{65,33},{97,65},{2,98}... | collective-permute-start | bytes 786440 | tf_op jit(solution)/shard_map/ppermute | solution.py:143
  136.3 31.6 %copy-start.2 = (f32[4,4,16,256]{3,2,1,0:T(8,128)}, f32[4,4,16,256]{3,2,1,0:T(8,128)S(1)}, u32[]{:S(2)}) copy-start(f32[4,4,16,256]{3,2,1,0:T(8,128)S(1)} %pad_maximum_fusion.5.refs_4_) | copy-start | bytes 786436
  136.3 12.7 %collective-permute-start.23 = (f32[4,4,16,256]{3,2,1,0:T(8,128)S(1)}, f32[4,4,16,256]{3,2,1,0:T(8,128)S(1)}, u32[]{:S(2)}, u32[]{:S(2)}) collective-permute-start(f32[4,4,16,256]{3,2,1,0:T(8,128)S(1)} %pad_maximum_fusion.5.refs_4_), channel_id=1, source_target_pairs={{0,8},{8,16},{16,24},{24,0},{1,9},{9,17},{17,25},{25,1},{2,10},{10... | collective-permute-start | bytes 786440 | tf_op jit(solution)/shard_map/ppermute | solution.py:143
  136.5 15.5 %collective-permute-start.24 = (f32[4,4,16,256]{3,2,1,0:T(8,128)S(1)}, f32[4,4,16,256]{3,2,1,0:T(8,128)S(1)}, u32[]{:S(2)}, u32[]{:S(2)}) collective-permute-start(f32[4,4,16,256]{3,2,1,0:T(8,128)S(1)} %pad_maximum_fusion.5.refs_4_), channel_id=1, source_target_pairs={{0,16},{8,24},{16,0},{24,8},{1,17},{9,25},{17,1},{25,9},{2,18},{10... | collective-permute-start | bytes 786440 | tf_op jit(solution)/shard_map/ppermute | solution.py:143
  138.7 29.1 %copy-start.7 = (f32[4,4,16,256]{3,2,1,0:T(8,128)}, f32[4,4,16,256]{3,2,1,0:T(8,128)S(1)}, u32[]{:S(2)}) copy-start(f32[4,4,16,256]{3,2,1,0:T(8,128)S(1)} %collective-permute-done.17.refs_1_) | copy-start | bytes 786436
  138.7 39.0 %collective-permute-start.25 = (f32[4,4,16,256]{3,2,1,0:T(8,128)S(1)}, f32[4,4,16,256]{3,2,1,0:T(8,128)S(1)}, u32[]{:S(2)}, u32[]{:S(2)}) collective-permute-start(f32[4,4,16,256]{3,2,1,0:T(8,128)S(1)} %pad_maximum_fusion.5.refs_4_), channel_id=1, source_target_pairs={{0,24},{8,0},{16,8},{24,16},{1,25},{9,1},{17,9},{25,17},{2,26},{10... | collective-permute-start | bytes 786440 | tf_op jit(solution)/shard_map/ppermute | solution.py:143
  145.9 22.0 %copy-start.8 = (f32[4,4,16,256]{3,2,1,0:T(8,128)}, f32[4,4,16,256]{3,2,1,0:T(8,128)S(1)}, u32[]{:S(2)}) copy-start(f32[4,4,16,256]{3,2,1,0:T(8,128)S(1)} %collective-permute-done.18.refs_2_) | copy-start | bytes 786436
  145.9 31.9 %collective-permute-start.26 = (f32[4,4,16,256]{3,2,1,0:T(8,128)S(1)}, f32[4,4,16,256]{3,2,1,0:T(8,128)S(1)}, u32[]{:S(2)}, u32[]{:S(2)}) collective-permute-start(f32[4,4,16,256]{3,2,1,0:T(8,128)S(1)} %pad_maximum_fusion.4.refs_0_), channel_id=1, source_target_pairs={{0,2},{2,0},{1,3},{3,1},{4,6},{6,4},{5,7},{7,5},{8,10},{10,8},{9,1... | collective-permute-start | bytes 786440 | tf_op jit(solution)/shard_map/ppermute | solution.py:210
  148.9 28.9 %copy-start.9 = (f32[4,4,16,256]{3,2,1,0:T(8,128)}, f32[4,4,16,256]{3,2,1,0:T(8,128)S(1)}, u32[]{:S(2)}) copy-start(f32[4,4,16,256]{3,2,1,0:T(8,128)S(1)} %collective-permute-done.19.refs_3_) | copy-start | bytes 786436
  148.9 29.4 %collective-permute-start.30 = (f32[4,4,16,256]{3,2,1,0:T(8,128)S(1)}, f32[4,4,16,256]{3,2,1,0:T(8,128)S(1)}, u32[]{:S(2)}, u32[]{:S(2)}) collective-permute-start(f32[4,4,16,256]{3,2,1,0:T(8,128)S(1)} %pad_maximum_fusion.5.refs_4_), channel_id=1, source_target_pairs={{0,2},{2,0},{1,3},{3,1},{4,6},{6,4},{5,7},{7,5},{8,10},{10,8},{9,1... | collective-permute-start | bytes 786440 | tf_op jit(solution)/shard_map/ppermute | solution.py:210
  149.0 29.4 %copy-start.10 = (f32[4,4,16,256]{3,2,1,0:T(8,128)}, f32[4,4,16,256]{3,2,1,0:T(8,128)S(1)}, u32[]{:S(2)}) copy-start(f32[4,4,16,256]{3,2,1,0:T(8,128)S(1)} %collective-permute-done.23.refs_5_) | copy-start | bytes 786436
  149.0 29.5 %collective-permute-start.27 = (f32[4,4,16,256]{3,2,1,0:T(8,128)S(1)}, f32[4,4,16,256]{3,2,1,0:T(8,128)S(1)}, u32[]{:S(2)}, u32[]{:S(2)}) collective-permute-start(f32[4,4,16,256]{3,2,1,0:T(8,128)S(1)} %collective-permute-done.17.refs_1_), channel_id=1, source_target_pairs={{0,2},{2,0},{1,3},{3,1},{4,6},{6,4},{5,7},{7,5},{8,10},{10,8},{9,1... | collective-permute-start | bytes 786440 | tf_op jit(solution)/shard_map/ppermute | solution.py:210
  152.1 26.4 %copy-start.11 = (f32[4,4,16,256]{3,2,1,0:T(8,128)}, f32[4,4,16,256]{3,2,1,0:T(8,128)S(1)}, u32[]{:S(2)}) copy-start(f32[4,4,16,256]{3,2,1,0:T(8,128)S(1)} %collective-permute-done.24.refs_6_) | copy-start | bytes 786436
  152.1 26.9 %collective-permute-start.28 = (f32[4,4,16,256]{3,2,1,0:T(8,128)S(1)}, f32[4,4,16,256]{3,2,1,0:T(8,128)}, u32[]{:S(2)}, u32[]{:S(2)}) collective-permute-start(f32[4,4,16,256]{3,2,1,0:T(8,128)S(1)} %collective-permute-done.18.refs_2_), channel_id=1, source_target_pairs={{0,2},{2,0},{1,3},{3,1},{4,6},{6,4},{5,7},{7,5},{8,10},{10,8},{9,1... | collective-permute-start | bytes 786440 | tf_op jit(solution)/shard_map/ppermute | solution.py:210
  177.7 3.0 %copy-start.12 = (f32[4,4,16,256]{3,2,1,0:T(8,128)}, f32[4,4,16,256]{3,2,1,0:T(8,128)S(1)}, u32[]{:S(2)}) copy-start(f32[4,4,16,256]{3,2,1,0:T(8,128)S(1)} %collective-permute-done.25.refs_7_) | copy-start | bytes 786436
  177.7 18.7 %collective-permute-start = (f32[1024,128]{1,0:T(8,128)}, f32[1024,128]{1,0:T(8,128)S(1)}, u32[]{:S(2)}, u32[]{:S(2)}) collective-permute-start(f32[1024,128]{1,0:T(8,128)} %sum_by_row.5), channel_id=1, source_target_pairs={{0,1},{1,0},{2,3},{3,2},{4,5},{5,4},{6,7},{7,6},{8,9},{9,8},{10,11... | collective-permute-start | bytes 1572872 | tf_op jit(solution)/shard_map/ppermute | solution.py:229
  177.8 2.9 %copy-start.13 = (f32[4,4,16,256]{3,2,1,0:T(8,128)}, f32[4,4,16,256]{3,2,1,0:T(8,128)S(1)}, u32[]{:S(2)}) copy-start(f32[4,4,16,256]{3,2,1,0:T(8,128)S(1)} %collective-permute-done.26.refs_8_) | copy-start | bytes 786436
  177.8 2.0 collective-permute-start.29
  178.3 2.4 %copy-start.14 = (f32[4,4,16,256]{3,2,1,0:T(8,128)}, f32[4,4,16,256]{3,2,1,0:T(8,128)S(1)}, u32[]{:S(2)}) copy-start(f32[4,4,16,256]{3,2,1,0:T(8,128)S(1)} %collective-permute-done.30.refs_12_) | copy-start | bytes 786436
  178.3 1.6 collective-permute-start.31
  178.5 2.2 %copy-start.15 = (f32[4,4,16,256]{3,2,1,0:T(8,128)}, f32[4,4,16,256]{3,2,1,0:T(8,128)S(1)}, u32[]{:S(2)}) copy-start(f32[4,4,16,256]{3,2,1,0:T(8,128)S(1)} %collective-permute-done.27.refs_9_) | copy-start | bytes 786436
  178.5 1.9 collective-permute-start.32
  179.0 1.7 collective-permute-start.33
  179.8 0.9 copy-start.16
  179.9 0.8 copy-start.17
  180.3 0.7 copy-start.18
  181.0 0.7 copy-start.19
  186.5 11.4 %copy-start.20 = (f32[2,1024]{1,0:T(2,128)S(1)}, f32[2,1024]{1,0:T(2,128)}, u32[]{:S(2)}) copy-start(f32[2,1024]{1,0:T(2,128)} %param.11) | copy-start | bytes 24580
  186.5 12.1 %copy-start.3 = (f32[2,1024,128]{2,1,0:T(8,128)S(1)}, f32[2,1024,128]{2,1,0:T(8,128)}, u32[]{:S(2)}) copy-start(f32[2,1024,128]{2,1,0:T(8,128)} %param.10) | copy-start | bytes 3145732

commit v3 on v2

--- a/solution.py
+++ b/solution.py
@@ -56,9 +56,10 @@
         swap_ref[...] = jnp.where(hit, 1.0, 0.0).astype(bf16)
 
     for first in range(0, samples, 16):
-        block = grad_ref[first : first + 16].reshape(16 * tables, width)
-        turned = jnp.dot(swap_ref[...], block, preferred_element_type=f32)
-        out_ref[:, first : first + 16, :] = turned.astype(bf16).reshape(tables, 16, width)
+        for top in range(0, tables, 16):
+            block = grad_ref[first : first + 16, top : top + 16].reshape(256, width)
+            turned = jnp.dot(swap_ref[...], block, preferred_element_type=f32)
+            out_ref[top : top + 16, first : first + 16, :] = turned.astype(bf16).reshape(16, 16, width)
     if len(refs) == 4:
         out_ref[:, samples : samples + 8, :] = refs[1][...]
 
@@ -69,10 +70,10 @@
     height = count + 8 * len(codes)
     return pl.pallas_call(
         pack_kernel,
-        grid=(tables // 16,),
-        in_specs=[pl.BlockSpec((count, 16, width), lambda i: (part, i, 0))]
-        + [pl.BlockSpec((16, 8, width), lambda i: (i, 0, 0))] * len(codes),
-        out_specs=pl.BlockSpec((16, height, width), lambda i: (i, 0, 0)),
+        grid=(tables // 64,),
+        in_specs=[pl.BlockSpec((count, 64, width), lambda i: (part, i, 0))]
+        + [pl.BlockSpec((64, 8, width), lambda i: (i, 0, 0))] * len(codes),
+        out_specs=pl.BlockSpec((64, height, width), lambda i: (i, 0, 0)),
         out_shape=jax.ShapeDtypeStruct((tables, height, width), bf16),
         scratch_shapes=[pltpu.VMEM((256, 256), bf16)],
         cost_estimate=pl.CostEstimate(flops=2 * 256 * count * tables * width, bytes_accessed=4 << 20, transcendentals=0),
@@ -81,8 +82,8 @@
 
 
 parts = 2
-group = 8
-stripe = 256
+group = 16
+stripe = 512
 
 
 def sum_kernel(part, base_ref, info_ref, data_ref, *refs):
@@ -119,7 +120,7 @@
 def summed(part, first, data, base, rows, before=()):
     senders, _, width = data.shape
     samples = width // parts
-    step = 16
+    step = 32
     return pl.pallas_call(
         functools.partial(sum_kernel, part),
         grid_spec=pltpu.PrefetchScalarGridSpec(
@@ -154,19 +155,15 @@
 
 def place_kernel(at_ref, *refs):
     out_ref = refs[-1]
-    here_y, here_x, here_z, here_c = (at_ref[k] for k in range(4))
+    here_y, here_x, here_c = (at_ref[k] for k in range(3))
     for number, piece in enumerate(refs[:-1]):
-        core, stream, far = number // 8, number // 4 % 2, number % 4
-        c = here_c if core == 0 else 1 - here_c
-        for near in range(ring):
-            dy, dx = (far, near) if stream == 0 else (near, far)
-            y = (here_y + ring - dy) % ring
-            x = (here_x + ring - dx) % ring
-            left = pl.multiple_of((x % 2) * 512 + stream * 256, 256)
-            for dz in range(ring):
-                z = (here_z + ring - dz) % ring
-                top = pl.multiple_of((x // 2) * 512 + c * 256 + y * 64 + z * 16, 16)
-                out_ref[pl.ds(top, 16), pl.ds(left, 256)] = piece[near, dz]
+        c = here_c if number < ring else 1 - here_c
+        y = (here_y - number) & 3
+        for dx in range(ring):
+            x = (here_x - dx) & 3
+            left = pl.multiple_of((x & 1) * 512, 512)
+            top = pl.multiple_of((x >> 1) * 512 + c * 256 + y * 64, 64)
+            out_ref[pl.ds(top, 64), pl.ds(left, 512)] = piece[dx]
 
 
 def placed(at, pieces):
@@ -186,7 +183,6 @@
 
 def dense_sum(inputs, cotangents):
     y, x, c = (lax.axis_index(a) for a in ("y", "x", "c"))
-    z = lax.axis_index(deep)
 
     def share(of):
         one = jnp.where((of & 2) == 0, inputs[:, :512], inputs[:, 512:])
@@ -201,14 +197,11 @@
     other = lax.ppermute(lax.dynamic_index_in_dim(halves, 1 - c, 0, keepdims=False), "c", swap)
     total = lax.dynamic_index_in_dim(halves, c, 0, keepdims=False) + other
     total = scattered(total.reshape(ring, 64, 512), "y", y)
-    total = scattered(total.reshape(ring, 16, 512), deep, z)
-    total = jnp.stack(gathered(total, deep))
-    left, right = (total[..., :256], total[..., 256:])
-    left = gathered(jnp.stack(gathered(left, "x")), "y")
-    right = gathered(jnp.stack(gathered(right, "y")), "x")
-    mine = left + right
+    ranks = gathered(total, deep)
+    total = (ranks[0] + ranks[2]) + (ranks[1] + ranks[3])
+    mine = gathered(jnp.stack(gathered(total, "x")), "y")
     theirs = [lax.ppermute(p, "c", swap) for p in mine]
-    return placed(jnp.stack([y, x, z, c]).astype(jnp.int32), mine + theirs)
+    return placed(jnp.stack([y, x, c]).astype(jnp.int32), mine + theirs)
 
 
 def per_device(
@@ -221,8 +214,10 @@
     def exchanged(value):
         return lax.all_to_all(value, every, split_axis=0, concat_axis=0, tiled=True)
 
-    first = exchanged(packed(pooled_grad, 0, (codes,)))
-    second = exchanged(packed(pooled_grad, 1))
+    near = packed(pooled_grad, 0, (codes,))
+    late = packed(pooled_grad, 1)
+    first = exchanged(near)
+    second = exchanged(late)
     half = lax.axis_index("zl").astype(jnp.int32)
     early = summed(0, first, first, jnp.zeros((1,), jnp.int32), tables * rows)
     theirs = summed(1, first, second, ((1 - half) * rows)[None], rows, (early,))

time: 202 us -> 195 us (0.965)
  waiting for transfers between devices: 62.9 us -> 82.9 us
  Pallas kernels: 53.6 us -> 39.8 us
  starting transfers between devices: 66.5 us -> 55.3 us
    ppermute x24 -> x15, waiting for transfers between devices: 60.4 us -> 82.8 us  [to_next(): lax.ppermute(value, axis, [(i, (i + step) % ring) for i in range(ring)])]
    ppermute x24 -> x15, starting transfers between devices: 37.9 us -> 19.2 us  [to_next(): lax.ppermute(value, axis, [(i, (i + step) % ring) for i in range(ring)])]
    ppermute x8 -> x4, starting transfers between devices: 7.59 us -> 15.6 us  [dense_sum(): theirs = [lax.ppermute(p, 'c', swap) for p in mine]]
    pallas_call x3, Pallas kernels: 35.3 us -> 27.9 us  [summed(): pl.pallas_call(functools.partial(sum_kernel, part), grid_spec=pltpu.Prefe...]
    pallas_call x2, Pallas kernels: 13.5 us -> 7.38 us  [packed(): pl.pallas_call(pack_kernel, grid=(tables // 64,), in_specs=[pl.BlockSpec(...]
    unnamed x44 -> x22, local copies, waits for them, and re-layouts: 5.44 us -> 4.24 us
  transfers between devices with their start and end apart: 36 -> 23, of which waited for: 14 -> 12; matrix products, arithmetic and copies ran while one was open for 2% -> 2% of each run, Pallas kernels for 23% -> 19%
where the time goes in v3:
time: 195 us; the launch traced here: 194 us
  waiting for transfers between devices  82.9 us (43%)
  starting transfers between devices  55.3 us (28%)
  Pallas kernels  39.8 us (20%)
  other arithmetic  8.18 us (4%)
  local copies, waits for them, and re-layouts  6.97 us (4%)
    ppermute x15, waiting for transfers between devices, to_next(): lax.ppermute(value, axis, [(i, (i + step) % ring) for i in range(ring)])  82.8 us
    pallas_call x3, Pallas kernels, summed(): pl.pallas_call(functools.partial(sum_kernel, part), grid_spec=pltpu.Prefe...  27.9 us
    all_to_all x2, starting transfers between devices, exchanged(): return lax.all_to_all(value, every, split_axis=0, concat_axis=0, tiled=True)  19.8 us
    ppermute x15, starting transfers between devices, to_next(): lax.ppermute(value, axis, [(i, (i + step) % ring) for i in range(ring)])  19.2 us
    ppermute x4, starting transfers between devices, dense_sum(): theirs = [lax.ppermute(p, 'c', swap) for p in mine]  15.6 us
    pallas_call x2, Pallas kernels, packed(): pl.pallas_call(pack_kernel, grid=(tables // 64,), in_specs=[pl.BlockSpec(...  7.38 us
    pallas_call x1, Pallas kernels, placed(): pl.pallas_call(place_kernel, in_specs=[pl.BlockSpec(memory_space=pltpu.SM...  4.45 us
    unnamed x22, local copies, waits for them, and re-layouts  4.24 us
  transfers between devices with their start and end apart: 23, of which 12 were waited for; matrix products, arithmetic and copies ran while one was open for 2% of the time, Pallas kernels for 19%

profile of v3, /device:TPU:1, one launch (start us, length us, event | category | flops | bytes accessed | tf_op | source)
XLA Modules:
  0.0 194.4 jit_solution(9847402162719828793)
XLA Ops:
  0.6 1.1 copy.95
  1.7 0.9 copy.94
  2.7 0.1 fusion.21
  2.8 0.2 fusion.22
  2.9 0.1 copy.100
  3.0 0.1 copy.101
  3.1 0.1 copy.102
  3.1 0.1 copy.103
  3.2 0.1 copy.104
  3.2 0.1 copy.105
  3.3 0.1 copy.106
  3.4 1.5 stack.76.refs_1_
  4.9 3.7 %pack.2 = bf16[128,72,128]{2,1,0:T(8,128)(2,1)} custom-call(bf16[128,128,128]{2,1,0:T(8,128)(2,1)} %refs_0_.3, bf16[128,8,128]{2,1,0:T(8,128)(2,1)} %stack.76.refs_1_), custom_call_target="tpu_custom_call" | custom-call | flops 536870912 | bytes 4194304 | tf_op jit(solution)/shard_map/pack/pallas_call | solution.py:71
  8.6 11.5 %all-to-all-start = ((bf16[128,72,128]{2,1,0:T(8,128)(2,1)}), bf16[128,72,128]{2,1,0:T(8,128)(2,1)S(1)}, u32[]{:S(2)}, u32[]{:S(2)}) async-start(bf16[128,72,128]{2,1,0:T(8,128)(2,1)} %pack.2), calls=%async_computation | async-start | bytes 4718592 | tf_op jit(solution)/shard_map/all_to_all | solution.py:215
  20.3 2.6 %collective-permute-start.3 = (bf16[128,1024]{1,0:T(8,128)(2,1)S(1)}, bf16[128,1024]{1,0:T(8,128)(2,1)}, u32[]{:S(2)}, u32[]{:S(2)}) collective-permute-start(bf16[128,1024]{1,0:T(8,128)(2,1)S(1)} %pad_maximum_fusion.4), channel_id=1, source_target_pairs={{0,24},{8,0},{16,8},{24,16},{1,25},{9,1},{17,9},{25,17},{2,26},{10... | collective-permute-start | bytes 786440 | tf_op jit(solution)/shard_map/ppermute | solution.py:144
  22.9 0.7 collective-permute-start.2
  23.6 0.6 collective-permute-start.1
  24.3 28.2 %collective-permute-done.3 = bf16[128,1024]{1,0:T(8,128)(2,1)} collective-permute-done((bf16[128,1024]{1,0:T(8,128)(2,1)S(1)}, bf16[128,1024]{1,0:T(8,128)(2,1)}, u32[]{:S(2)}, u32[]{:S(2)}) %collective-permute-start.3) | collective-permute-done | bytes 262176 | tf_op jit(solution)/shard_map/ppermute | solution.py:144
  52.4 1.5 collective-permute-done.2
  54.0 5.5 %collective-permute-done.1 = bf16[128,1024]{1,0:T(8,128)(2,1)} collective-permute-done((bf16[128,1024]{1,0:T(8,128)(2,1)S(1)}, bf16[128,1024]{1,0:T(8,128)(2,1)}, u32[]{:S(2)}, u32[]{:S(2)}) %collective-permute-start.1) | collective-permute-done | bytes 262176 | tf_op jit(solution)/shard_map/ppermute | solution.py:144
  59.5 1.2 pad_maximum_fusion
  60.6 0.5 fusion
  61.1 0.8 dynamic-slice_bitcast_fusion
  62.0 0.8 collective-permute-start.4
  62.7 3.7 %pack.3 = bf16[128,64,128]{2,1,0:T(8,128)(2,1)} custom-call(bf16[128,128,128]{2,1,0:T(8,128)(2,1)} %refs_0_.3), custom_call_target="tpu_custom_call" | custom-call | flops 536870912 | bytes 4194304 | tf_op jit(solution)/shard_map/pack/pallas_call | solution.py:71
  66.4 1.4 copy-done
  67.8 8.3 %all-to-all-start.1 = ((bf16[128,64,128]{2,1,0:T(8,128)(2,1)}), bf16[128,64,128]{2,1,0:T(8,128)(2,1)}, u32[]{:S(2)}, u32[]{:S(2)}) async-start(bf16[128,64,128]{2,1,0:T(8,128)(2,1)} %pack.3), calls=%async_computation.1 | async-start | bytes 4194304 | tf_op jit(solution)/shard_map/all_to_all | solution.py:215
  76.1 1.1 bitcast_add_fusion
  77.3 2.7 %collective-permute-start.7 = (f32[64,512]{1,0:T(8,128)S(1)}, f32[64,512]{1,0:T(8,128)S(1)}, u32[]{:S(2)}, u32[]{:S(2)}) collective-permute-start(f32[64,512]{1,0:T(8,128)S(1)} %get-tuple-element.12), channel_id=1, source_target_pairs={{0,96},{32,0},{64,32},{96,64},{1,97},{33,1},{65,33},{97,65},{2,98}... | collective-permute-start | bytes 393224 | tf_op jit(solution)/shard_map/ppermute | solution.py:144
  80.0 0.5 collective-permute-start.6
  80.5 0.6 collective-permute-start.5
  81.1 21.1 %collective-permute-done.7 = f32[64,512]{1,0:T(8,128)S(1)} collective-permute-done((f32[64,512]{1,0:T(8,128)S(1)}, f32[64,512]{1,0:T(8,128)S(1)}, u32[]{:S(2)}, u32[]{:S(2)}) %collective-permute-start.7) | collective-permute-done | bytes 131104 | tf_op jit(solution)/shard_map/ppermute | solution.py:144
  102.2 1.7 collective-permute-done.6
  103.9 2.6 %collective-permute-done.5 = f32[64,512]{1,0:T(8,128)S(1)} collective-permute-done((f32[64,512]{1,0:T(8,128)S(1)}, f32[64,512]{1,0:T(8,128)S(1)}, u32[]{:S(2)}, u32[]{:S(2)}) %collective-permute-start.5) | collective-permute-done | bytes 131104 | tf_op jit(solution)/shard_map/ppermute | solution.py:144
  106.6 1.5 collective-permute-start.9
  108.1 1.9 collective-permute-start.10
  110.0 1.2 collective-permute-start.8
  111.2 1.7 collective-permute-done.9
  113.0 4.0 %collective-permute-done.8 = f32[64,512]{1,0:T(8,128)S(1)} collective-permute-done((f32[64,512]{1,0:T(8,128)S(1)}, f32[64,512]{1,0:T(8,128)S(1)}, u32[]{:S(2)}, u32[]{:S(2)}) %collective-permute-start.8) | collective-permute-done | bytes 131104 | tf_op jit(solution)/shard_map/ppermute | solution.py:144
  117.0 2.4 %collective-permute-start.13 = (f32[64,512]{1,0:T(8,128)S(1)}, f32[64,512]{1,0:T(8,128)S(1)}, u32[]{:S(2)}, u32[]{:S(2)}) collective-permute-start(f32[64,512]{1,0:T(8,128)S(1)} %add_add_fusion), channel_id=1, source_target_pairs={{0,24},{8,0},{16,8},{24,16},{1,25},{9,1},{17,9},{25,17},{2,26},{10... | collective-permute-start | bytes 393224 | tf_op jit(solution)/shard_map/ppermute | solution.py:144
  119.4 0.5 collective-permute-start.12
  120.0 0.7 collective-permute-start.11
  120.6 1.1 collective-permute-done.13
  121.7 3.2 %collective-permute-done.12 = f32[64,512]{1,0:T(8,128)S(1)} collective-permute-done((f32[64,512]{1,0:T(8,128)S(1)}, f32[64,512]{1,0:T(8,128)S(1)}, u32[]{:S(2)}, u32[]{:S(2)}) %collective-permute-start.12) | collective-permute-done | bytes 131104 | tf_op jit(solution)/shard_map/ppermute | solution.py:144
  124.9 3.5 %collective-permute-done.11 = f32[64,512]{1,0:T(8,128)S(1)} collective-permute-done((f32[64,512]{1,0:T(8,128)S(1)}, f32[64,512]{1,0:T(8,128)S(1)}, u32[]{:S(2)}, u32[]{:S(2)}) %collective-permute-start.11) | collective-permute-done | bytes 131104 | tf_op jit(solution)/shard_map/ppermute | solution.py:144
  128.4 0.7 collective-permute-start.14
  129.1 1.7 collective-permute-start.15
  130.8 0.8 collective-permute-start.16
  131.6 1.9 collective-permute-start.17
  133.5 8.7 %collective-permute-done.14.refs_1_ = f32[4,64,512]{2,1,0:T(8,128)S(1)} collective-permute-done((f32[4,64,512]{2,1,0:T(8,128)S(1)}, f32[4,64,512]{2,1,0:T(8,128)S(1)}, u32[]{:S(2)}, u32[]{:S(2)}) %collective-permute-start.14) | collective-permute-done | bytes 524320 | tf_op jit(solution)/shard_map/ppermute | solution.py:144
  142.2 13.0 %collective-permute-start.18 = (f32[4,64,512]{2,1,0:T(8,128)S(1)}, f32[4,64,512]{2,1,0:T(8,128)}, u32[]{:S(2)}, u32[]{:S(2)}) collective-permute-start(f32[4,64,512]{2,1,0:T(8,128)S(1)} %collective-permute-done.14.refs_1_), channel_id=1, source_target_pairs={{0,2},{2,0},{1,3},{3,1},{4,6},{6,4},{5,7},{7,5},{8,10},{10,8},{9,1... | collective-permute-start | bytes 1572872 | tf_op jit(solution)/shard_map/ppermute | solution.py:203
  155.3 0.1 collective-permute-start.19
  155.4 0.5 collective-permute-start.20
  155.9 12.4 %sum_by_row.3.refs_0_ = f32[2048,128]{1,0:T(8,128)} custom-call(s32[1]{0:T(128)} %constant.60.clone.1.base_ref, bf16[128,72,128]{2,1,0:T(8,128)(2,1)} %copy-done, bf16[128,72,128]{2,1,0:T(8,128)(2,1)} %copy-done), custom_call_target="tpu_custom_call" | custom-call | flops 4294967296 | bytes 3145728 | tf_op jit(solution)/shard_map/sum_by_row/pallas_call | solution.py:124
  168.3 7.7 %sum_by_row.5 = f32[1024,128]{1,0:T(8,128)} custom-call(s32[1]{0:T(128)} %bitcast.34.base_ref, bf16[128,72,128]{2,1,0:T(8,128)(2,1)} %copy-done, bf16[128,64,128]{2,1,0:T(8,128)(2,1)} %all-to-all-done.1.data_ref, f32[2048,128]{1,0:T(8,128)} %sum_by_row.3.refs_0_), custom_call_target="tpu_custom_call" | custom-call | flops 2147483648 | bytes 3145728 | tf_op jit(solution)/shard_map/sum_by_row/pallas_call | solution.py:124
  176.0 0.6 pad_add_fusion.at_ref
  176.7 0.0 collective-permute-done.19.refs_6_
  176.7 0.8 copy-done.6
  177.5 4.4 %place.1 = f32[1024,1024]{1,0:T(8,128)} custom-call(s32[3]{0:T(128)} %pad_add_fusion.at_ref, f32[4,64,512]{2,1,0:T(8,128)} %copy-done.1, f32[4,64,512]{2,1,0:T(8,128)} %copy-done.3, f32[4,64,512]{2,1,0:T(8,128)} %copy-done.4, f32[4,64,512]{2,1,0:T(8,128)} %copy-done.5, f32[4,64,512]{2,1,0:T(8,128)} %copy-done.6, ...), custom_call_target="tpu_custom_call" | custom-call | flops 3145728 | bytes 8388608 | tf_op jit(solution)/shard_map/place/pallas_call | solution.py:170
  181.9 7.8 %sum_by_row.4 = f32[1024,128]{1,0:T(8,128)} custom-call(s32[1]{0:T(128)} %bitcast.base_ref, bf16[128,72,128]{2,1,0:T(8,128)(2,1)} %copy-done, bf16[128,64,128]{2,1,0:T(8,128)(2,1)} %all-to-all-done.1.data_ref, f32[2048,128]{1,0:T(8,128)} %sum_by_row.3.refs_0_), custom_call_target="tpu_custom_call" | custom-call | flops 2147483648 | bytes 3145728 | tf_op jit(solution)/shard_map/sum_by_row/pallas_call | solution.py:124
  189.7 0.0 collective-permute-done
  189.7 1.6 multiply_reduce_fusion
  191.3 0.6 fusion.23
  191.9 2.5 %divide_subtract_fusion = f32[2,1024,128]{2,1,0:T(8,128)} fusion(f32[2,1024,128]{2,1,0:T(8,128)S(1)} %copy-done.2, f32[1,1024,128]{2,1,0:T(8,128)} %bitcast.195, f32[1,1024,128]{2,1,0:T(8,128)S(1)} %bitcast.193, f32[2,1024]{1,0:T(2,128)S(1)} %get-tuple-element.3, pred[]{:T(512)S(6)} %eq.63), kind=kLoop, calls=%fused_computation.2 | loop fusion | flops 1572864 | bytes 3153921 | tf_op jit(solution)/shard_map/sub | solution.py:228
  (40 shorter events, 0.5 us)
Async XLA Ops:
  8.6 11.5 %copy-start.7 = (bf16[128,1024]{1,0:T(8,128)(2,1)S(1)}, bf16[128,1024]{1,0:T(8,128)(2,1)}, u32[]{:S(2)}) copy-start(bf16[128,1024]{1,0:T(8,128)(2,1)} %param.13) | copy-start | bytes 786436
  8.6 11.6 %copy-start.8 = (bf16[128,1024]{1,0:T(8,128)(2,1)S(1)}, bf16[128,1024]{1,0:T(8,128)(2,1)}, u32[]{:S(2)}) copy-start(bf16[128,1024]{1,0:T(8,128)(2,1)} %param.12) | copy-start | bytes 786436
  8.6 57.8 %all-to-all-start = ((bf16[128,72,128]{2,1,0:T(8,128)(2,1)}), bf16[128,72,128]{2,1,0:T(8,128)(2,1)S(1)}, u32[]{:S(2)}, u32[]{:S(2)}) async-start(bf16[128,72,128]{2,1,0:T(8,128)(2,1)} %pack.2), calls=%async_computation | async-start | bytes 4718592 | tf_op jit(solution)/shard_map/all_to_all | solution.py:215
  20.3 32.2 %collective-permute-start.3 = (bf16[128,1024]{1,0:T(8,128)(2,1)S(1)}, bf16[128,1024]{1,0:T(8,128)(2,1)}, u32[]{:S(2)}, u32[]{:S(2)}) collective-permute-start(bf16[128,1024]{1,0:T(8,128)(2,1)S(1)} %pad_maximum_fusion.4), channel_id=1, source_target_pairs={{0,24},{8,0},{16,8},{24,16},{1,25},{9,1},{17,9},{25,17},{2,26},{10... | collective-permute-start | bytes 786440 | tf_op jit(solution)/shard_map/ppermute | solution.py:144
  22.9 31.0 %collective-permute-start.2 = (bf16[128,1024]{1,0:T(8,128)(2,1)S(1)}, bf16[128,1024]{1,0:T(8,128)(2,1)}, u32[]{:S(2)}, u32[]{:S(2)}) collective-permute-start(bf16[128,1024]{1,0:T(8,128)(2,1)S(1)} %pad_maximum_fusion.3), channel_id=1, source_target_pairs={{0,16},{8,24},{16,0},{24,8},{1,17},{9,25},{17,1},{25,9},{2,18},{10... | collective-permute-start | bytes 786440 | tf_op jit(solution)/shard_map/ppermute | solution.py:144
  23.6 35.9 %collective-permute-start.1 = (bf16[128,1024]{1,0:T(8,128)(2,1)S(1)}, bf16[128,1024]{1,0:T(8,128)(2,1)}, u32[]{:S(2)}, u32[]{:S(2)}) collective-permute-start(bf16[128,1024]{1,0:T(8,128)(2,1)S(1)} %pad_maximum_fusion.2), channel_id=1, source_target_pairs={{0,8},{8,16},{16,24},{24,0},{1,9},{9,17},{17,25},{25,1},{2,10},{10... | collective-permute-start | bytes 786440 | tf_op jit(solution)/shard_map/ppermute | solution.py:144
  62.0 14.2 %collective-permute-start.4 = (f32[256,512]{1,0:T(8,128)}, f32[256,512]{1,0:T(8,128)}, u32[]{:S(2)}, u32[]{:S(2)}) collective-permute-start(f32[256,512]{1,0:T(8,128)} %dynamic-slice_bitcast_fusion), channel_id=1, source_target_pairs={{0,2},{2,0},{1,3},{3,1},{4,6},{6,4},{5,7},{7,5},{8,10},{10,8},{9,1... | collective-permute-start | bytes 1572872 | tf_op jit(solution)/shard_map/ppermute | solution.py:197
  66.4 1.4 copy-start
  67.8 100.5 %all-to-all-start.1 = ((bf16[128,64,128]{2,1,0:T(8,128)(2,1)}), bf16[128,64,128]{2,1,0:T(8,128)(2,1)}, u32[]{:S(2)}, u32[]{:S(2)}) async-start(bf16[128,64,128]{2,1,0:T(8,128)(2,1)} %pack.3), calls=%async_computation.1 | async-start | bytes 4194304 | tf_op jit(solution)/shard_map/all_to_all | solution.py:215
  77.3 24.9 %collective-permute-start.7 = (f32[64,512]{1,0:T(8,128)S(1)}, f32[64,512]{1,0:T(8,128)S(1)}, u32[]{:S(2)}, u32[]{:S(2)}) collective-permute-start(f32[64,512]{1,0:T(8,128)S(1)} %get-tuple-element.12), channel_id=1, source_target_pairs={{0,96},{32,0},{64,32},{96,64},{1,97},{33,1},{65,33},{97,65},{2,98}... | collective-permute-start | bytes 393224 | tf_op jit(solution)/shard_map/ppermute | solution.py:144
  80.0 23.9 %collective-permute-start.6 = (f32[64,512]{1,0:T(8,128)S(1)}, f32[64,512]{1,0:T(8,128)S(1)}, u32[]{:S(2)}, u32[]{:S(2)}) collective-permute-start(f32[64,512]{1,0:T(8,128)S(1)} %get-tuple-element.13), channel_id=1, source_target_pairs={{0,64},{32,96},{64,0},{96,32},{1,65},{33,97},{65,1},{97,33},{2,66}... | collective-permute-start | bytes 393224 | tf_op jit(solution)/shard_map/ppermute | solution.py:144
  80.5 26.0 %collective-permute-start.5 = (f32[64,512]{1,0:T(8,128)S(1)}, f32[64,512]{1,0:T(8,128)S(1)}, u32[]{:S(2)}, u32[]{:S(2)}) collective-permute-start(f32[64,512]{1,0:T(8,128)S(1)} %get-tuple-element.11), channel_id=1, source_target_pairs={{0,32},{32,64},{64,96},{96,0},{1,33},{33,65},{65,97},{97,1},{2,34}... | collective-permute-start | bytes 393224 | tf_op jit(solution)/shard_map/ppermute | solution.py:144
  106.6 6.4 %collective-permute-start.9 = (f32[64,512]{1,0:T(8,128)S(1)}, f32[64,512]{1,0:T(8,128)S(1)}, u32[]{:S(2)}, u32[]{:S(2)}) collective-permute-start(f32[64,512]{1,0:T(8,128)S(1)} %fusion.4), channel_id=1, source_target_pairs={{0,1},{1,4},{4,5},{5,0},{2,3},{3,6},{6,7},{7,2},{8,9},{9,12},{12,1... | collective-permute-start | bytes 393224 | tf_op jit(solution)/shard_map/ppermute | solution.py:144
  108.1 4.8 %collective-permute-start.10 = (f32[64,512]{1,0:T(8,128)S(1)}, f32[64,512]{1,0:T(8,128)S(1)}, u32[]{:S(2)}, u32[]{:S(2)}) collective-permute-start(f32[64,512]{1,0:T(8,128)S(1)} %fusion.4), channel_id=1, source_target_pairs={{0,5},{1,0},{4,1},{5,4},{2,7},{3,2},{6,3},{7,6},{8,13},{9,8},{12,9... | collective-permute-start | bytes 393224 | tf_op jit(solution)/shard_map/ppermute | solution.py:144
  110.0 7.0 %collective-permute-start.8 = (f32[64,512]{1,0:T(8,128)S(1)}, f32[64,512]{1,0:T(8,128)S(1)}, u32[]{:S(2)}, u32[]{:S(2)}) collective-permute-start(f32[64,512]{1,0:T(8,128)S(1)} %fusion.4), channel_id=1, source_target_pairs={{0,4},{1,5},{4,0},{5,1},{2,6},{3,7},{6,2},{7,3},{8,12},{9,13},{12,... | collective-permute-start | bytes 393224 | tf_op jit(solution)/shard_map/ppermute | solution.py:144
  117.0 4.7 %collective-permute-start.13 = (f32[64,512]{1,0:T(8,128)S(1)}, f32[64,512]{1,0:T(8,128)S(1)}, u32[]{:S(2)}, u32[]{:S(2)}) collective-permute-start(f32[64,512]{1,0:T(8,128)S(1)} %add_add_fusion), channel_id=1, source_target_pairs={{0,24},{8,0},{16,8},{24,16},{1,25},{9,1},{17,9},{25,17},{2,26},{10... | collective-permute-start | bytes 393224 | tf_op jit(solution)/shard_map/ppermute | solution.py:144
  119.4 5.4 %collective-permute-start.12 = (f32[64,512]{1,0:T(8,128)S(1)}, f32[64,512]{1,0:T(8,128)S(1)}, u32[]{:S(2)}, u32[]{:S(2)}) collective-permute-start(f32[64,512]{1,0:T(8,128)S(1)} %add_add_fusion), channel_id=1, source_target_pairs={{0,16},{8,24},{16,0},{24,8},{1,17},{9,25},{17,1},{25,9},{2,18},{10... | collective-permute-start | bytes 393224 | tf_op jit(solution)/shard_map/ppermute | solution.py:144
  120.0 8.4 %collective-permute-start.11 = (f32[64,512]{1,0:T(8,128)S(1)}, f32[64,512]{1,0:T(8,128)S(1)}, u32[]{:S(2)}, u32[]{:S(2)}) collective-permute-start(f32[64,512]{1,0:T(8,128)S(1)} %add_add_fusion), channel_id=1, source_target_pairs={{0,8},{8,16},{16,24},{24,0},{1,9},{9,17},{17,25},{25,1},{2,10},{10... | collective-permute-start | bytes 393224 | tf_op jit(solution)/shard_map/ppermute | solution.py:144
  128.4 39.9 %copy-start.1 = (f32[4,64,512]{2,1,0:T(8,128)}, f32[4,64,512]{2,1,0:T(8,128)S(1)}, u32[]{:S(2)}) copy-start(f32[4,64,512]{2,1,0:T(8,128)S(1)} %pad_maximum_fusion.1.refs_0_) | copy-start | bytes 1572868
  128.4 13.8 %collective-permute-start.14 = (f32[4,64,512]{2,1,0:T(8,128)S(1)}, f32[4,64,512]{2,1,0:T(8,128)S(1)}, u32[]{:S(2)}, u32[]{:S(2)}) collective-permute-start(f32[4,64,512]{2,1,0:T(8,128)S(1)} %pad_maximum_fusion.1.refs_0_), channel_id=1, source_target_pairs={{0,32},{32,64},{64,96},{96,0},{1,33},{33,65},{65,97},{97,1},{2,34}... | collective-permute-start | bytes 1572872 | tf_op jit(solution)/shard_map/ppermute | solution.py:144
  129.1 26.1 %collective-permute-start.15 = (f32[4,64,512]{2,1,0:T(8,128)S(1)}, f32[4,64,512]{2,1,0:T(8,128)S(1)}, u32[]{:S(2)}, u32[]{:S(2)}) collective-permute-start(f32[4,64,512]{2,1,0:T(8,128)S(1)} %pad_maximum_fusion.1.refs_0_), channel_id=1, source_target_pairs={{0,64},{32,96},{64,0},{96,32},{1,65},{33,97},{65,1},{97,33},{2,66}... | collective-permute-start | bytes 1572872 | tf_op jit(solution)/shard_map/ppermute | solution.py:144
  130.8 24.6 %collective-permute-start.16 = (f32[4,64,512]{2,1,0:T(8,128)S(1)}, f32[4,64,512]{2,1,0:T(8,128)S(1)}, u32[]{:S(2)}, u32[]{:S(2)}) collective-permute-start(f32[4,64,512]{2,1,0:T(8,128)S(1)} %pad_maximum_fusion.1.refs_0_), channel_id=1, source_target_pairs={{0,96},{32,0},{64,32},{96,64},{1,97},{33,1},{65,33},{97,65},{2,98}... | collective-permute-start | bytes 1572872 | tf_op jit(solution)/shard_map/ppermute | solution.py:144
  131.6 45.1 %collective-permute-start.17 = (f32[4,64,512]{2,1,0:T(8,128)S(1)}, f32[4,64,512]{2,1,0:T(8,128)S(1)}, u32[]{:S(2)}, u32[]{:S(2)}) collective-permute-start(f32[4,64,512]{2,1,0:T(8,128)S(1)} %pad_maximum_fusion.1.refs_0_), channel_id=1, source_target_pairs={{0,2},{2,0},{1,3},{3,1},{4,6},{6,4},{5,7},{7,5},{8,10},{10,8},{9,1... | collective-permute-start | bytes 1572872 | tf_op jit(solution)/shard_map/ppermute | solution.py:203
  142.2 26.1 %copy-start.3 = (f32[4,64,512]{2,1,0:T(8,128)}, f32[4,64,512]{2,1,0:T(8,128)S(1)}, u32[]{:S(2)}) copy-start(f32[4,64,512]{2,1,0:T(8,128)S(1)} %collective-permute-done.14.refs_1_) | copy-start | bytes 1572868
  142.2 34.5 %collective-permute-start.18 = (f32[4,64,512]{2,1,0:T(8,128)S(1)}, f32[4,64,512]{2,1,0:T(8,128)}, u32[]{:S(2)}, u32[]{:S(2)}) collective-permute-start(f32[4,64,512]{2,1,0:T(8,128)S(1)} %collective-permute-done.14.refs_1_), channel_id=1, source_target_pairs={{0,2},{2,0},{1,3},{3,1},{4,6},{6,4},{5,7},{7,5},{8,10},{10,8},{9,1... | collective-permute-start | bytes 1572872 | tf_op jit(solution)/shard_map/ppermute | solution.py:203
  155.2 13.0 %copy-start.4 = (f32[4,64,512]{2,1,0:T(8,128)}, f32[4,64,512]{2,1,0:T(8,128)S(1)}, u32[]{:S(2)}) copy-start(f32[4,64,512]{2,1,0:T(8,128)S(1)} %collective-permute-done.15.refs_2_) | copy-start | bytes 1572868
  155.3 21.4 %collective-permute-start.19 = (f32[4,64,512]{2,1,0:T(8,128)S(1)}, f32[4,64,512]{2,1,0:T(8,128)}, u32[]{:S(2)}, u32[]{:S(2)}) collective-permute-start(f32[4,64,512]{2,1,0:T(8,128)S(1)} %collective-permute-done.15.refs_2_), channel_id=1, source_target_pairs={{0,2},{2,0},{1,3},{3,1},{4,6},{6,4},{5,7},{7,5},{8,10},{10,8},{9,1... | collective-permute-start | bytes 1572872 | tf_op jit(solution)/shard_map/ppermute | solution.py:203
  155.3 13.0 %copy-start.5 = (f32[4,64,512]{2,1,0:T(8,128)}, f32[4,64,512]{2,1,0:T(8,128)S(1)}, u32[]{:S(2)}) copy-start(f32[4,64,512]{2,1,0:T(8,128)S(1)} %collective-permute-done.16.refs_3_) | copy-start | bytes 1572868
  155.4 21.3 %collective-permute-start.20 = (f32[4,64,512]{2,1,0:T(8,128)S(1)}, f32[4,64,512]{2,1,0:T(8,128)}, u32[]{:S(2)}, u32[]{:S(2)}) collective-permute-start(f32[4,64,512]{2,1,0:T(8,128)S(1)} %collective-permute-done.16.refs_3_), channel_id=1, source_target_pairs={{0,2},{2,0},{1,3},{3,1},{4,6},{6,4},{5,7},{7,5},{8,10},{10,8},{9,1... | collective-permute-start | bytes 1572872 | tf_op jit(solution)/shard_map/ppermute | solution.py:203
  176.0 13.6 %collective-permute-start = (f32[1024,128]{1,0:T(8,128)}, f32[1024,128]{1,0:T(8,128)S(1)}, u32[]{:S(2)}, u32[]{:S(2)}) collective-permute-start(f32[1024,128]{1,0:T(8,128)} %sum_by_row.5), channel_id=1, source_target_pairs={{0,1},{1,0},{2,3},{3,2},{4,5},{5,4},{6,7},{7,6},{8,9},{9,8},{10,11... | collective-permute-start | bytes 1572872 | tf_op jit(solution)/shard_map/ppermute | solution.py:224
  176.7 0.8 copy-start.6
  181.9 9.4 %copy-start.9 = (f32[2,1024]{1,0:T(2,128)S(1)}, f32[2,1024]{1,0:T(2,128)}, u32[]{:S(2)}) copy-start(f32[2,1024]{1,0:T(2,128)} %param.11) | copy-start | bytes 24580
  181.9 10.0 %copy-start.2 = (f32[2,1024,128]{2,1,0:T(8,128)S(1)}, f32[2,1024,128]{2,1,0:T(8,128)}, u32[]{:S(2)}) copy-start(f32[2,1024,128]{2,1,0:T(8,128)} %param.10) | copy-start | bytes 3145732

commit v4 on v3

--- a/solution.py
+++ b/solution.py
@@ -65,13 +65,14 @@
 
 
 def packed(grads, part, codes=()):
-    samples, tables, width = grads.shape
-    count = samples // parts
+    start, stop = cut[part : part + 2]
+    _, tables, width = grads.shape
+    count = stop - start
     height = count + 8 * len(codes)
     return pl.pallas_call(
         pack_kernel,
         grid=(tables // 64,),
-        in_specs=[pl.BlockSpec((count, 64, width), lambda i: (part, i, 0))]
+        in_specs=[pl.BlockSpec((pl.Element(count), pl.Element(64), pl.Element(width)), lambda i: (start, i * 64, 0))]
         + [pl.BlockSpec((64, 8, width), lambda i: (i, 0, 0))] * len(codes),
         out_specs=pl.BlockSpec((64, height, width), lambda i: (i, 0, 0)),
         out_shape=jax.ShapeDtypeStruct((tables, height, width), bf16),
@@ -81,14 +82,14 @@
     )(grads, *codes)
 
 
-parts = 2
+cut = (0, 80, 128)
 group = 16
 stripe = 512
 
 
 def sum_kernel(part, base_ref, info_ref, data_ref, *refs):
     out_ref, mine_ref = refs[-2], refs[-1]
-    senders, samples, _ = data_ref.shape
+    senders, samples, width = data_ref.shape
     rows = out_ref.shape[0]
 
     @pl.when(pl.program_id(0) == 0)
@@ -97,17 +98,15 @@
         mine_ref[...] = sized(base_ref[0] + lax.broadcasted_iota(jnp.int32, mine_ref.shape, 0)).astype(f32)
 
     zero = jnp.zeros((), bf16)
-    here = slice(part * samples, (part + 1) * samples)
+    here = slice(*cut[part : part + 2])
     for first in range(0, senders, group):
-        pairs = [
-            jnp.concatenate([info_ref[k][:, here], info_ref[k + 1][:, here]], axis=1)
-            for k in range(first, first + group, 2)
-        ]
+        infos = jnp.concatenate([info_ref[k][:, here] for k in range(first, first + group)], axis=1)
+        infos = [infos[:, k : k + width] for k in range(0, group * samples, width)]
         values = jnp.concatenate([data_ref[k, 0:samples, :] for k in range(first, first + group)], axis=0)
         for top in range(0, rows, stripe):
             mine = mine_ref[top : top + stripe, :].astype(bf16)
             hots = []
-            for info in pairs:
+            for info in infos:
                 hot = jnp.where(mine == info[3:4], info[7:8], zero)
                 for j in (2, 1, 0):
                     hot = jnp.where(mine == info[j : j + 1], info[4 + j : 5 + j], hot)
@@ -119,7 +118,7 @@
 
 def summed(part, first, data, base, rows, before=()):
     senders, _, width = data.shape
-    samples = width // parts
+    samples = cut[part + 1] - cut[part]
     step = 32
     return pl.pallas_call(
         functools.partial(sum_kernel, part),
@@ -127,7 +126,7 @@
             num_scalar_prefetch=1,
             grid=(senders // step,),
             in_specs=[
-                pl.BlockSpec((step, 8, width), lambda i, b: (i, samples // 8, 0)),
+                pl.BlockSpec((step, 8, width), lambda i, b: (i, cut[1] // 8, 0)),
                 pl.BlockSpec((step, samples, width), lambda i, b: (i, 0, 0)),
             ]
             + [pl.BlockSpec((rows, width), lambda i, b: (b[0] // rows, 0))] * len(before),
@@ -153,30 +152,90 @@
     return own + arrived[0] + arrived[1] + arrived[2]
 
 
+def step_of(power, factor):
+    return jnp.exp2(power.astype(f32)) * (factor.astype(f32) * (1 / 32767 / 8192))
+
+
+def code_kernel(*refs):
+    out_ref = refs[-1]
+    total = (refs[0][...] + refs[2][...]) + (refs[1][...] + refs[3][...])
+    top = jnp.max(jnp.abs(total), axis=1, keepdims=True)
+    power = jnp.clip(jnp.floor(jnp.log2(jnp.maximum(top, 1e-30))), -90.0, 90.0).astype(jnp.int32)
+    factor = jnp.ceil(top * jnp.exp2(-power.astype(f32)) * 8192).astype(jnp.int32)
+    factor = jnp.clip(factor, 0, 32767)
+    step = step_of(power, factor)
+    value = jnp.round(total * jnp.where(step > 0, 1 / step, 0.0))
+    value = jnp.clip(value, -32767, 32767).astype(jnp.int32)
+    lane = lax.broadcasted_iota(jnp.int32, (total.shape[0], 128), 1)
+    out_ref[:, :512] = value.astype(jnp.int16)
+    out_ref[:, 512:] = jnp.where(lane == 0, power, factor).astype(jnp.int16)
+
+
+def coded_sum(ranks):
+    return pl.pallas_call(
+        code_kernel,
+        out_shape=jax.ShapeDtypeStruct((64, 640), jnp.int16),
+        cost_estimate=pl.CostEstimate(flops=1 << 20, bytes_accessed=1 << 20, transcendentals=0),
+        name="code_sum",
+    )(*ranks)
+
+
 def place_kernel(at_ref, *refs):
-    out_ref = refs[-1]
+    pieces, out_ref, held, sems = refs[: 2 * ring], refs[-3], refs[-2], refs[-1]
     here_y, here_x, here_c = (at_ref[k] for k in range(3))
-    for number, piece in enumerate(refs[:-1]):
+    copies = []
+    for number, piece in enumerate(pieces):
         c = here_c if number < ring else 1 - here_c
         y = (here_y - number) & 3
         for dx in range(ring):
             x = (here_x - dx) & 3
             left = pl.multiple_of((x & 1) * 512, 512)
             top = pl.multiple_of((x >> 1) * 512 + c * 256 + y * 64, 64)
-            out_ref[pl.ds(top, 64), pl.ds(left, 512)] = piece[dx]
+            block = piece[dx].astype(jnp.int32)
+            step = step_of(block[:, 512:513], block[:, 513:514])
+            held[number, dx] = block[:, :512].astype(f32) * step
+            copies.append(
+                pltpu.make_async_copy(
+                    held.at[number, dx], out_ref.at[pl.ds(top, 64), pl.ds(left, 512)], sems.at[number, dx]
+                )
+            )
+            copies[-1].start()
+    for copy in copies:
+        copy.wait()
 
 
 def placed(at, pieces):
     return pl.pallas_call(
         place_kernel,
         in_specs=[pl.BlockSpec(memory_space=pltpu.SMEM)] + [pl.BlockSpec(memory_space=pltpu.VMEM)] * len(pieces),
-        out_specs=pl.BlockSpec(memory_space=pltpu.VMEM),
+        out_specs=pl.BlockSpec(memory_space=pl.ANY),
         out_shape=jax.ShapeDtypeStruct((1024, 1024), f32),
+        scratch_shapes=[
+            pltpu.VMEM((2 * ring, ring, 64, 512), f32),
+            pltpu.SemaphoreType.DMA((2 * ring, ring)),
+        ],
         cost_estimate=pl.CostEstimate(flops=3 << 20, bytes_accessed=8 << 20, transcendentals=0),
         name="place",
     )(at, *pieces)
 
 
+def share_kernel(at_ref, left_ref, right_ref, *out_refs):
+    for step, out_ref in enumerate(out_refs):
+        of = (at_ref[0] + step) & 3
+        out_ref[:, :512] = left_ref[:, pl.ds(pl.multiple_of((of >> 1) * 512, 512), 512)]
+        out_ref[:, 512:] = right_ref[:, pl.ds(pl.multiple_of((of & 1) * 512, 512), 512)]
+
+
+def shares(x, inputs, cotangents):
+    return pl.pallas_call(
+        share_kernel,
+        in_specs=[pl.BlockSpec(memory_space=pltpu.SMEM)] + [pl.BlockSpec(memory_space=pltpu.VMEM)] * 2,
+        out_shape=[jax.ShapeDtypeStruct(inputs.shape, bf16)] * ring,
+        cost_estimate=pl.CostEstimate(flops=1 << 19, bytes_accessed=2 << 20, transcendentals=0),
+        name="share",
+    )(x[None], inputs, cotangents)
+
+
 def gathered(value, axis):
     return [value] + [to_next(value, axis, step) for step in range(1, ring)]
 
@@ -184,12 +243,8 @@
 def dense_sum(inputs, cotangents):
     y, x, c = (lax.axis_index(a) for a in ("y", "x", "c"))
 
-    def share(of):
-        one = jnp.where((of & 2) == 0, inputs[:, :512], inputs[:, 512:])
-        two = jnp.where((of & 1) == 0, cotangents[:, :512], cotangents[:, 512:])
-        return jnp.concatenate([one, two], axis=1)
-
-    parts = [share(x)] + [to_next(share((x + step) & 3), "x", step) for step in range(1, ring)]
+    parts = shares(x.astype(jnp.int32), inputs, cotangents)
+    parts = [parts[0]] + [to_next(parts[step], "x", step) for step in range(1, ring)]
     both = jnp.concatenate(parts, axis=0)
     local = lax.dot_general(both[:, :512], both[:, 512:], (((0,), (0,)), ((), ())), preferred_element_type=f32)
     halves = local.reshape(2, 256, 512)
@@ -198,10 +253,49 @@
     total = lax.dynamic_index_in_dim(halves, c, 0, keepdims=False) + other
     total = scattered(total.reshape(ring, 64, 512), "y", y)
     ranks = gathered(total, deep)
-    total = (ranks[0] + ranks[2]) + (ranks[1] + ranks[3])
+    total = coded_sum(ranks)
     mine = gathered(jnp.stack(gathered(total, "x")), "y")
     theirs = [lax.ppermute(p, "c", swap) for p in mine]
     return placed(jnp.stack([y, x, c]).astype(jnp.int32), mine + theirs)
+
+
+def update_kernel(at_ref, table_ref, accum_ref, prior_ref, grad_ref, *refs):
+    out_ref, new_ref = refs[-2:]
+    at = at_ref[0]
+    accum = jnp.where(at == 0, accum_ref[0:1, :], accum_ref[1:2, :])
+    for top in range(0, grad_ref.shape[0], 128):
+        span = slice(top, top + 128)
+        grad = grad_ref[span, :]
+        before = jnp.broadcast_to(accum[:, span], (128, 128)).T
+        after = before + jnp.mean(grad * grad, axis=1, keepdims=True)
+        out_ref[0, span, :] = table_ref[0, span, :] - learn_rate * grad / jnp.sqrt(after)
+        row = after.T[0:1, :]
+        new_ref[0:1, span] = jnp.where(at == 0, row, prior_ref[0:1, span])
+        new_ref[1:2, span] = jnp.where(at == 0, prior_ref[1:2, span], row)
+
+
+def updated(at, table_rows, row_accum, prior, grad, before=()):
+    tables, rows, width = table_rows.shape
+    small = pl.BlockSpec((tables, rows), lambda i, b: (0, 0))
+    return pl.pallas_call(
+        update_kernel,
+        grid_spec=pltpu.PrefetchScalarGridSpec(
+            num_scalar_prefetch=1,
+            grid=(1,),
+            in_specs=[
+                pl.BlockSpec((1, rows, width), lambda i, b: (b[0], 0, 0)),
+                small,
+                small,
+                pl.BlockSpec((rows, width), lambda i, b: (0, 0)),
+            ]
+            + [pl.BlockSpec(memory_space=pl.ANY)] * len(before),
+            out_specs=[pl.BlockSpec((1, rows, width), lambda i, b: (b[0], 0, 0)), small],
+        ),
+        out_shape=[jax.ShapeDtypeStruct(table_rows.shape, f32), jax.ShapeDtypeStruct(row_accum.shape, f32)],
+        input_output_aliases={5: 0} if before else {},
+        cost_estimate=pl.CostEstimate(flops=1 << 20, bytes_accessed=2 << 20, transcendentals=0),
+        name="update",
+    )(at[None], table_rows, row_accum, prior, grad, *before)
 
 
 def per_device(
@@ -223,9 +317,8 @@
     theirs = summed(1, first, second, ((1 - half) * rows)[None], rows, (early,))
     arrived = lax.ppermute(theirs, "zl", [(0, 1), (1, 0)])
     own = summed(1, first, second, (half * rows)[None], rows, (early,))
-    row_grad = jnp.where(half == 0, jnp.stack([own, arrived]), jnp.stack([arrived, own]))
-    new_accum = row_accum + jnp.mean(row_grad * row_grad, axis=-1)
-    new_rows = table_rows - learn_rate * row_grad / jnp.sqrt(new_accum)[..., None]
+    part_rows, part_accum = updated(half, table_rows, row_accum, row_accum, own)
+    new_rows, new_accum = updated(1 - half, table_rows, row_accum, part_accum, arrived, (part_rows,))
     return (new_rows, new_accum, dense_grad)
 
 

time: 195 us -> 180 us (0.923)
  waiting for transfers between devices: 82.9 us -> 64.8 us
  starting transfers between devices: 55.3 us -> 45.4 us
  Pallas kernels: 39.8 us -> 49.2 us
  local copies, waits for them, and re-layouts: 6.97 us -> 13.5 us
  other arithmetic: 8.18 us -> 4.19 us
    ppermute x15, waiting for transfers between devices: 82.8 us -> 63.5 us  [to_next(): lax.ppermute(value, axis, [(i, (i + step) % ring) for i in range(ring)])]
    ppermute x4, starting transfers between devices: 15.6 us -> 3.58 us  [dense_sum(): theirs = [lax.ppermute(p, 'c', swap) for p in mine]]
    pallas_call x0 -> x4, Pallas kernels: none -> 9.06 us  [the longest x2 5.1 us: updated(): pl.pallas_call(update_kernel, grid_spec=pltpu.PrefetchScalarGridSpec(num_...]
    unnamed x22 -> x35, local copies, waits for them, and re-layouts: 4.24 us -> 10.1 us
    sub x1 -> x0, other arithmetic: 2.55 us -> none  [per_device(): table_rows - learn_rate * row_grad / jnp.sqrt(new_accum)[..., None]]
  transfers between devices with their start and end apart: 23 -> 23, of which waited for: 12 -> 13; matrix products, arithmetic and copies ran while one was open for 2% -> 6% of each run, Pallas kernels for 19% -> 24%
where the time goes in v4:
time: 180 us
  waiting for transfers between devices  64.8 us (36%)
  Pallas kernels  49.2 us (27%)
  starting transfers between devices  45.4 us (25%)
  local copies, waits for them, and re-layouts  13.5 us (8%)
  other arithmetic  4.19 us (2%)
    ppermute x15, waiting for transfers between devices, to_next(): lax.ppermute(value, axis, [(i, (i + step) % ring) for i in range(ring)])  63.5 us
    pallas_call x3, Pallas kernels, summed(): pl.pallas_call(functools.partial(sum_kernel, part), grid_spec=pltpu.Prefe...  27.9 us
    ppermute x15, starting transfers between devices, to_next(): lax.ppermute(value, axis, [(i, (i + step) % ring) for i in range(ring)])  20.8 us
    all_to_all x2, starting transfers between devices, exchanged(): return lax.all_to_all(value, every, split_axis=0, concat_axis=0, tiled=True)  18.8 us
    unnamed x35, local copies, waits for them, and re-layouts  10.1 us
    pallas_call x2, Pallas kernels, packed(): pl.pallas_call(pack_kernel, grid=(tables // 64,), in_specs=[pl.BlockSpec(...  7.41 us
    pallas_call x2, Pallas kernels, updated(): pl.pallas_call(update_kernel, grid_spec=pltpu.PrefetchScalarGridSpec(num_...  5.1 us
    pallas_call x1, Pallas kernels, placed(): pl.pallas_call(place_kernel, in_specs=[pl.BlockSpec(memory_space=pltpu.SM...  4.87 us
  transfers between devices with their start and end apart: 23, of which 13 were waited for; matrix products, arithmetic and copies ran while one was open for 6% of the time, Pallas kernels for 24%

profile of v4, /device:TPU:1, one launch (start us, length us, event | category | flops | bytes accessed | tf_op | source)
XLA Modules:
  0.0 179.7 jit_solution(3794922962461736423)
XLA Ops:
  0.6 1.1 copy.96
  1.7 0.9 copy.95
  2.8 0.2 fusion.22
  3.4 1.5 stack.62.refs_1_
  4.9 4.2 %pack.2 = bf16[128,88,128]{2,1,0:T(8,128)(2,1)} custom-call(bf16[128,128,128]{2,1,0:T(8,128)(2,1)} %refs_0_.3, bf16[128,8,128]{2,1,0:T(8,128)(2,1)} %stack.62.refs_1_), custom_call_target="tpu_custom_call" | custom-call | flops 671088640 | bytes 4194304 | tf_op jit(solution)/shard_map/pack/pallas_call | solution.py:72
  9.0 11.5 %all-to-all-start = ((bf16[128,88,128]{2,1,0:T(8,128)(2,1)}), bf16[128,88,128]{2,1,0:T(8,128)(2,1)S(1)}, u32[]{:S(2)}, u32[]{:S(2)}) async-start(bf16[128,88,128]{2,1,0:T(8,128)(2,1)} %pack.2), calls=%async_computation | async-start | bytes 5767168 | tf_op jit(solution)/shard_map/all_to_all | solution.py:309
  20.5 2.1 %share.1 = (bf16[128,1024]{1,0:T(8,128)(2,1)}, bf16[128,1024]{1,0:T(8,128)(2,1)}, bf16[128,1024]{1,0:T(8,128)(2,1)}, bf16[128,1024]{1,0:T(8,128)(2,1)}) custom-call(s32[1]{0:T(128)} %bitcast.37.at_ref, bf16[128,1024]{1,0:T(8,128)(2,1)} %left_ref.1, bf16[128,1024]{1,0:T(8,128)(2,1)} %right_ref.1), custom_call_target="tpu_custom_call" | custom-call | flops 524288 | bytes 2097152 | tf_op jit(solution)/shard_map/share/pallas_call | solution.py:230
  22.6 1.4 collective-permute-start.1
  24.0 2.4 %collective-permute-start.2 = (bf16[128,1024]{1,0:T(8,128)(2,1)}, bf16[128,1024]{1,0:T(8,128)(2,1)S(1)}, u32[]{:S(2)}, u32[]{:S(2)}) collective-permute-start(bf16[128,1024]{1,0:T(8,128)(2,1)} %get-tuple-element.17), channel_id=1, source_target_pairs={{0,16},{8,24},{16,0},{24,8},{1,17},{9,25},{17,1},{25,9},{2,18},{10... | collective-permute-start | bytes 786440 | tf_op jit(solution)/shard_map/ppermute | solution.py:143
  26.4 1.2 collective-permute-start.3
  27.6 1.7 constant_dynamic-update-slice_fusion.3
  29.2 30.7 %collective-permute-done.1 = bf16[128,1024]{1,0:T(8,128)(2,1)} collective-permute-done((bf16[128,1024]{1,0:T(8,128)(2,1)}, bf16[128,1024]{1,0:T(8,128)(2,1)}, u32[]{:S(2)}, u32[]{:S(2)}) %collective-permute-start.1) | collective-permute-done | bytes 262176 | tf_op jit(solution)/shard_map/ppermute | solution.py:143
  59.9 1.7 constant_dynamic-update-slice_fusion.2
  61.6 4.0 %collective-permute-done.2 = bf16[128,1024]{1,0:T(8,128)(2,1)S(1)} collective-permute-done((bf16[128,1024]{1,0:T(8,128)(2,1)}, bf16[128,1024]{1,0:T(8,128)(2,1)S(1)}, u32[]{:S(2)}, u32[]{:S(2)}) %collective-permute-start.2) | collective-permute-done | bytes 262176 | tf_op jit(solution)/shard_map/ppermute | solution.py:143
  65.5 0.7 constant_dynamic-update-slice_fusion.1
  66.3 0.7 constant_dynamic-update-slice_fusion
  67.0 1.7 fusion
  68.7 1.0 copy-done.2
  69.7 1.1 collective-permute-start.4
  70.7 3.2 %pack.3 = bf16[128,48,128]{2,1,0:T(8,128)(2,1)} custom-call(bf16[128,128,128]{2,1,0:T(8,128)(2,1)} %refs_0_.3), custom_call_target="tpu_custom_call" | custom-call | flops 402653184 | bytes 4194304 | tf_op jit(solution)/shard_map/pack/pallas_call | solution.py:72
  73.9 7.3 %all-to-all-start.1 = ((bf16[128,48,128]{2,1,0:T(8,128)(2,1)}), bf16[128,48,128]{2,1,0:T(8,128)(2,1)}, u32[]{:S(2)}, u32[]{:S(2)}) async-start(bf16[128,48,128]{2,1,0:T(8,128)(2,1)} %pack.3), calls=%async_computation.1 | async-start | bytes 3145728 | tf_op jit(solution)/shard_map/all_to_all | solution.py:309
  81.3 1.3 bitcast_add_fusion
  82.6 0.7 dynamic-slice_bitcast_fusion.3
  83.3 2.6 %collective-permute-start.7 = (f32[64,512]{1,0:T(8,128)}, f32[64,512]{1,0:T(8,128)}, u32[]{:S(2)}, u32[]{:S(2)}) collective-permute-start(f32[64,512]{1,0:T(8,128)} %get-tuple-element.26), channel_id=1, source_target_pairs={{0,96},{32,0},{64,32},{96,64},{1,97},{33,1},{65,33},{97,65},{2,98}... | collective-permute-start | bytes 393224 | tf_op jit(solution)/shard_map/ppermute | solution.py:143
  85.9 0.5 collective-permute-start.6
  86.4 0.6 collective-permute-start.5
  87.0 14.8 %collective-permute-done.7 = f32[64,512]{1,0:T(8,128)} collective-permute-done((f32[64,512]{1,0:T(8,128)}, f32[64,512]{1,0:T(8,128)}, u32[]{:S(2)}, u32[]{:S(2)}) %collective-permute-start.7) | collective-permute-done | bytes 131104 | tf_op jit(solution)/shard_map/ppermute | solution.py:143
  101.9 1.6 collective-permute-done.6
  103.5 2.9 %collective-permute-done.5 = f32[64,512]{1,0:T(8,128)} collective-permute-done((f32[64,512]{1,0:T(8,128)S(1)}, f32[64,512]{1,0:T(8,128)}, u32[]{:S(2)}, u32[]{:S(2)}) %collective-permute-start.5) | collective-permute-done | bytes 131104 | tf_op jit(solution)/shard_map/ppermute | solution.py:143
  106.4 1.1 fusion.4.refs_0_
  107.5 1.4 collective-permute-start.8
  108.8 3.2 %collective-permute-start.9 = (f32[64,512]{1,0:T(8,128)S(1)}, f32[64,512]{1,0:T(8,128)S(1)}, u32[]{:S(2)}, u32[]{:S(2)}) collective-permute-start(f32[64,512]{1,0:T(8,128)S(1)} %fusion.4.refs_0_), channel_id=1, source_target_pairs={{0,4},{1,5},{4,0},{5,1},{2,6},{3,7},{6,2},{7,3},{8,12},{9,13},{12,... | collective-permute-start | bytes 393224 | tf_op jit(solution)/shard_map/ppermute | solution.py:143
  112.0 0.8 collective-permute-start.10
  112.8 1.3 collective-permute-done.8.refs_1_
  114.1 3.7 %collective-permute-done.9.refs_2_ = f32[64,512]{1,0:T(8,128)S(1)} collective-permute-done((f32[64,512]{1,0:T(8,128)S(1)}, f32[64,512]{1,0:T(8,128)S(1)}, u32[]{:S(2)}, u32[]{:S(2)}) %collective-permute-start.9) | collective-permute-done | bytes 131104 | tf_op jit(solution)/shard_map/ppermute | solution.py:143
  117.8 0.6 copy-done.13
  118.4 0.6 copy-done.14
  119.0 1.9 %code_sum.1 = s16[64,640]{1,0:T(8,128)(2,1)} custom-call(f32[64,512]{1,0:T(8,128)} %copy-done.3, f32[64,512]{1,0:T(8,128)} %copy-done.12, f32[64,512]{1,0:T(8,128)} %copy-done.13, f32[64,512]{1,0:T(8,128)} %copy-done.14), custom_call_target="tpu_custom_call" | custom-call | flops 1048576 | bytes 1048576 | tf_op jit(solution)/shard_map/code_sum/pallas_call | solution.py:175
  120.9 2.0 %collective-permute-start.13 = (s16[64,640]{1,0:T(8,128)(2,1)}, s16[64,640]{1,0:T(8,128)(2,1)S(1)}, u32[]{:S(2)}, u32[]{:S(2)}) collective-permute-start(s16[64,640]{1,0:T(8,128)(2,1)} %code_sum.1), channel_id=1, source_target_pairs={{0,24},{8,0},{16,8},{24,16},{1,25},{9,1},{17,9},{25,17},{2,26},{10... | collective-permute-start | bytes 245768 | tf_op jit(solution)/shard_map/ppermute | solution.py:143
  123.0 0.7 collective-permute-start.12
  123.7 0.6 collective-permute-start.11
  124.3 0.4 collective-permute-done.13
  124.8 3.2 %collective-permute-done.12 = s16[64,640]{1,0:T(8,128)(2,1)S(1)} collective-permute-done((s16[64,640]{1,0:T(8,128)(2,1)}, s16[64,640]{1,0:T(8,128)(2,1)S(1)}, u32[]{:S(2)}, u32[]{:S(2)}) %collective-permute-start.12) | collective-permute-done | bytes 81952 | tf_op jit(solution)/shard_map/ppermute | solution.py:143
  128.0 0.8 collective-permute-done.11
  128.9 0.9 pad_add_fusion.refs_0_
  129.8 0.9 collective-permute-start.14
  130.6 1.7 collective-permute-start.15
  132.3 0.8 collective-permute-start.16
  133.1 14.7 %sum_by_row.3.refs_0_ = f32[2048,128]{1,0:T(8,128)} custom-call(s32[1]{0:T(128)} %constant.55.clone.1.base_ref, bf16[128,88,128]{2,1,0:T(8,128)(2,1)} %copy-done, bf16[128,88,128]{2,1,0:T(8,128)(2,1)} %copy-done), custom_call_target="tpu_custom_call" | custom-call | flops 5368709120 | bytes 3145728 | tf_op jit(solution)/shard_map/sum_by_row/pallas_call | solution.py:123
  147.8 6.6 %sum_by_row.5 = f32[1024,128]{1,0:T(8,128)} custom-call(s32[1]{0:T(128)} %bitcast.35.base_ref, bf16[128,88,128]{2,1,0:T(8,128)(2,1)} %copy-done, bf16[128,48,128]{2,1,0:T(8,128)(2,1)} %all-to-all-done.1.data_ref, f32[2048,128]{1,0:T(8,128)} %sum_by_row.3.refs_0_), custom_call_target="tpu_custom_call" | custom-call | flops 1610612736 | bytes 3145728 | tf_op jit(solution)/shard_map/sum_by_row/pallas_call | solution.py:123
  154.4 1.2 collective-permute-start
  155.6 3.0 %collective-permute-start.17 = (s16[4,64,640]{2,1,0:T(8,128)(2,1)S(1)}, s16[4,64,640]{2,1,0:T(8,128)(2,1)S(1)}, u32[]{:S(2)}, u32[]{:S(2)}) collective-permute-start(s16[4,64,640]{2,1,0:T(8,128)(2,1)S(1)} %pad_add_fusion.refs_0_), channel_id=1, source_target_pairs={{0,2},{2,0},{1,3},{3,1},{4,6},{6,4},{5,7},{7,5},{8,10},{10,8},{9,1... | collective-permute-start | bytes 983048 | tf_op jit(solution)/shard_map/ppermute | solution.py:258
  158.7 0.4 collective-permute-start.19
  159.2 0.7 pad_add_fusion.1.at_ref
  159.9 0.4 collective-permute-done.18.refs_5_
  160.3 0.5 collective-permute-done.19.refs_6_
  160.8 0.5 collective-permute-done.20.refs_7_
  161.3 0.2 copy-done.10
  161.5 0.8 copy-done.11
  162.3 4.9 %place.1 = f32[1024,1024]{1,0:T(8,128)} custom-call(s32[3]{0:T(128)} %pad_add_fusion.1.at_ref, s16[4,64,640]{2,1,0:T(8,128)(2,1)} %copy-done.1, s16[4,64,640]{2,1,0:T(8,128)(2,1)} %copy-done.5, s16[4,64,640]{2,1,0:T(8,128)(2,1)} %copy-done.6, s16[4,64,640]{2,1,0:T(8,128)(2,1)} %copy-done.7, s16[4,64,640]{2,1,0:T(8,128)(2,1)} %copy-done.8, ...), custom_call_target="tpu_custom_call" | custom-call | flops 3145728 | bytes 8388608 | tf_op jit(solution)/shard_map/place/pallas_call | solution.py:208
  167.1 6.6 %sum_by_row.4.grad_ref = f32[1024,128]{1,0:T(8,128)} custom-call(s32[1]{0:T(128)} %bitcast.2.base_ref, bf16[128,88,128]{2,1,0:T(8,128)(2,1)} %copy-done, bf16[128,48,128]{2,1,0:T(8,128)(2,1)} %all-to-all-done.1.data_ref, f32[2048,128]{1,0:T(8,128)} %sum_by_row.3.refs_0_), custom_call_target="tpu_custom_call" | custom-call | flops 1610612736 | bytes 3145728 | tf_op jit(solution)/shard_map/sum_by_row/pallas_call | solution.py:123
  173.7 2.6 %update.2 = (f32[2,1024,128]{2,1,0:T(8,128)}, f32[2,1024]{1,0:T(2,128)}) custom-call(s32[1]{0:T(128)} %bitcast.1.at_ref, f32[2,1024,128]{2,1,0:T(8,128)} %table_ref.3, f32[2,1024]{1,0:T(2,128)} %accum_ref.3, f32[2,1024]{1,0:T(2,128)} %accum_ref.3, f32[1024,128]{1,0:T(8,128)} %sum_by_row.4.grad_ref), custom_call_target="tpu_custom_call" | custom-call | flops 1048576 | bytes 2097152 | tf_op jit(solution)/shard_map/update/pallas_call | solution.py:280
  176.3 0.8 copy-done.4
  177.1 2.6 %update.3 = (f32[2,1024,128]{2,1,0:T(8,128)}, f32[2,1024]{1,0:T(2,128)}) custom-call(s32[1]{0:T(128)} %bitcast.at_ref, f32[2,1024,128]{2,1,0:T(8,128)} %table_ref.3, f32[2,1024]{1,0:T(2,128)} %accum_ref.3, f32[2,1024]{1,0:T(2,128)} %get-tuple-element.11.prior_ref, f32[1024,128]{1,0:T(8,128)} %copy-done.4, ...), custom_call_target="tpu_custom_call", output_to_operand_aliasing={{0}: (5, {})} | custom-call | flops 1048576 | bytes 2097152 | tf_op jit(solution)/shard_map/update/pallas_call | solution.py:280
  (48 shorter events, 0.8 us)
Async XLA Ops:
  9.0 64.9 %all-to-all-start = ((bf16[128,88,128]{2,1,0:T(8,128)(2,1)}), bf16[128,88,128]{2,1,0:T(8,128)(2,1)S(1)}, u32[]{:S(2)}, u32[]{:S(2)}) async-start(bf16[128,88,128]{2,1,0:T(8,128)(2,1)} %pack.2), calls=%async_computation | async-start | bytes 5767168 | tf_op jit(solution)/shard_map/all_to_all | solution.py:309
  22.6 37.3 %collective-permute-start.1 = (bf16[128,1024]{1,0:T(8,128)(2,1)}, bf16[128,1024]{1,0:T(8,128)(2,1)}, u32[]{:S(2)}, u32[]{:S(2)}) collective-permute-start(bf16[128,1024]{1,0:T(8,128)(2,1)} %get-tuple-element.16), channel_id=1, source_target_pairs={{0,8},{8,16},{16,24},{24,0},{1,9},{9,17},{17,25},{25,1},{2,10},{10... | collective-permute-start | bytes 786440 | tf_op jit(solution)/shard_map/ppermute | solution.py:143
  24.0 41.6 %collective-permute-start.2 = (bf16[128,1024]{1,0:T(8,128)(2,1)}, bf16[128,1024]{1,0:T(8,128)(2,1)S(1)}, u32[]{:S(2)}, u32[]{:S(2)}) collective-permute-start(bf16[128,1024]{1,0:T(8,128)(2,1)} %get-tuple-element.17), channel_id=1, source_target_pairs={{0,16},{8,24},{16,0},{24,8},{1,17},{9,25},{17,1},{25,9},{2,18},{10... | collective-permute-start | bytes 786440 | tf_op jit(solution)/shard_map/ppermute | solution.py:143
  26.4 39.9 %collective-permute-start.3 = (bf16[128,1024]{1,0:T(8,128)(2,1)}, bf16[128,1024]{1,0:T(8,128)(2,1)S(1)}, u32[]{:S(2)}, u32[]{:S(2)}) collective-permute-start(bf16[128,1024]{1,0:T(8,128)(2,1)} %get-tuple-element.18), channel_id=1, source_target_pairs={{0,24},{8,0},{16,8},{24,16},{1,25},{9,1},{17,9},{25,17},{2,26},{10... | collective-permute-start | bytes 786440 | tf_op jit(solution)/shard_map/ppermute | solution.py:143
  68.6 1.0 copy-start.2
  69.7 11.6 %collective-permute-start.4 = (f32[256,512]{1,0:T(8,128)S(1)}, f32[256,512]{1,0:T(8,128)}, u32[]{:S(2)}, u32[]{:S(2)}) collective-permute-start(f32[256,512]{1,0:T(8,128)S(1)} %dynamic-slice_bitcast_fusion), channel_id=1, source_target_pairs={{0,2},{2,0},{1,3},{3,1},{4,6},{6,4},{5,7},{7,5},{8,10},{10,8},{9,1... | collective-permute-start | bytes 1572872 | tf_op jit(solution)/shard_map/ppermute | solution.py:252
  73.9 33.5 %copy-start = (bf16[128,88,128]{2,1,0:T(8,128)(2,1)}, bf16[128,88,128]{2,1,0:T(8,128)(2,1)S(1)}, u32[]{:S(2)}) copy-start(bf16[128,88,128]{2,1,0:T(8,128)(2,1)S(1)} %all-to-all-done.info_ref.data_ref) | copy-start | bytes 8650756
  73.9 73.9 %all-to-all-start.1 = ((bf16[128,48,128]{2,1,0:T(8,128)(2,1)}), bf16[128,48,128]{2,1,0:T(8,128)(2,1)}, u32[]{:S(2)}, u32[]{:S(2)}) async-start(bf16[128,48,128]{2,1,0:T(8,128)(2,1)} %pack.3), calls=%async_computation.1 | async-start | bytes 3145728 | tf_op jit(solution)/shard_map/all_to_all | solution.py:309
  83.3 18.6 %collective-permute-start.7 = (f32[64,512]{1,0:T(8,128)}, f32[64,512]{1,0:T(8,128)}, u32[]{:S(2)}, u32[]{:S(2)}) collective-permute-start(f32[64,512]{1,0:T(8,128)} %get-tuple-element.26), channel_id=1, source_target_pairs={{0,96},{32,0},{64,32},{96,64},{1,97},{33,1},{65,33},{97,65},{2,98}... | collective-permute-start | bytes 393224 | tf_op jit(solution)/shard_map/ppermute | solution.py:143
  85.9 17.6 %collective-permute-start.6 = (f32[64,512]{1,0:T(8,128)}, f32[64,512]{1,0:T(8,128)}, u32[]{:S(2)}, u32[]{:S(2)}) collective-permute-start(f32[64,512]{1,0:T(8,128)} %get-tuple-element.27), channel_id=1, source_target_pairs={{0,64},{32,96},{64,0},{96,32},{1,65},{33,97},{65,1},{97,33},{2,66}... | collective-permute-start | bytes 393224 | tf_op jit(solution)/shard_map/ppermute | solution.py:143
  86.4 19.9 %collective-permute-start.5 = (f32[64,512]{1,0:T(8,128)S(1)}, f32[64,512]{1,0:T(8,128)}, u32[]{:S(2)}, u32[]{:S(2)}) collective-permute-start(f32[64,512]{1,0:T(8,128)S(1)} %get-tuple-element.25), channel_id=1, source_target_pairs={{0,32},{32,64},{64,96},{96,0},{1,33},{33,65},{65,97},{97,1},{2,34}... | collective-permute-start | bytes 393224 | tf_op jit(solution)/shard_map/ppermute | solution.py:143
  107.4 10.3 %copy-start.3 = (f32[64,512]{1,0:T(8,128)}, f32[64,512]{1,0:T(8,128)S(1)}, u32[]{:S(2)}) copy-start(f32[64,512]{1,0:T(8,128)S(1)} %fusion.4.refs_0_) | copy-start | bytes 393220
  107.5 6.6 %collective-permute-start.8 = (f32[64,512]{1,0:T(8,128)S(1)}, f32[64,512]{1,0:T(8,128)S(1)}, u32[]{:S(2)}, u32[]{:S(2)}) collective-permute-start(f32[64,512]{1,0:T(8,128)S(1)} %fusion.4.refs_0_), channel_id=1, source_target_pairs={{0,1},{1,4},{4,5},{5,0},{2,3},{3,6},{6,7},{7,2},{8,9},{9,12},{12,1... | collective-permute-start | bytes 393224 | tf_op jit(solution)/shard_map/ppermute | solution.py:143
  108.8 8.9 %collective-permute-start.9 = (f32[64,512]{1,0:T(8,128)S(1)}, f32[64,512]{1,0:T(8,128)S(1)}, u32[]{:S(2)}, u32[]{:S(2)}) collective-permute-start(f32[64,512]{1,0:T(8,128)S(1)} %fusion.4.refs_0_), channel_id=1, source_target_pairs={{0,4},{1,5},{4,0},{5,1},{2,6},{3,7},{6,2},{7,3},{8,12},{9,13},{12,... | collective-permute-start | bytes 393224 | tf_op jit(solution)/shard_map/ppermute | solution.py:143
  112.0 5.7 %collective-permute-start.10 = (f32[64,512]{1,0:T(8,128)S(1)}, f32[64,512]{1,0:T(8,128)S(1)}, u32[]{:S(2)}, u32[]{:S(2)}) collective-permute-start(f32[64,512]{1,0:T(8,128)S(1)} %fusion.4.refs_0_), channel_id=1, source_target_pairs={{0,5},{1,0},{4,1},{5,4},{2,7},{3,2},{6,3},{7,6},{8,13},{9,8},{12,9... | collective-permute-start | bytes 393224 | tf_op jit(solution)/shard_map/ppermute | solution.py:143
  114.0 3.7 %copy-start.12 = (f32[64,512]{1,0:T(8,128)}, f32[64,512]{1,0:T(8,128)S(1)}, u32[]{:S(2)}) copy-start(f32[64,512]{1,0:T(8,128)S(1)} %collective-permute-done.8.refs_1_) | copy-start | bytes 393220
  117.8 0.6 copy-start.13
  118.4 0.7 copy-start.14
  120.9 3.8 %collective-permute-start.13 = (s16[64,640]{1,0:T(8,128)(2,1)}, s16[64,640]{1,0:T(8,128)(2,1)S(1)}, u32[]{:S(2)}, u32[]{:S(2)}) collective-permute-start(s16[64,640]{1,0:T(8,128)(2,1)} %code_sum.1), channel_id=1, source_target_pairs={{0,24},{8,0},{16,8},{24,16},{1,25},{9,1},{17,9},{25,17},{2,26},{10... | collective-permute-start | bytes 245768 | tf_op jit(solution)/shard_map/ppermute | solution.py:143
  123.0 5.1 %collective-permute-start.12 = (s16[64,640]{1,0:T(8,128)(2,1)}, s16[64,640]{1,0:T(8,128)(2,1)S(1)}, u32[]{:S(2)}, u32[]{:S(2)}) collective-permute-start(s16[64,640]{1,0:T(8,128)(2,1)} %code_sum.1), channel_id=1, source_target_pairs={{0,16},{8,24},{16,0},{24,8},{1,17},{9,25},{17,1},{25,9},{2,18},{10... | collective-permute-start | bytes 245768 | tf_op jit(solution)/shard_map/ppermute | solution.py:143
  123.7 5.1 %collective-permute-start.11 = (s16[64,640]{1,0:T(8,128)(2,1)}, s16[64,640]{1,0:T(8,128)(2,1)S(1)}, u32[]{:S(2)}, u32[]{:S(2)}) collective-permute-start(s16[64,640]{1,0:T(8,128)(2,1)} %code_sum.1), channel_id=1, source_target_pairs={{0,8},{8,16},{16,24},{24,0},{1,9},{9,17},{17,25},{25,1},{2,10},{10... | collective-permute-start | bytes 245768 | tf_op jit(solution)/shard_map/ppermute | solution.py:143
  129.8 25.8 %copy-start.1 = (s16[4,64,640]{2,1,0:T(8,128)(2,1)}, s16[4,64,640]{2,1,0:T(8,128)(2,1)S(1)}, u32[]{:S(2)}) copy-start(s16[4,64,640]{2,1,0:T(8,128)(2,1)S(1)} %pad_add_fusion.refs_0_) | copy-start | bytes 983044
  129.8 28.8 %collective-permute-start.14 = (s16[4,64,640]{2,1,0:T(8,128)(2,1)S(1)}, s16[4,64,640]{2,1,0:T(8,128)(2,1)S(1)}, u32[]{:S(2)}, u32[]{:S(2)}) collective-permute-start(s16[4,64,640]{2,1,0:T(8,128)(2,1)S(1)} %pad_add_fusion.refs_0_), channel_id=1, source_target_pairs={{0,32},{32,64},{64,96},{96,0},{1,33},{33,65},{65,97},{97,1},{2,34}... | collective-permute-start | bytes 983048 | tf_op jit(solution)/shard_map/ppermute | solution.py:143
  130.6 28.0 %collective-permute-start.15 = (s16[4,64,640]{2,1,0:T(8,128)(2,1)S(1)}, s16[4,64,640]{2,1,0:T(8,128)(2,1)S(1)}, u32[]{:S(2)}, u32[]{:S(2)}) collective-permute-start(s16[4,64,640]{2,1,0:T(8,128)(2,1)S(1)} %pad_add_fusion.refs_0_), channel_id=1, source_target_pairs={{0,64},{32,96},{64,0},{96,32},{1,65},{33,97},{65,1},{97,33},{2,66}... | collective-permute-start | bytes 983048 | tf_op jit(solution)/shard_map/ppermute | solution.py:143
  132.3 26.8 %collective-permute-start.16 = (s16[4,64,640]{2,1,0:T(8,128)(2,1)S(1)}, s16[4,64,640]{2,1,0:T(8,128)(2,1)S(1)}, u32[]{:S(2)}, u32[]{:S(2)}) collective-permute-start(s16[4,64,640]{2,1,0:T(8,128)(2,1)S(1)} %pad_add_fusion.refs_0_), channel_id=1, source_target_pairs={{0,96},{32,0},{64,32},{96,64},{1,97},{33,1},{65,33},{97,65},{2,98}... | collective-permute-start | bytes 983048 | tf_op jit(solution)/shard_map/ppermute | solution.py:143
  154.4 21.9 %collective-permute-start = (f32[1024,128]{1,0:T(8,128)}, f32[1024,128]{1,0:T(8,128)S(1)}, u32[]{:S(2)}, u32[]{:S(2)}) collective-permute-start(f32[1024,128]{1,0:T(8,128)} %sum_by_row.5), channel_id=1, source_target_pairs={{0,1},{1,0},{2,3},{3,2},{4,5},{5,4},{6,7},{7,6},{8,9},{9,8},{10,11... | collective-permute-start | bytes 1572872 | tf_op jit(solution)/shard_map/ppermute | solution.py:318
  155.6 4.2 %collective-permute-start.17 = (s16[4,64,640]{2,1,0:T(8,128)(2,1)S(1)}, s16[4,64,640]{2,1,0:T(8,128)(2,1)S(1)}, u32[]{:S(2)}, u32[]{:S(2)}) collective-permute-start(s16[4,64,640]{2,1,0:T(8,128)(2,1)S(1)} %pad_add_fusion.refs_0_), channel_id=1, source_target_pairs={{0,2},{2,0},{1,3},{3,1},{4,6},{6,4},{5,7},{7,5},{8,10},{10,8},{9,1... | collective-permute-start | bytes 983048 | tf_op jit(solution)/shard_map/ppermute | solution.py:258
  158.6 2.7 %copy-start.5 = (s16[4,64,640]{2,1,0:T(8,128)(2,1)}, s16[4,64,640]{2,1,0:T(8,128)(2,1)S(1)}, u32[]{:S(2)}) copy-start(s16[4,64,640]{2,1,0:T(8,128)(2,1)S(1)} %collective-permute-done.14.refs_1_) | copy-start | bytes 983044
  158.6 1.7 collective-permute-start.18
  158.7 2.6 %copy-start.6 = (s16[4,64,640]{2,1,0:T(8,128)(2,1)}, s16[4,64,640]{2,1,0:T(8,128)(2,1)S(1)}, u32[]{:S(2)}) copy-start(s16[4,64,640]{2,1,0:T(8,128)(2,1)S(1)} %collective-permute-done.15.refs_2_) | copy-start | bytes 983044
  158.7 2.1 %collective-permute-start.19 = (s16[4,64,640]{2,1,0:T(8,128)(2,1)S(1)}, s16[4,64,640]{2,1,0:T(8,128)(2,1)S(1)}, u32[]{:S(2)}, u32[]{:S(2)}) collective-permute-start(s16[4,64,640]{2,1,0:T(8,128)(2,1)S(1)} %collective-permute-done.15.refs_2_), channel_id=1, source_target_pairs={{0,2},{2,0},{1,3},{3,1},{4,6},{6,4},{5,7},{7,5},{8,10},{10,8},{9,1... | collective-permute-start | bytes 983048 | tf_op jit(solution)/shard_map/ppermute | solution.py:258
  159.1 2.1 %copy-start.7 = (s16[4,64,640]{2,1,0:T(8,128)(2,1)}, s16[4,64,640]{2,1,0:T(8,128)(2,1)S(1)}, u32[]{:S(2)}) copy-start(s16[4,64,640]{2,1,0:T(8,128)(2,1)S(1)} %collective-permute-done.16.refs_3_) | copy-start | bytes 983044
  159.1 2.1 %collective-permute-start.20 = (s16[4,64,640]{2,1,0:T(8,128)(2,1)S(1)}, s16[4,64,640]{2,1,0:T(8,128)(2,1)S(1)}, u32[]{:S(2)}, u32[]{:S(2)}) collective-permute-start(s16[4,64,640]{2,1,0:T(8,128)(2,1)S(1)} %collective-permute-done.16.refs_3_), channel_id=1, source_target_pairs={{0,2},{2,0},{1,3},{3,1},{4,6},{6,4},{5,7},{7,5},{8,10},{10,8},{9,1... | collective-permute-start | bytes 983048 | tf_op jit(solution)/shard_map/ppermute | solution.py:258
  159.8 1.4 copy-start.8
  160.3 1.0 copy-start.9
  160.8 0.7 copy-start.10
  161.5 0.8 copy-start.11
  176.3 0.8 copy-start.4

commit v5 on v4

--- a/solution.py
+++ b/solution.py
@@ -21,27 +21,40 @@
     return jnp.where(row >= 1024, -size, size)
 
 
-def coded(row):
-    return sized(row).astype(f32).astype(bf16)
-
-
-def slot_codes(lengths, looked):
-    rows = jnp.transpose(looked, (1, 2, 0))
-    count = jnp.transpose(lengths, (1, 0))
-    slots = rows.shape[1]
-    active = [count > j for j in range(slots)]
-    row = [rows[:, j, :] for j in range(slots)]
-    codes, weights = [], []
+def codes_kernel(row_ref, count_ref, out_ref):
+    samples, slots, tables = row_ref.shape
+    row = [row_ref[:, j, :] for j in range(slots)]
+    active = [count_ref[...] > j for j in range(slots)]
+    kinds = []
     for j in range(slots):
         first = active[j]
         for i in range(j):
             first = first & (row[i] != row[j])
-        weight = jnp.ones_like(count)
+        kinds.append(jnp.where(first, sized(row[j]), 0))
+    for j in range(slots):
+        weight = jnp.ones_like(row[j])
         for i in range(j + 1, slots):
-            weight = weight + (active[i] & (row[i] == row[j])).astype(jnp.int32)
-        codes.append(jnp.where(first, coded(row[j]), jnp.zeros((), bf16)))
-        weights.append(weight.astype(f32).astype(bf16))
-    return jnp.stack(codes + weights, axis=1)
+            weight = weight + jnp.where(active[i] & (row[i] == row[j]), 1, 0)
+        kinds.append(weight)
+    kinds = [kind.astype(f32).T.astype(bf16) for kind in kinds]
+    size = 16 * len(kinds)
+    to = lax.broadcasted_iota(jnp.int32, (size, size), 0)
+    of = lax.broadcasted_iota(jnp.int32, (size, size), 1)
+    turn = jnp.where(((to & 7) == (of >> 4)) & ((to >> 3) == (of & 15)), 1.0, 0.0).astype(bf16)
+    for top in range(0, tables, 16):
+        block = jnp.concatenate([kind[top : top + 16, :] for kind in kinds], axis=0)
+        turned = jnp.dot(turn, block, preferred_element_type=f32)
+        out_ref[top : top + 16] = turned.reshape(16, len(kinds), samples).astype(bf16)
+
+
+def slot_codes(lengths, looked):
+    samples, tables, slots = looked.shape
+    return pl.pallas_call(
+        codes_kernel,
+        out_shape=jax.ShapeDtypeStruct((tables, 2 * slots, samples), bf16),
+        cost_estimate=pl.CostEstimate(flops=1 << 20, bytes_accessed=1 << 20, transcendentals=0),
+        name="slot_codes",
+    )(jnp.transpose(looked, (0, 2, 1)), lengths)
 
 
 def pack_kernel(*refs):
@@ -83,7 +96,7 @@
 
 
 cut = (0, 80, 128)
-group = 16
+group = 32
 stripe = 512
 
 
@@ -119,7 +132,7 @@
 def summed(part, first, data, base, rows, before=()):
     senders, _, width = data.shape
     samples = cut[part + 1] - cut[part]
-    step = 32
+    step = 64
     return pl.pallas_call(
         functools.partial(sum_kernel, part),
         grid_spec=pltpu.PrefetchScalarGridSpec(
@@ -181,38 +194,46 @@
 
 
 def place_kernel(at_ref, *refs):
-    pieces, out_ref, held, sems = refs[: 2 * ring], refs[-3], refs[-2], refs[-1]
-    here_y, here_x, here_c = (at_ref[k] for k in range(3))
-    copies = []
-    for number, piece in enumerate(pieces):
-        c = here_c if number < ring else 1 - here_c
-        y = (here_y - number) & 3
-        for dx in range(ring):
-            x = (here_x - dx) & 3
-            left = pl.multiple_of((x & 1) * 512, 512)
-            top = pl.multiple_of((x >> 1) * 512 + c * 256 + y * 64, 64)
-            block = piece[dx].astype(jnp.int32)
-            step = step_of(block[:, 512:513], block[:, 513:514])
-            held[number, dx] = block[:, :512].astype(f32) * step
-            copies.append(
-                pltpu.make_async_copy(
-                    held.at[number, dx], out_ref.at[pl.ds(top, 64), pl.ds(left, 512)], sems.at[number, dx]
+    pieces, (out_ref, held, sems, taken, ins) = refs[:2], refs[2:]
+    here_x, here_c = at_ref[0], at_ref[1]
+    loads = {}
+    for core in range(2):
+        for y in range(ring):
+            load = pltpu.make_async_copy(pieces[core].at[y], taken.at[core, y], ins.at[core, y])
+            load.start()
+            loads[core, y] = load
+    stores = []
+    for core in range(2):
+        c = here_c if core == 0 else 1 - here_c
+        for y in range(ring):
+            loads[core, y].wait()
+            for dx in range(ring):
+                x = (here_x - dx) & 3
+                left = pl.multiple_of((x & 1) * 512, 512)
+                top = pl.multiple_of((x >> 1) * 512 + c * 256 + y * 64, 64)
+                block = taken[core, y, dx].astype(jnp.int32)
+                step = step_of(block[:, 512:513], block[:, 513:514])
+                held[core, y, dx] = block[:, :512].astype(f32) * step
+                store = pltpu.make_async_copy(
+                    held.at[core, y, dx], out_ref.at[pl.ds(top, 64), pl.ds(left, 512)], sems.at[core, y, dx]
                 )
-            )
-            copies[-1].start()
-    for copy in copies:
-        copy.wait()
+                store.start()
+                stores.append(store)
+    for store in stores:
+        store.wait()
 
 
 def placed(at, pieces):
     return pl.pallas_call(
         place_kernel,
-        in_specs=[pl.BlockSpec(memory_space=pltpu.SMEM)] + [pl.BlockSpec(memory_space=pltpu.VMEM)] * len(pieces),
+        in_specs=[pl.BlockSpec(memory_space=pltpu.SMEM)] + [pl.BlockSpec(memory_space=pl.ANY)] * 2,
         out_specs=pl.BlockSpec(memory_space=pl.ANY),
         out_shape=jax.ShapeDtypeStruct((1024, 1024), f32),
         scratch_shapes=[
-            pltpu.VMEM((2 * ring, ring, 64, 512), f32),
-            pltpu.SemaphoreType.DMA((2 * ring, ring)),
+            pltpu.VMEM((2, ring, ring, 64, 512), f32),
+            pltpu.SemaphoreType.DMA((2, ring, ring)),
+            pltpu.VMEM((2, ring, ring, 64, 640), jnp.int16),
+            pltpu.SemaphoreType.DMA((2, ring)),
         ],
         cost_estimate=pl.CostEstimate(flops=3 << 20, bytes_accessed=8 << 20, transcendentals=0),
         name="place",
@@ -254,9 +275,11 @@
     total = scattered(total.reshape(ring, 64, 512), "y", y)
     ranks = gathered(total, deep)
     total = coded_sum(ranks)
-    mine = gathered(jnp.stack(gathered(total, "x")), "y")
-    theirs = [lax.ppermute(p, "c", swap) for p in mine]
-    return placed(jnp.stack([y, x, c]).astype(jnp.int32), mine + theirs)
+    total = jnp.stack(gathered(total, "x"))
+    total = jnp.broadcast_to(total[None], (ring, *total.shape))
+    mine = lax.all_to_all(total, "y", split_axis=0, concat_axis=0, tiled=True)
+    theirs = lax.ppermute(mine, "c", swap)
+    return placed(jnp.stack([x, c]).astype(jnp.int32), (mine, theirs))
 
 
 def update_kernel(at_ref, table_ref, accum_ref, prior_ref, grad_ref, *refs):

time: 180 us -> 186 us (1.033)
  waiting for transfers between devices: 64.8 us -> 82.6 us
  starting transfers between devices: 45.4 us -> 39.3 us
  local copies, waits for them, and re-layouts: 13.5 us -> 8.15 us
  other arithmetic: 4.19 us -> 1.7 us
    all_to_all x2, waiting for transfers between devices: 0.01 us -> 43.5 us  [exchanged(): return lax.all_to_all(value, every, split_axis=0, concat_axis=0, tiled=True)]
    ppermute x15 -> x12, waiting for transfers between devices: 63.5 us -> 27.9 us  [to_next(): lax.ppermute(value, axis, [(i, (i + step) % ring) for i in range(ring)])]
    all_to_all x0 -> x1, waiting for transfers between devices: none -> 7.47 us  [dense_sum(): mine = lax.all_to_all(total, 'y', split_axis=0, concat_axis=0, tiled=True)]
    all_to_all x2, starting transfers between devices: 18.8 us -> 13.5 us  [exchanged(): return lax.all_to_all(value, every, split_axis=0, concat_axis=0, tiled=True)]
    pallas_call x0 -> x1, Pallas kernels: none -> 3.55 us  [slot_codes(): pl.pallas_call(codes_kernel, out_shape=jax.ShapeDtypeStruct((tables, 2 *...]
    all_to_all x0 -> x1, starting transfers between devices: none -> 3.54 us  [dense_sum(): mine = lax.all_to_all(total, 'y', split_axis=0, concat_axis=0, tiled=True)]
    unnamed x35 -> x19, local copies, waits for them, and re-layouts: 10.1 us -> 6.81 us
    ppermute x15 -> x12, starting transfers between devices: 20.8 us -> 18.4 us  [to_next(): lax.ppermute(value, axis, [(i, (i + step) % ring) for i in range(ring)])]
  transfers between devices with their start and end apart: 23 -> 18, of which waited for: 13 -> 15; matrix products, arithmetic and copies ran while one was open for 6% -> 1% of each run, Pallas kernels for 24% -> 23%
where the time goes in v5:
time: 186 us; the launch traced here: 184 us
  waiting for transfers between devices  82.6 us (44%)
  Pallas kernels  50.9 us (27%)
  starting transfers between devices  39.3 us (21%)
  local copies, waits for them, and re-layouts  8.15 us (4%)
    all_to_all x2, waiting for transfers between devices, exchanged(): return lax.all_to_all(value, every, split_axis=0, concat_axis=0, tiled=True)  43.5 us
    ppermute x12, waiting for transfers between devices, to_next(): lax.ppermute(value, axis, [(i, (i + step) % ring) for i in range(ring)])  27.9 us
    pallas_call x3, Pallas kernels, summed(): pl.pallas_call(functools.partial(sum_kernel, part), grid_spec=pltpu.Prefe...  26.7 us
    ppermute x12, starting transfers between devices, to_next(): lax.ppermute(value, axis, [(i, (i + step) % ring) for i in range(ring)])  18.4 us
    all_to_all x2, starting transfers between devices, exchanged(): return lax.all_to_all(value, every, split_axis=0, concat_axis=0, tiled=True)  13.5 us
    all_to_all x1, waiting for transfers between devices, dense_sum(): mine = lax.all_to_all(total, 'y', split_axis=0, concat_axis=0, tiled=True)  7.47 us
    pallas_call x2, Pallas kernels, packed(): pl.pallas_call(pack_kernel, grid=(tables // 64,), in_specs=[pl.BlockSpec(...  7.41 us
    unnamed x19, local copies, waits for them, and re-layouts  6.81 us
  transfers between devices with their start and end apart: 18, of which 15 were waited for; matrix products, arithmetic and copies ran while one was open for 1% of the time, Pallas kernels for 23%

profile of v5, /device:TPU:1, one launch (start us, length us, event | category | flops | bytes accessed | tf_op | source)
XLA Modules:
  0.0 184.1 jit_solution(11734381944480922704)
XLA Ops:
  0.6 2.1 %share.1 = (bf16[128,1024]{1,0:T(8,128)(2,1)}, bf16[128,1024]{1,0:T(8,128)(2,1)}, bf16[128,1024]{1,0:T(8,128)(2,1)}, bf16[128,1024]{1,0:T(8,128)(2,1)}) custom-call(s32[1]{0:T(128)} %bitcast.5.at_ref, bf16[128,1024]{1,0:T(8,128)(2,1)} %left_ref.1, bf16[128,1024]{1,0:T(8,128)(2,1)} %right_ref.1), custom_call_target="tpu_custom_call" | custom-call | flops 524288 | bytes 2097152 | tf_op jit(solution)/shard_map/share/pallas_call | solution.py:251
  2.7 2.0 %collective-permute-start.1 = (bf16[128,1024]{1,0:T(8,128)(2,1)}, bf16[128,1024]{1,0:T(8,128)(2,1)S(1)}, u32[]{:S(2)}, u32[]{:S(2)}) collective-permute-start(bf16[128,1024]{1,0:T(8,128)(2,1)} %get-tuple-element.16), channel_id=1, source_target_pairs={{0,8},{8,16},{16,24},{24,0},{1,9},{9,17},{17,25},{25,1},{2,10},{10... | collective-permute-start | bytes 786440 | tf_op jit(solution)/shard_map/ppermute | solution.py:156
  4.7 2.5 %collective-permute-start.2 = (bf16[128,1024]{1,0:T(8,128)(2,1)}, bf16[128,1024]{1,0:T(8,128)(2,1)S(1)}, u32[]{:S(2)}, u32[]{:S(2)}) collective-permute-start(bf16[128,1024]{1,0:T(8,128)(2,1)} %get-tuple-element.17), channel_id=1, source_target_pairs={{0,16},{8,24},{16,0},{24,8},{1,17},{9,25},{17,1},{25,9},{2,18},{10... | collective-permute-start | bytes 786440 | tf_op jit(solution)/shard_map/ppermute | solution.py:156
  7.2 1.2 collective-permute-start.3
  8.3 1.0 constant_dynamic-update-slice_fusion.3
  9.3 2.5 %collective-permute-done.1 = bf16[128,1024]{1,0:T(8,128)(2,1)S(1)} collective-permute-done((bf16[128,1024]{1,0:T(8,128)(2,1)}, bf16[128,1024]{1,0:T(8,128)(2,1)S(1)}, u32[]{:S(2)}, u32[]{:S(2)}) %collective-permute-start.1) | collective-permute-done | bytes 262176 | tf_op jit(solution)/shard_map/ppermute | solution.py:156
  11.9 6.9 %collective-permute-done.2 = bf16[128,1024]{1,0:T(8,128)(2,1)S(1)} collective-permute-done((bf16[128,1024]{1,0:T(8,128)(2,1)}, bf16[128,1024]{1,0:T(8,128)(2,1)S(1)}, u32[]{:S(2)}, u32[]{:S(2)}) %collective-permute-start.2) | collective-permute-done | bytes 262176 | tf_op jit(solution)/shard_map/ppermute | solution.py:156
  18.8 0.0 collective-permute-done.3
  18.8 0.5 fusion
  19.3 1.6 collective-permute-start.4
  20.9 1.5 collective-permute-done.4
  22.5 0.1 bitcast_add_fusion
  22.6 2.8 %collective-permute-start.7 = (f32[64,512]{1,0:T(8,128)S(1)}, f32[64,512]{1,0:T(8,128)S(1)}, u32[]{:S(2)}, u32[]{:S(2)}) collective-permute-start(f32[64,512]{1,0:T(8,128)S(1)} %get-tuple-element.20), channel_id=1, source_target_pairs={{0,96},{32,0},{64,32},{96,64},{1,97},{33,1},{65,33},{97,65},{2,98}... | collective-permute-start | bytes 393224 | tf_op jit(solution)/shard_map/ppermute | solution.py:156
  25.4 0.3 collective-permute-start.6
  25.7 0.7 collective-permute-start.5
  26.4 4.1 %collective-permute-done.7 = f32[64,512]{1,0:T(8,128)S(1)} collective-permute-done((f32[64,512]{1,0:T(8,128)S(1)}, f32[64,512]{1,0:T(8,128)S(1)}, u32[]{:S(2)}, u32[]{:S(2)}) %collective-permute-start.7) | collective-permute-done | bytes 131104 | tf_op jit(solution)/shard_map/ppermute | solution.py:156
  30.6 0.7 collective-permute-done.6
  31.3 3.8 %collective-permute-done.5 = f32[64,512]{1,0:T(8,128)S(1)} collective-permute-done((f32[64,512]{1,0:T(8,128)S(1)}, f32[64,512]{1,0:T(8,128)S(1)}, u32[]{:S(2)}, u32[]{:S(2)}) %collective-permute-start.5) | collective-permute-done | bytes 131104 | tf_op jit(solution)/shard_map/ppermute | solution.py:156
  35.2 0.0 copy-start.3
  35.2 1.7 collective-permute-start.8
  36.9 3.3 %collective-permute-start.9 = (f32[64,512]{1,0:T(8,128)S(1)}, f32[64,512]{1,0:T(8,128)S(1)}, u32[]{:S(2)}, u32[]{:S(2)}) collective-permute-start(f32[64,512]{1,0:T(8,128)S(1)} %fusion.4.refs_0_), channel_id=1, source_target_pairs={{0,4},{1,5},{4,0},{5,1},{2,6},{3,7},{6,2},{7,3},{8,12},{9,13},{12,... | collective-permute-start | bytes 393224 | tf_op jit(solution)/shard_map/ppermute | solution.py:156
  40.2 0.7 collective-permute-start.10
  40.9 1.5 collective-permute-done.8.refs_1_
  42.4 0.0 copy-start.5
  42.4 3.7 %collective-permute-done.9.refs_2_ = f32[64,512]{1,0:T(8,128)S(1)} collective-permute-done((f32[64,512]{1,0:T(8,128)S(1)}, f32[64,512]{1,0:T(8,128)S(1)}, u32[]{:S(2)}, u32[]{:S(2)}) %collective-permute-start.9) | collective-permute-done | bytes 131104 | tf_op jit(solution)/shard_map/ppermute | solution.py:156
  46.1 0.0 copy-start.6
  46.1 0.0 collective-permute-done.10.refs_3_
  46.1 0.0 copy-done.3
  46.1 0.0 copy-done.5
  46.1 0.6 copy-done.6
  46.8 0.7 copy-done.7
  47.4 1.9 %code_sum.1 = s16[64,640]{1,0:T(8,128)(2,1)} custom-call(f32[64,512]{1,0:T(8,128)} %copy-done.3, f32[64,512]{1,0:T(8,128)} %copy-done.5, f32[64,512]{1,0:T(8,128)} %copy-done.6, f32[64,512]{1,0:T(8,128)} %copy-done.7), custom_call_target="tpu_custom_call" | custom-call | flops 1048576 | bytes 1048576 | tf_op jit(solution)/shard_map/code_sum/pallas_call | solution.py:188
  49.3 1.9 %collective-permute-start.13 = (s16[64,640]{1,0:T(8,128)(2,1)}, s16[64,640]{1,0:T(8,128)(2,1)S(1)}, u32[]{:S(2)}, u32[]{:S(2)}) collective-permute-start(s16[64,640]{1,0:T(8,128)(2,1)} %code_sum.1), channel_id=1, source_target_pairs={{0,24},{8,0},{16,8},{24,16},{1,25},{9,1},{17,9},{25,17},{2,26},{10... | collective-permute-start | bytes 245768 | tf_op jit(solution)/shard_map/ppermute | solution.py:156
  51.2 0.9 collective-permute-start.12
  52.1 0.4 collective-permute-start.11
  52.5 0.5 collective-permute-done.13
  53.0 3.2 %collective-permute-done.12 = s16[64,640]{1,0:T(8,128)(2,1)S(1)} collective-permute-done((s16[64,640]{1,0:T(8,128)(2,1)}, s16[64,640]{1,0:T(8,128)(2,1)S(1)}, u32[]{:S(2)}, u32[]{:S(2)}) %collective-permute-start.12) | collective-permute-done | bytes 81952 | tf_op jit(solution)/shard_map/ppermute | solution.py:156
  56.3 0.8 collective-permute-done.11
  57.1 0.9 pad_add_fusion
  58.0 1.2 broadcast_in_dim.23
  59.3 3.5 %all-to-all-start.2 = ((s16[4,4,64,640]{3,2,1,0:T(8,128)(2,1)}), s16[4,4,64,640]{3,2,1,0:T(8,128)(2,1)S(1)}, u32[]{:S(2)}, u32[]{:S(2)}) async-start(s16[4,4,64,640]{3,2,1,0:T(8,128)(2,1)} %broadcast_in_dim.23), calls=%async_computation.2 | async-start | bytes 2621440 | tf_op jit(solution)/shard_map/all_to_all | solution.py:280
  62.8 3.5 %slot_codes.1.refs_1_ = bf16[128,8,128]{2,1,0:T(8,128)(2,1)} custom-call(s32[128,4,128]{2,1,0:T(4,128)} %bitcast.34, s32[128,128]{1,0:T(8,128)} %count_ref.1), custom_call_target="tpu_custom_call" | custom-call | flops 1048576 | bytes 1048576 | tf_op jit(solution)/shard_map/slot_codes/pallas_call | solution.py:52
  66.4 4.2 %pack.2 = bf16[128,88,128]{2,1,0:T(8,128)(2,1)} custom-call(bf16[128,128,128]{2,1,0:T(8,128)(2,1)} %refs_0_.3, bf16[128,8,128]{2,1,0:T(8,128)(2,1)} %slot_codes.1.refs_1_), custom_call_target="tpu_custom_call" | custom-call | flops 671088640 | bytes 4194304 | tf_op jit(solution)/shard_map/pack/pallas_call | solution.py:85
  70.5 7.5 %all-to-all-done.2.refs_0_ = s16[4,4,64,640]{3,2,1,0:T(8,128)(2,1)S(1)} async-done(((s16[4,4,64,640]{3,2,1,0:T(8,128)(2,1)}), s16[4,4,64,640]{3,2,1,0:T(8,128)(2,1)S(1)}, u32[]{:S(2)}, u32[]{:S(2)}) %all-to-all-start.2) | async-done | bytes 1310752 | tf_op jit(solution)/shard_map/all_to_all | solution.py:280
  78.0 1.1 copy-done.1
  79.1 8.0 %all-to-all-start = ((bf16[128,88,128]{2,1,0:T(8,128)(2,1)}), bf16[128,88,128]{2,1,0:T(8,128)(2,1)S(1)}, u32[]{:S(2)}, u32[]{:S(2)}) async-start(bf16[128,88,128]{2,1,0:T(8,128)(2,1)} %pack.2), calls=%async_computation | async-start | bytes 5767168 | tf_op jit(solution)/shard_map/all_to_all | solution.py:332
  87.1 3.2 %pack.3 = bf16[128,48,128]{2,1,0:T(8,128)(2,1)} custom-call(bf16[128,128,128]{2,1,0:T(8,128)(2,1)} %refs_0_.3), custom_call_target="tpu_custom_call" | custom-call | flops 402653184 | bytes 4194304 | tf_op jit(solution)/shard_map/pack/pallas_call | solution.py:85
  90.3 35.3 %all-to-all-done.info_ref.data_ref = bf16[128,88,128]{2,1,0:T(8,128)(2,1)S(1)} async-done(((bf16[128,88,128]{2,1,0:T(8,128)(2,1)}), bf16[128,88,128]{2,1,0:T(8,128)(2,1)S(1)}, u32[]{:S(2)}, u32[]{:S(2)}) %all-to-all-start) | async-done | bytes 2883616 | tf_op jit(solution)/shard_map/all_to_all | solution.py:332
  125.7 1.6 copy-done
  127.2 5.5 %all-to-all-start.1 = ((bf16[128,48,128]{2,1,0:T(8,128)(2,1)}), bf16[128,48,128]{2,1,0:T(8,128)(2,1)}, u32[]{:S(2)}, u32[]{:S(2)}) async-start(bf16[128,48,128]{2,1,0:T(8,128)(2,1)} %pack.3), calls=%async_computation.1 | async-start | bytes 3145728 | tf_op jit(solution)/shard_map/all_to_all | solution.py:332
  132.7 1.5 collective-permute-start.14
  134.3 14.3 %sum_by_row.3.refs_0_ = f32[2048,128]{1,0:T(8,128)} custom-call(s32[1]{0:T(128)} %constant.37.clone.1.base_ref, bf16[128,88,128]{2,1,0:T(8,128)(2,1)} %copy-done, bf16[128,88,128]{2,1,0:T(8,128)(2,1)} %copy-done), custom_call_target="tpu_custom_call" | custom-call | flops 5368709120 | bytes 3145728 | tf_op jit(solution)/shard_map/sum_by_row/pallas_call | solution.py:136
  148.6 8.2 %all-to-all-done.1.data_ref = bf16[128,48,128]{2,1,0:T(8,128)(2,1)} async-done(((bf16[128,48,128]{2,1,0:T(8,128)(2,1)}), bf16[128,48,128]{2,1,0:T(8,128)(2,1)}, u32[]{:S(2)}, u32[]{:S(2)}) %all-to-all-start.1) | async-done | bytes 1572896 | tf_op jit(solution)/shard_map/all_to_all | solution.py:332
  156.7 6.2 %sum_by_row.5 = f32[1024,128]{1,0:T(8,128)} custom-call(s32[1]{0:T(128)} %bitcast.4.base_ref, bf16[128,88,128]{2,1,0:T(8,128)(2,1)} %copy-done, bf16[128,48,128]{2,1,0:T(8,128)(2,1)} %all-to-all-done.1.data_ref, f32[2048,128]{1,0:T(8,128)} %sum_by_row.3.refs_0_), custom_call_target="tpu_custom_call" | custom-call | flops 1610612736 | bytes 3145728 | tf_op jit(solution)/shard_map/sum_by_row/pallas_call | solution.py:136
  162.9 0.8 collective-permute-start
  163.7 0.7 pad_add_fusion.1.at_ref
  164.3 6.2 %sum_by_row.4.grad_ref = f32[1024,128]{1,0:T(8,128)} custom-call(s32[1]{0:T(128)} %bitcast.2.base_ref, bf16[128,88,128]{2,1,0:T(8,128)(2,1)} %copy-done, bf16[128,48,128]{2,1,0:T(8,128)(2,1)} %all-to-all-done.1.data_ref, f32[2048,128]{1,0:T(8,128)} %sum_by_row.3.refs_0_), custom_call_target="tpu_custom_call" | custom-call | flops 1610612736 | bytes 3145728 | tf_op jit(solution)/shard_map/sum_by_row/pallas_call | solution.py:136
  170.5 2.6 %update.2 = (f32[2,1024,128]{2,1,0:T(8,128)}, f32[2,1024]{1,0:T(2,128)}) custom-call(s32[1]{0:T(128)} %bitcast.1.at_ref, f32[2,1024,128]{2,1,0:T(8,128)} %table_ref.3, f32[2,1024]{1,0:T(2,128)} %accum_ref.3, f32[2,1024]{1,0:T(2,128)} %accum_ref.3, f32[1024,128]{1,0:T(8,128)} %sum_by_row.4.grad_ref), custom_call_target="tpu_custom_call" | custom-call | flops 1048576 | bytes 2097152 | tf_op jit(solution)/shard_map/update/pallas_call | solution.py:303
  173.1 2.1 %collective-permute-done.grad_ref = f32[1024,128]{1,0:T(8,128)S(1)} collective-permute-done((f32[1024,128]{1,0:T(8,128)}, f32[1024,128]{1,0:T(8,128)S(1)}, u32[]{:S(2)}, u32[]{:S(2)}) %collective-permute-start) | collective-permute-done | bytes 524320 | tf_op jit(solution)/shard_map/ppermute | solution.py:341
  175.2 0.8 copy-done.4
  176.0 2.6 %update.3 = (f32[2,1024,128]{2,1,0:T(8,128)}, f32[2,1024]{1,0:T(2,128)}) custom-call(s32[1]{0:T(128)} %bitcast.at_ref, f32[2,1024,128]{2,1,0:T(8,128)} %table_ref.3, f32[2,1024]{1,0:T(2,128)} %accum_ref.3, f32[2,1024]{1,0:T(2,128)} %get-tuple-element.11.prior_ref, f32[1024,128]{1,0:T(8,128)} %copy-done.4, ...), custom_call_target="tpu_custom_call", output_to_operand_aliasing={{0}: (5, {})} | custom-call | flops 1048576 | bytes 2097152 | tf_op jit(solution)/shard_map/update/pallas_call | solution.py:303
  178.6 0.0 collective-permute-done.14.refs_1_
  178.6 1.1 copy-done.2
  179.7 4.2 %place.1 = f32[1024,1024]{1,0:T(8,128)} custom-call(s32[2]{0:T(128)} %pad_add_fusion.1.at_ref, s16[4,4,64,640]{3,2,1,0:T(8,128)(2,1)} %copy-done.1, s16[4,4,64,640]{3,2,1,0:T(8,128)(2,1)} %copy-done.2), custom_call_target="tpu_custom_call" | custom-call | flops 3145728 | bytes 8388608 | tf_op jit(solution)/shard_map/place/pallas_call | solution.py:227
  (11 shorter events, 0.2 us)
Async XLA Ops:
  2.7 9.1 %collective-permute-start.1 = (bf16[128,1024]{1,0:T(8,128)(2,1)}, bf16[128,1024]{1,0:T(8,128)(2,1)S(1)}, u32[]{:S(2)}, u32[]{:S(2)}) collective-permute-start(bf16[128,1024]{1,0:T(8,128)(2,1)} %get-tuple-element.16), channel_id=1, source_target_pairs={{0,8},{8,16},{16,24},{24,0},{1,9},{9,17},{17,25},{25,1},{2,10},{10... | collective-permute-start | bytes 786440 | tf_op jit(solution)/shard_map/ppermute | solution.py:156
  4.7 14.0 %collective-permute-start.2 = (bf16[128,1024]{1,0:T(8,128)(2,1)}, bf16[128,1024]{1,0:T(8,128)(2,1)S(1)}, u32[]{:S(2)}, u32[]{:S(2)}) collective-permute-start(bf16[128,1024]{1,0:T(8,128)(2,1)} %get-tuple-element.17), channel_id=1, source_target_pairs={{0,16},{8,24},{16,0},{24,8},{1,17},{9,25},{17,1},{25,9},{2,18},{10... | collective-permute-start | bytes 786440 | tf_op jit(solution)/shard_map/ppermute | solution.py:156
  7.2 11.6 %collective-permute-start.3 = (bf16[128,1024]{1,0:T(8,128)(2,1)}, bf16[128,1024]{1,0:T(8,128)(2,1)S(1)}, u32[]{:S(2)}, u32[]{:S(2)}) collective-permute-start(bf16[128,1024]{1,0:T(8,128)(2,1)} %get-tuple-element.18), channel_id=1, source_target_pairs={{0,24},{8,0},{16,8},{24,16},{1,25},{9,1},{17,9},{25,17},{2,26},{10... | collective-permute-start | bytes 786440 | tf_op jit(solution)/shard_map/ppermute | solution.py:156
  19.3 3.1 %collective-permute-start.4 = (f32[256,512]{1,0:T(8,128)S(1)}, f32[256,512]{1,0:T(8,128)S(1)}, u32[]{:S(2)}, u32[]{:S(2)}) collective-permute-start(f32[256,512]{1,0:T(8,128)S(1)} %dynamic-slice_bitcast_fusion), channel_id=1, source_target_pairs={{0,2},{2,0},{1,3},{3,1},{4,6},{6,4},{5,7},{7,5},{8,10},{10,8},{9,1... | collective-permute-start | bytes 1572872 | tf_op jit(solution)/shard_map/ppermute | solution.py:273
  22.6 8.0 %collective-permute-start.7 = (f32[64,512]{1,0:T(8,128)S(1)}, f32[64,512]{1,0:T(8,128)S(1)}, u32[]{:S(2)}, u32[]{:S(2)}) collective-permute-start(f32[64,512]{1,0:T(8,128)S(1)} %get-tuple-element.20), channel_id=1, source_target_pairs={{0,96},{32,0},{64,32},{96,64},{1,97},{33,1},{65,33},{97,65},{2,98}... | collective-permute-start | bytes 393224 | tf_op jit(solution)/shard_map/ppermute | solution.py:156
  25.4 5.9 %collective-permute-start.6 = (f32[64,512]{1,0:T(8,128)S(1)}, f32[64,512]{1,0:T(8,128)S(1)}, u32[]{:S(2)}, u32[]{:S(2)}) collective-permute-start(f32[64,512]{1,0:T(8,128)S(1)} %get-tuple-element.21), channel_id=1, source_target_pairs={{0,64},{32,96},{64,0},{96,32},{1,65},{33,97},{65,1},{97,33},{2,66}... | collective-permute-start | bytes 393224 | tf_op jit(solution)/shard_map/ppermute | solution.py:156
  25.7 9.4 %collective-permute-start.5 = (f32[64,512]{1,0:T(8,128)S(1)}, f32[64,512]{1,0:T(8,128)S(1)}, u32[]{:S(2)}, u32[]{:S(2)}) collective-permute-start(f32[64,512]{1,0:T(8,128)S(1)} %get-tuple-element.19), channel_id=1, source_target_pairs={{0,32},{32,64},{64,96},{96,0},{1,33},{33,65},{65,97},{97,1},{2,34}... | collective-permute-start | bytes 393224 | tf_op jit(solution)/shard_map/ppermute | solution.py:156
  35.2 10.9 %copy-start.3 = (f32[64,512]{1,0:T(8,128)}, f32[64,512]{1,0:T(8,128)S(1)}, u32[]{:S(2)}) copy-start(f32[64,512]{1,0:T(8,128)S(1)} %fusion.4.refs_0_) | copy-start | bytes 393220
  35.2 7.2 %collective-permute-start.8 = (f32[64,512]{1,0:T(8,128)S(1)}, f32[64,512]{1,0:T(8,128)S(1)}, u32[]{:S(2)}, u32[]{:S(2)}) collective-permute-start(f32[64,512]{1,0:T(8,128)S(1)} %fusion.4.refs_0_), channel_id=1, source_target_pairs={{0,1},{1,4},{4,5},{5,0},{2,3},{3,6},{6,7},{7,2},{8,9},{9,12},{12,1... | collective-permute-start | bytes 393224 | tf_op jit(solution)/shard_map/ppermute | solution.py:156
  36.9 9.2 %collective-permute-start.9 = (f32[64,512]{1,0:T(8,128)S(1)}, f32[64,512]{1,0:T(8,128)S(1)}, u32[]{:S(2)}, u32[]{:S(2)}) collective-permute-start(f32[64,512]{1,0:T(8,128)S(1)} %fusion.4.refs_0_), channel_id=1, source_target_pairs={{0,4},{1,5},{4,0},{5,1},{2,6},{3,7},{6,2},{7,3},{8,12},{9,13},{12,... | collective-permute-start | bytes 393224 | tf_op jit(solution)/shard_map/ppermute | solution.py:156
  40.2 5.9 %collective-permute-start.10 = (f32[64,512]{1,0:T(8,128)S(1)}, f32[64,512]{1,0:T(8,128)S(1)}, u32[]{:S(2)}, u32[]{:S(2)}) collective-permute-start(f32[64,512]{1,0:T(8,128)S(1)} %fusion.4.refs_0_), channel_id=1, source_target_pairs={{0,5},{1,0},{4,1},{5,4},{2,7},{3,2},{6,3},{7,6},{8,13},{9,8},{12,9... | collective-permute-start | bytes 393224 | tf_op jit(solution)/shard_map/ppermute | solution.py:156
  42.4 3.7 %copy-start.5 = (f32[64,512]{1,0:T(8,128)}, f32[64,512]{1,0:T(8,128)S(1)}, u32[]{:S(2)}) copy-start(f32[64,512]{1,0:T(8,128)S(1)} %collective-permute-done.8.refs_1_) | copy-start | bytes 393220
  46.1 0.7 copy-start.6
  46.8 0.7 copy-start.7
  49.3 3.7 %collective-permute-start.13 = (s16[64,640]{1,0:T(8,128)(2,1)}, s16[64,640]{1,0:T(8,128)(2,1)S(1)}, u32[]{:S(2)}, u32[]{:S(2)}) collective-permute-start(s16[64,640]{1,0:T(8,128)(2,1)} %code_sum.1), channel_id=1, source_target_pairs={{0,24},{8,0},{16,8},{24,16},{1,25},{9,1},{17,9},{25,17},{2,26},{10... | collective-permute-start | bytes 245768 | tf_op jit(solution)/shard_map/ppermute | solution.py:156
  51.2 5.0 %collective-permute-start.12 = (s16[64,640]{1,0:T(8,128)(2,1)}, s16[64,640]{1,0:T(8,128)(2,1)S(1)}, u32[]{:S(2)}, u32[]{:S(2)}) collective-permute-start(s16[64,640]{1,0:T(8,128)(2,1)} %code_sum.1), channel_id=1, source_target_pairs={{0,16},{8,24},{16,0},{24,8},{1,17},{9,25},{17,1},{25,9},{2,18},{10... | collective-permute-start | bytes 245768 | tf_op jit(solution)/shard_map/ppermute | solution.py:156
  52.1 5.0 %collective-permute-start.11 = (s16[64,640]{1,0:T(8,128)(2,1)}, s16[64,640]{1,0:T(8,128)(2,1)S(1)}, u32[]{:S(2)}, u32[]{:S(2)}) collective-permute-start(s16[64,640]{1,0:T(8,128)(2,1)} %code_sum.1), channel_id=1, source_target_pairs={{0,8},{8,16},{16,24},{24,0},{1,9},{9,17},{17,25},{25,1},{2,10},{10... | collective-permute-start | bytes 245768 | tf_op jit(solution)/shard_map/ppermute | solution.py:156
  59.3 18.7 %all-to-all-start.2 = ((s16[4,4,64,640]{3,2,1,0:T(8,128)(2,1)}), s16[4,4,64,640]{3,2,1,0:T(8,128)(2,1)S(1)}, u32[]{:S(2)}, u32[]{:S(2)}) async-start(s16[4,4,64,640]{3,2,1,0:T(8,128)(2,1)} %broadcast_in_dim.23), calls=%async_computation.2 | async-start | bytes 2621440 | tf_op jit(solution)/shard_map/all_to_all | solution.py:280
  78.0 1.1 copy-start.1
  79.1 46.6 %all-to-all-start = ((bf16[128,88,128]{2,1,0:T(8,128)(2,1)}), bf16[128,88,128]{2,1,0:T(8,128)(2,1)S(1)}, u32[]{:S(2)}, u32[]{:S(2)}) async-start(bf16[128,88,128]{2,1,0:T(8,128)(2,1)} %pack.2), calls=%async_computation | async-start | bytes 5767168 | tf_op jit(solution)/shard_map/all_to_all | solution.py:332
  125.7 1.6 copy-start
  127.2 29.5 %all-to-all-start.1 = ((bf16[128,48,128]{2,1,0:T(8,128)(2,1)}), bf16[128,48,128]{2,1,0:T(8,128)(2,1)}, u32[]{:S(2)}, u32[]{:S(2)}) async-start(bf16[128,48,128]{2,1,0:T(8,128)(2,1)} %pack.3), calls=%async_computation.1 | async-start | bytes 3145728 | tf_op jit(solution)/shard_map/all_to_all | solution.py:332
  132.7 45.9 %collective-permute-start.14 = (s16[4,4,64,640]{3,2,1,0:T(8,128)(2,1)}, s16[4,4,64,640]{3,2,1,0:T(8,128)(2,1)S(1)}, u32[]{:S(2)}, u32[]{:S(2)}) collective-permute-start(s16[4,4,64,640]{3,2,1,0:T(8,128)(2,1)} %copy-done.1), channel_id=1, source_target_pairs={{0,2},{2,0},{1,3},{3,1},{4,6},{6,4},{5,7},{7,5},{8,10},{10,8},{9,1... | collective-permute-start | bytes 3932168 | tf_op jit(solution)/shard_map/ppermute | solution.py:281
  162.9 12.3 %collective-permute-start = (f32[1024,128]{1,0:T(8,128)}, f32[1024,128]{1,0:T(8,128)S(1)}, u32[]{:S(2)}, u32[]{:S(2)}) collective-permute-start(f32[1024,128]{1,0:T(8,128)} %sum_by_row.5), channel_id=1, source_target_pairs={{0,1},{1,0},{2,3},{3,2},{4,5},{5,4},{6,7},{7,6},{8,9},{9,8},{10,11... | collective-permute-start | bytes 1572872 | tf_op jit(solution)/shard_map/ppermute | solution.py:341
  175.2 0.8 copy-start.4
  178.6 1.1 copy-start.2

commit v6 on v4

--- a/solution.py
+++ b/solution.py
@@ -21,27 +21,40 @@
     return jnp.where(row >= 1024, -size, size)
 
 
-def coded(row):
-    return sized(row).astype(f32).astype(bf16)
-
-
-def slot_codes(lengths, looked):
-    rows = jnp.transpose(looked, (1, 2, 0))
-    count = jnp.transpose(lengths, (1, 0))
-    slots = rows.shape[1]
-    active = [count > j for j in range(slots)]
-    row = [rows[:, j, :] for j in range(slots)]
-    codes, weights = [], []
+def codes_kernel(row_ref, count_ref, out_ref):
+    samples, slots, tables = row_ref.shape
+    row = [row_ref[:, j, :] for j in range(slots)]
+    active = [count_ref[...] > j for j in range(slots)]
+    kinds = []
     for j in range(slots):
         first = active[j]
         for i in range(j):
             first = first & (row[i] != row[j])
-        weight = jnp.ones_like(count)
+        kinds.append(jnp.where(first, sized(row[j]), 0))
+    for j in range(slots):
+        weight = jnp.ones_like(row[j])
         for i in range(j + 1, slots):
-            weight = weight + (active[i] & (row[i] == row[j])).astype(jnp.int32)
-        codes.append(jnp.where(first, coded(row[j]), jnp.zeros((), bf16)))
-        weights.append(weight.astype(f32).astype(bf16))
-    return jnp.stack(codes + weights, axis=1)
+            weight = weight + jnp.where(active[i] & (row[i] == row[j]), 1, 0)
+        kinds.append(weight)
+    kinds = [kind.astype(f32).T.astype(bf16) for kind in kinds]
+    size = 16 * len(kinds)
+    to = lax.broadcasted_iota(jnp.int32, (size, size), 0)
+    of = lax.broadcasted_iota(jnp.int32, (size, size), 1)
+    turn = jnp.where(((to & 7) == (of >> 4)) & ((to >> 3) == (of & 15)), 1.0, 0.0).astype(bf16)
+    for top in range(0, tables, 16):
+        block = jnp.concatenate([kind[top : top + 16, :] for kind in kinds], axis=0)
+        turned = jnp.dot(turn, block, preferred_element_type=f32)
+        out_ref[top : top + 16] = turned.reshape(16, len(kinds), samples).astype(bf16)
+
+
+def slot_codes(lengths, looked):
+    samples, tables, slots = looked.shape
+    return pl.pallas_call(
+        codes_kernel,
+        out_shape=jax.ShapeDtypeStruct((tables, 2 * slots, samples), bf16),
+        cost_estimate=pl.CostEstimate(flops=1 << 20, bytes_accessed=1 << 20, transcendentals=0),
+        name="slot_codes",
+    )(jnp.transpose(looked, (0, 2, 1)), lengths)
 
 
 def pack_kernel(*refs):
@@ -83,7 +96,7 @@
 
 
 cut = (0, 80, 128)
-group = 16
+group = 32
 stripe = 512
 
 
@@ -119,7 +132,7 @@
 def summed(part, first, data, base, rows, before=()):
     senders, _, width = data.shape
     samples = cut[part + 1] - cut[part]
-    step = 32
+    step = 64
     return pl.pallas_call(
         functools.partial(sum_kernel, part),
         grid_spec=pltpu.PrefetchScalarGridSpec(
@@ -176,6 +189,7 @@
         code_kernel,
         out_shape=jax.ShapeDtypeStruct((64, 640), jnp.int16),
         cost_estimate=pl.CostEstimate(flops=1 << 20, bytes_accessed=1 << 20, transcendentals=0),
+        compiler_params=pltpu.CompilerParams(vmem_limit_bytes=4 << 20),
         name="code_sum",
     )(*ranks)
 
@@ -215,6 +229,7 @@
             pltpu.SemaphoreType.DMA((2 * ring, ring)),
         ],
         cost_estimate=pl.CostEstimate(flops=3 << 20, bytes_accessed=8 << 20, transcendentals=0),
+        compiler_params=pltpu.CompilerParams(vmem_limit_bytes=12 << 20),
         name="place",
     )(at, *pieces)
 
@@ -294,6 +309,7 @@
         out_shape=[jax.ShapeDtypeStruct(table_rows.shape, f32), jax.ShapeDtypeStruct(row_accum.shape, f32)],
         input_output_aliases={5: 0} if before else {},
         cost_estimate=pl.CostEstimate(flops=1 << 20, bytes_accessed=2 << 20, transcendentals=0),
+        compiler_params=pltpu.CompilerParams(vmem_limit_bytes=8 << 20),
         name="update",
     )(at[None], table_rows, row_accum, prior, grad, *before)
 

time: 180 us -> 171 us (0.950)
  local copies, waits for them, and re-layouts: 13.5 us -> 7.57 us
  Pallas kernels: 49.2 us -> 46.4 us
    unnamed x35 -> x13, local copies, waits for them, and re-layouts: 10.1 us -> 6.08 us
    pallas_call x0 -> x1, Pallas kernels: none -> 3.54 us  [slot_codes(): pl.pallas_call(codes_kernel, out_shape=jax.ShapeDtypeStruct((tables, 2 *...]
    pallas_call x2, Pallas kernels: 5.1 us -> 2.64 us  [updated(): pl.pallas_call(update_kernel, grid_spec=pltpu.PrefetchScalarGridSpec(num_...]
    another operation x9 -> x0, local copies, waits for them, and re-layouts: 1.86 us -> none  [slot_codes(): return jnp.stack(codes + weights, axis=1)]
  transfers between devices with their start and end apart: 23 -> 23, of which waited for: 13 -> 14; matrix products, arithmetic and copies ran while one was open for 6% -> 6% of each run, Pallas kernels for 24% -> 22%
where the time goes in v6:
time: 171 us; the launch traced here: 170 us
  waiting for transfers between devices  65 us (38%)
  Pallas kernels  46.4 us (27%)
  starting transfers between devices  46.3 us (27%)
  local copies, waits for them, and re-layouts  7.57 us (4%)
  other arithmetic  2.46 us (1%)
    ppermute x15, waiting for transfers between devices, to_next(): lax.ppermute(value, axis, [(i, (i + step) % ring) for i in range(ring)])  63.2 us
    pallas_call x3, Pallas kernels, summed(): pl.pallas_call(functools.partial(sum_kernel, part), grid_spec=pltpu.Prefe...  26.9 us
    ppermute x15, starting transfers between devices, to_next(): lax.ppermute(value, axis, [(i, (i + step) % ring) for i in range(ring)])  20.8 us
    all_to_all x2, starting transfers between devices, exchanged(): return lax.all_to_all(value, every, split_axis=0, concat_axis=0, tiled=True)  18.8 us
    pallas_call x2, Pallas kernels, packed(): pl.pallas_call(pack_kernel, grid=(tables // 64,), in_specs=[pl.BlockSpec(...  7.39 us
    unnamed x13, local copies, waits for them, and re-layouts  6.08 us
    ppermute x4, starting transfers between devices, dense_sum(): theirs = [lax.ppermute(p, 'c', swap) for p in mine]  3.78 us
    pallas_call x1, Pallas kernels, placed(): pl.pallas_call(place_kernel, in_specs=[pl.BlockSpec(memory_space=pltpu.SM...  3.73 us
  transfers between devices with their start and end apart: 23, of which 14 were waited for; matrix products, arithmetic and copies ran while one was open for 6% of the time, Pallas kernels for 22%

profile of v6, /device:TPU:1, one launch (start us, length us, event | category | flops | bytes accessed | tf_op | source)
XLA Modules:
  0.0 170.2 jit_solution(192829819490727519)
XLA Ops:
  0.6 3.5 %slot_codes.1.refs_1_ = bf16[128,8,128]{2,1,0:T(8,128)(2,1)} custom-call(s32[128,4,128]{2,1,0:T(4,128)} %bitcast.35, s32[128,128]{1,0:T(8,128)} %count_ref.1), custom_call_target="tpu_custom_call" | custom-call | flops 1048576 | bytes 1048576 | tf_op jit(solution)/shard_map/slot_codes/pallas_call | solution.py:52
  4.2 4.2 %pack.2 = bf16[128,88,128]{2,1,0:T(8,128)(2,1)} custom-call(bf16[128,128,128]{2,1,0:T(8,128)(2,1)} %refs_0_.3, bf16[128,8,128]{2,1,0:T(8,128)(2,1)} %slot_codes.1.refs_1_), custom_call_target="tpu_custom_call" | custom-call | flops 671088640 | bytes 4194304 | tf_op jit(solution)/shard_map/pack/pallas_call | solution.py:85
  8.3 11.5 %all-to-all-start = ((bf16[128,88,128]{2,1,0:T(8,128)(2,1)}), bf16[128,88,128]{2,1,0:T(8,128)(2,1)S(1)}, u32[]{:S(2)}, u32[]{:S(2)}) async-start(bf16[128,88,128]{2,1,0:T(8,128)(2,1)} %pack.2), calls=%async_computation | async-start | bytes 5767168 | tf_op jit(solution)/shard_map/all_to_all | solution.py:325
  19.8 2.1 %share.1 = (bf16[128,1024]{1,0:T(8,128)(2,1)}, bf16[128,1024]{1,0:T(8,128)(2,1)}, bf16[128,1024]{1,0:T(8,128)(2,1)}, bf16[128,1024]{1,0:T(8,128)(2,1)}) custom-call(s32[1]{0:T(128)} %bitcast.6.at_ref, bf16[128,1024]{1,0:T(8,128)(2,1)} %left_ref.1, bf16[128,1024]{1,0:T(8,128)(2,1)} %right_ref.1), custom_call_target="tpu_custom_call" | custom-call | flops 524288 | bytes 2097152 | tf_op jit(solution)/shard_map/share/pallas_call | solution.py:245
  21.9 1.4 collective-permute-start.1
  23.3 2.4 %collective-permute-start.2 = (bf16[128,1024]{1,0:T(8,128)(2,1)}, bf16[128,1024]{1,0:T(8,128)(2,1)S(1)}, u32[]{:S(2)}, u32[]{:S(2)}) collective-permute-start(bf16[128,1024]{1,0:T(8,128)(2,1)} %get-tuple-element.17), channel_id=1, source_target_pairs={{0,16},{8,24},{16,0},{24,8},{1,17},{9,25},{17,1},{25,9},{2,18},{10... | collective-permute-start | bytes 786440 | tf_op jit(solution)/shard_map/ppermute | solution.py:156
  25.7 1.2 collective-permute-start.3
  26.9 1.7 constant_dynamic-update-slice_fusion.3
  28.5 30.7 %collective-permute-done.1 = bf16[128,1024]{1,0:T(8,128)(2,1)} collective-permute-done((bf16[128,1024]{1,0:T(8,128)(2,1)}, bf16[128,1024]{1,0:T(8,128)(2,1)}, u32[]{:S(2)}, u32[]{:S(2)}) %collective-permute-start.1) | collective-permute-done | bytes 262176 | tf_op jit(solution)/shard_map/ppermute | solution.py:156
  59.2 1.7 constant_dynamic-update-slice_fusion.2
  60.9 4.0 %collective-permute-done.2 = bf16[128,1024]{1,0:T(8,128)(2,1)S(1)} collective-permute-done((bf16[128,1024]{1,0:T(8,128)(2,1)}, bf16[128,1024]{1,0:T(8,128)(2,1)S(1)}, u32[]{:S(2)}, u32[]{:S(2)}) %collective-permute-start.2) | collective-permute-done | bytes 262176 | tf_op jit(solution)/shard_map/ppermute | solution.py:156
  64.8 0.7 constant_dynamic-update-slice_fusion.1
  65.6 0.0 collective-permute-done.3
  65.6 0.7 constant_dynamic-update-slice_fusion
  66.3 1.7 fusion
  67.9 0.0 copy-start.4
  68.0 1.0 copy-done.4
  69.0 1.1 collective-permute-start.4
  70.0 3.2 %pack.3 = bf16[128,48,128]{2,1,0:T(8,128)(2,1)} custom-call(bf16[128,128,128]{2,1,0:T(8,128)(2,1)} %refs_0_.3), custom_call_target="tpu_custom_call" | custom-call | flops 402653184 | bytes 4194304 | tf_op jit(solution)/shard_map/pack/pallas_call | solution.py:85
  73.2 0.0 all-to-all-done.info_ref.data_ref
  73.2 7.3 %all-to-all-start.1 = ((bf16[128,48,128]{2,1,0:T(8,128)(2,1)}), bf16[128,48,128]{2,1,0:T(8,128)(2,1)}, u32[]{:S(2)}, u32[]{:S(2)}) async-start(bf16[128,48,128]{2,1,0:T(8,128)(2,1)} %pack.3), calls=%async_computation.1 | async-start | bytes 3145728 | tf_op jit(solution)/shard_map/all_to_all | solution.py:325
  80.6 1.3 bitcast_add_fusion
  81.9 0.7 dynamic-slice_bitcast_fusion.3
  82.6 2.6 %collective-permute-start.7 = (f32[64,512]{1,0:T(8,128)}, f32[64,512]{1,0:T(8,128)}, u32[]{:S(2)}, u32[]{:S(2)}) collective-permute-start(f32[64,512]{1,0:T(8,128)} %get-tuple-element.20), channel_id=1, source_target_pairs={{0,96},{32,0},{64,32},{96,64},{1,97},{33,1},{65,33},{97,65},{2,98}... | collective-permute-start | bytes 393224 | tf_op jit(solution)/shard_map/ppermute | solution.py:156
  85.2 0.5 collective-permute-start.6
  85.7 0.6 collective-permute-start.5
  86.3 14.8 %collective-permute-done.7 = f32[64,512]{1,0:T(8,128)} collective-permute-done((f32[64,512]{1,0:T(8,128)}, f32[64,512]{1,0:T(8,128)}, u32[]{:S(2)}, u32[]{:S(2)}) %collective-permute-start.7) | collective-permute-done | bytes 131104 | tf_op jit(solution)/shard_map/ppermute | solution.py:156
  101.2 1.6 collective-permute-done.6
  102.8 2.9 %collective-permute-done.5 = f32[64,512]{1,0:T(8,128)} collective-permute-done((f32[64,512]{1,0:T(8,128)S(1)}, f32[64,512]{1,0:T(8,128)}, u32[]{:S(2)}, u32[]{:S(2)}) %collective-permute-start.5) | collective-permute-done | bytes 131104 | tf_op jit(solution)/shard_map/ppermute | solution.py:156
  105.7 1.1 fusion.4.refs_0_
  106.7 1.4 collective-permute-start.8
  108.1 3.2 %collective-permute-start.9 = (f32[64,512]{1,0:T(8,128)S(1)}, f32[64,512]{1,0:T(8,128)S(1)}, u32[]{:S(2)}, u32[]{:S(2)}) collective-permute-start(f32[64,512]{1,0:T(8,128)S(1)} %fusion.4.refs_0_), channel_id=1, source_target_pairs={{0,4},{1,5},{4,0},{5,1},{2,6},{3,7},{6,2},{7,3},{8,12},{9,13},{12,... | collective-permute-start | bytes 393224 | tf_op jit(solution)/shard_map/ppermute | solution.py:156
  111.3 0.8 collective-permute-start.10
  112.1 1.3 collective-permute-done.8.refs_1_
  113.3 3.7 %collective-permute-done.9.refs_2_ = f32[64,512]{1,0:T(8,128)S(1)} collective-permute-done((f32[64,512]{1,0:T(8,128)S(1)}, f32[64,512]{1,0:T(8,128)S(1)}, u32[]{:S(2)}, u32[]{:S(2)}) %collective-permute-start.9) | collective-permute-done | bytes 131104 | tf_op jit(solution)/shard_map/ppermute | solution.py:156
  117.0 0.2 code_sum.1
  117.2 2.1 %collective-permute-start.13 = (s16[64,640]{1,0:T(8,128)(2,1)S(1)}, s16[64,640]{1,0:T(8,128)(2,1)S(1)}, u32[]{:S(2)}, u32[]{:S(2)}) collective-permute-start(s16[64,640]{1,0:T(8,128)(2,1)S(1)} %code_sum.1), channel_id=1, source_target_pairs={{0,24},{8,0},{16,8},{24,16},{1,25},{9,1},{17,9},{25,17},{2,26},{10... | collective-permute-start | bytes 245768 | tf_op jit(solution)/shard_map/ppermute | solution.py:156
  119.3 0.7 collective-permute-start.12
  120.1 0.6 collective-permute-start.11
  120.7 0.1 collective-permute-done.13
  120.8 3.4 %collective-permute-done.12 = s16[64,640]{1,0:T(8,128)(2,1)S(1)} collective-permute-done((s16[64,640]{1,0:T(8,128)(2,1)S(1)}, s16[64,640]{1,0:T(8,128)(2,1)S(1)}, u32[]{:S(2)}, u32[]{:S(2)}) %collective-permute-start.12) | collective-permute-done | bytes 81952 | tf_op jit(solution)/shard_map/ppermute | solution.py:156
  124.2 0.8 collective-permute-done.11
  125.0 0.9 collective-permute-start.14
  125.9 1.7 collective-permute-start.15
  127.5 0.8 collective-permute-start.16
  128.4 14.3 %sum_by_row.3.refs_0_ = f32[2048,128]{1,0:T(8,128)} custom-call(s32[1]{0:T(128)} %constant.37.clone.1.base_ref, bf16[128,88,128]{2,1,0:T(8,128)(2,1)} %copy-done.3, bf16[128,88,128]{2,1,0:T(8,128)(2,1)} %copy-done.3), custom_call_target="tpu_custom_call" | custom-call | flops 5368709120 | bytes 3145728 | tf_op jit(solution)/shard_map/sum_by_row/pallas_call | solution.py:136
  142.7 6.2 %sum_by_row.5 = f32[1024,128]{1,0:T(8,128)} custom-call(s32[1]{0:T(128)} %bitcast.4.base_ref, bf16[128,88,128]{2,1,0:T(8,128)(2,1)} %copy-done.3, bf16[128,48,128]{2,1,0:T(8,128)(2,1)} %all-to-all-done.1.data_ref, f32[2048,128]{1,0:T(8,128)} %sum_by_row.3.refs_0_), custom_call_target="tpu_custom_call" | custom-call | flops 1610612736 | bytes 3145728 | tf_op jit(solution)/shard_map/sum_by_row/pallas_call | solution.py:136
  148.9 1.8 %collective-permute-start = (f32[1024,128]{1,0:T(8,128)}, f32[1024,128]{1,0:T(8,128)S(1)}, u32[]{:S(2)}, u32[]{:S(2)}) collective-permute-start(f32[1024,128]{1,0:T(8,128)} %sum_by_row.5), channel_id=1, source_target_pairs={{0,1},{1,0},{2,3},{3,2},{4,5},{5,4},{6,7},{7,6},{8,9},{9,8},{10,11... | collective-permute-start | bytes 1572872 | tf_op jit(solution)/shard_map/ppermute | solution.py:334
  150.8 3.0 %collective-permute-start.17 = (s16[4,64,640]{2,1,0:T(8,128)(2,1)S(1)}, s16[4,64,640]{2,1,0:T(8,128)(2,1)S(1)}, u32[]{:S(2)}, u32[]{:S(2)}) collective-permute-start(s16[4,64,640]{2,1,0:T(8,128)(2,1)S(1)} %pad_add_fusion.refs_0_), channel_id=1, source_target_pairs={{0,2},{2,0},{1,3},{3,1},{4,6},{6,4},{5,7},{7,5},{8,10},{10,8},{9,1... | collective-permute-start | bytes 983048 | tf_op jit(solution)/shard_map/ppermute | solution.py:273
  153.7 0.0 collective-permute-start.18
  153.7 0.5 collective-permute-start.19
  154.3 0.3 collective-permute-start.20
  154.6 0.1 pad_add_fusion.1.at_ref
  154.6 0.4 collective-permute-done.17.refs_4_
  155.0 0.5 collective-permute-done.18.refs_5_
  155.5 0.5 collective-permute-done.19.refs_6_
  155.9 0.5 collective-permute-done.20.refs_7_
  156.4 3.7 %place.1 = f32[1024,1024]{1,0:T(8,128)} custom-call(s32[3]{0:T(128)S(1)} %pad_add_fusion.1.at_ref, s16[4,64,640]{2,1,0:T(8,128)(2,1)S(1)} %pad_add_fusion.refs_0_, s16[4,64,640]{2,1,0:T(8,128)(2,1)S(1)} %collective-permute-done.14.refs_1_, s16[4,64,640]{2,1,0:T(8,128)(2,1)S(1)} %collective-permute-done.15.refs_2_, ...), custom_call_target="tpu_custom_call" | custom-call | flops 3145728 | bytes 8388608 | tf_op jit(solution)/shard_map/place/pallas_call | solution.py:222
  160.1 0.0 copy-start
  160.2 0.0 copy-start.2
  160.2 6.3 %sum_by_row.4.grad_ref = f32[1024,128]{1,0:T(8,128)} custom-call(s32[1]{0:T(128)} %bitcast.2.base_ref, bf16[128,88,128]{2,1,0:T(8,128)(2,1)} %copy-done.3, bf16[128,48,128]{2,1,0:T(8,128)(2,1)} %all-to-all-done.1.data_ref, f32[2048,128]{1,0:T(8,128)} %sum_by_row.3.refs_0_), custom_call_target="tpu_custom_call" | custom-call | flops 1610612736 | bytes 3145728 | tf_op jit(solution)/shard_map/sum_by_row/pallas_call | solution.py:136
  166.5 1.0 copy-done.1
  167.5 1.3 update.2
  168.9 1.3 update.3
  (14 shorter events, 0.1 us)
Async XLA Ops:
  8.3 64.9 %all-to-all-start = ((bf16[128,88,128]{2,1,0:T(8,128)(2,1)}), bf16[128,88,128]{2,1,0:T(8,128)(2,1)S(1)}, u32[]{:S(2)}, u32[]{:S(2)}) async-start(bf16[128,88,128]{2,1,0:T(8,128)(2,1)} %pack.2), calls=%async_computation | async-start | bytes 5767168 | tf_op jit(solution)/shard_map/all_to_all | solution.py:325
  21.9 37.3 %collective-permute-start.1 = (bf16[128,1024]{1,0:T(8,128)(2,1)}, bf16[128,1024]{1,0:T(8,128)(2,1)}, u32[]{:S(2)}, u32[]{:S(2)}) collective-permute-start(bf16[128,1024]{1,0:T(8,128)(2,1)} %get-tuple-element.16), channel_id=1, source_target_pairs={{0,8},{8,16},{16,24},{24,0},{1,9},{9,17},{17,25},{25,1},{2,10},{10... | collective-permute-start | bytes 786440 | tf_op jit(solution)/shard_map/ppermute | solution.py:156
  23.3 41.5 %collective-permute-start.2 = (bf16[128,1024]{1,0:T(8,128)(2,1)}, bf16[128,1024]{1,0:T(8,128)(2,1)S(1)}, u32[]{:S(2)}, u32[]{:S(2)}) collective-permute-start(bf16[128,1024]{1,0:T(8,128)(2,1)} %get-tuple-element.17), channel_id=1, source_target_pairs={{0,16},{8,24},{16,0},{24,8},{1,17},{9,25},{17,1},{25,9},{2,18},{10... | collective-permute-start | bytes 786440 | tf_op jit(solution)/shard_map/ppermute | solution.py:156
  25.7 39.9 %collective-permute-start.3 = (bf16[128,1024]{1,0:T(8,128)(2,1)}, bf16[128,1024]{1,0:T(8,128)(2,1)S(1)}, u32[]{:S(2)}, u32[]{:S(2)}) collective-permute-start(bf16[128,1024]{1,0:T(8,128)(2,1)} %get-tuple-element.18), channel_id=1, source_target_pairs={{0,24},{8,0},{16,8},{24,16},{1,25},{9,1},{17,9},{25,17},{2,26},{10... | collective-permute-start | bytes 786440 | tf_op jit(solution)/shard_map/ppermute | solution.py:156
  67.9 1.0 copy-start.4
  69.0 11.6 %collective-permute-start.4 = (f32[256,512]{1,0:T(8,128)S(1)}, f32[256,512]{1,0:T(8,128)}, u32[]{:S(2)}, u32[]{:S(2)}) collective-permute-start(f32[256,512]{1,0:T(8,128)S(1)} %dynamic-slice_bitcast_fusion), channel_id=1, source_target_pairs={{0,2},{2,0},{1,3},{3,1},{4,6},{6,4},{5,7},{7,5},{8,10},{10,8},{9,1... | collective-permute-start | bytes 1572872 | tf_op jit(solution)/shard_map/ppermute | solution.py:267
  73.2 33.5 %copy-start.3 = (bf16[128,88,128]{2,1,0:T(8,128)(2,1)}, bf16[128,88,128]{2,1,0:T(8,128)(2,1)S(1)}, u32[]{:S(2)}) copy-start(bf16[128,88,128]{2,1,0:T(8,128)(2,1)S(1)} %all-to-all-done.info_ref.data_ref) | copy-start | bytes 8650756
  73.2 69.5 %all-to-all-start.1 = ((bf16[128,48,128]{2,1,0:T(8,128)(2,1)}), bf16[128,48,128]{2,1,0:T(8,128)(2,1)}, u32[]{:S(2)}, u32[]{:S(2)}) async-start(bf16[128,48,128]{2,1,0:T(8,128)(2,1)} %pack.3), calls=%async_computation.1 | async-start | bytes 3145728 | tf_op jit(solution)/shard_map/all_to_all | solution.py:325
  82.6 18.6 %collective-permute-start.7 = (f32[64,512]{1,0:T(8,128)}, f32[64,512]{1,0:T(8,128)}, u32[]{:S(2)}, u32[]{:S(2)}) collective-permute-start(f32[64,512]{1,0:T(8,128)} %get-tuple-element.20), channel_id=1, source_target_pairs={{0,96},{32,0},{64,32},{96,64},{1,97},{33,1},{65,33},{97,65},{2,98}... | collective-permute-start | bytes 393224 | tf_op jit(solution)/shard_map/ppermute | solution.py:156
  85.2 17.6 %collective-permute-start.6 = (f32[64,512]{1,0:T(8,128)}, f32[64,512]{1,0:T(8,128)}, u32[]{:S(2)}, u32[]{:S(2)}) collective-permute-start(f32[64,512]{1,0:T(8,128)} %get-tuple-element.21), channel_id=1, source_target_pairs={{0,64},{32,96},{64,0},{96,32},{1,65},{33,97},{65,1},{97,33},{2,66}... | collective-permute-start | bytes 393224 | tf_op jit(solution)/shard_map/ppermute | solution.py:156
  85.7 19.9 %collective-permute-start.5 = (f32[64,512]{1,0:T(8,128)S(1)}, f32[64,512]{1,0:T(8,128)}, u32[]{:S(2)}, u32[]{:S(2)}) collective-permute-start(f32[64,512]{1,0:T(8,128)S(1)} %get-tuple-element.19), channel_id=1, source_target_pairs={{0,32},{32,64},{64,96},{96,0},{1,33},{33,65},{65,97},{97,1},{2,34}... | collective-permute-start | bytes 393224 | tf_op jit(solution)/shard_map/ppermute | solution.py:156
  106.7 6.6 %collective-permute-start.8 = (f32[64,512]{1,0:T(8,128)S(1)}, f32[64,512]{1,0:T(8,128)S(1)}, u32[]{:S(2)}, u32[]{:S(2)}) collective-permute-start(f32[64,512]{1,0:T(8,128)S(1)} %fusion.4.refs_0_), channel_id=1, source_target_pairs={{0,1},{1,4},{4,5},{5,0},{2,3},{3,6},{6,7},{7,2},{8,9},{9,12},{12,1... | collective-permute-start | bytes 393224 | tf_op jit(solution)/shard_map/ppermute | solution.py:156
  108.1 8.9 %collective-permute-start.9 = (f32[64,512]{1,0:T(8,128)S(1)}, f32[64,512]{1,0:T(8,128)S(1)}, u32[]{:S(2)}, u32[]{:S(2)}) collective-permute-start(f32[64,512]{1,0:T(8,128)S(1)} %fusion.4.refs_0_), channel_id=1, source_target_pairs={{0,4},{1,5},{4,0},{5,1},{2,6},{3,7},{6,2},{7,3},{8,12},{9,13},{12,... | collective-permute-start | bytes 393224 | tf_op jit(solution)/shard_map/ppermute | solution.py:156
  111.3 5.7 %collective-permute-start.10 = (f32[64,512]{1,0:T(8,128)S(1)}, f32[64,512]{1,0:T(8,128)S(1)}, u32[]{:S(2)}, u32[]{:S(2)}) collective-permute-start(f32[64,512]{1,0:T(8,128)S(1)} %fusion.4.refs_0_), channel_id=1, source_target_pairs={{0,5},{1,0},{4,1},{5,4},{2,7},{3,2},{6,3},{7,6},{8,13},{9,8},{12,9... | collective-permute-start | bytes 393224 | tf_op jit(solution)/shard_map/ppermute | solution.py:156
  117.2 3.6 %collective-permute-start.13 = (s16[64,640]{1,0:T(8,128)(2,1)S(1)}, s16[64,640]{1,0:T(8,128)(2,1)S(1)}, u32[]{:S(2)}, u32[]{:S(2)}) collective-permute-start(s16[64,640]{1,0:T(8,128)(2,1)S(1)} %code_sum.1), channel_id=1, source_target_pairs={{0,24},{8,0},{16,8},{24,16},{1,25},{9,1},{17,9},{25,17},{2,26},{10... | collective-permute-start | bytes 245768 | tf_op jit(solution)/shard_map/ppermute | solution.py:156
  119.3 4.8 %collective-permute-start.12 = (s16[64,640]{1,0:T(8,128)(2,1)S(1)}, s16[64,640]{1,0:T(8,128)(2,1)S(1)}, u32[]{:S(2)}, u32[]{:S(2)}) collective-permute-start(s16[64,640]{1,0:T(8,128)(2,1)S(1)} %code_sum.1), channel_id=1, source_target_pairs={{0,16},{8,24},{16,0},{24,8},{1,17},{9,25},{17,1},{25,9},{2,18},{10... | collective-permute-start | bytes 245768 | tf_op jit(solution)/shard_map/ppermute | solution.py:156
  120.1 4.9 %collective-permute-start.11 = (s16[64,640]{1,0:T(8,128)(2,1)S(1)}, s16[64,640]{1,0:T(8,128)(2,1)S(1)}, u32[]{:S(2)}, u32[]{:S(2)}) collective-permute-start(s16[64,640]{1,0:T(8,128)(2,1)S(1)} %code_sum.1), channel_id=1, source_target_pairs={{0,8},{8,16},{16,24},{24,0},{1,9},{9,17},{17,25},{25,1},{2,10},{10... | collective-permute-start | bytes 245768 | tf_op jit(solution)/shard_map/ppermute | solution.py:156
  125.0 28.7 %collective-permute-start.14 = (s16[4,64,640]{2,1,0:T(8,128)(2,1)S(1)}, s16[4,64,640]{2,1,0:T(8,128)(2,1)S(1)}, u32[]{:S(2)}, u32[]{:S(2)}) collective-permute-start(s16[4,64,640]{2,1,0:T(8,128)(2,1)S(1)} %pad_add_fusion.refs_0_), channel_id=1, source_target_pairs={{0,32},{32,64},{64,96},{96,0},{1,33},{33,65},{65,97},{97,1},{2,34}... | collective-permute-start | bytes 983048 | tf_op jit(solution)/shard_map/ppermute | solution.py:156
  125.9 27.9 %collective-permute-start.15 = (s16[4,64,640]{2,1,0:T(8,128)(2,1)S(1)}, s16[4,64,640]{2,1,0:T(8,128)(2,1)S(1)}, u32[]{:S(2)}, u32[]{:S(2)}) collective-permute-start(s16[4,64,640]{2,1,0:T(8,128)(2,1)S(1)} %pad_add_fusion.refs_0_), channel_id=1, source_target_pairs={{0,64},{32,96},{64,0},{96,32},{1,65},{33,97},{65,1},{97,33},{2,66}... | collective-permute-start | bytes 983048 | tf_op jit(solution)/shard_map/ppermute | solution.py:156
  127.5 26.7 %collective-permute-start.16 = (s16[4,64,640]{2,1,0:T(8,128)(2,1)S(1)}, s16[4,64,640]{2,1,0:T(8,128)(2,1)S(1)}, u32[]{:S(2)}, u32[]{:S(2)}) collective-permute-start(s16[4,64,640]{2,1,0:T(8,128)(2,1)S(1)} %pad_add_fusion.refs_0_), channel_id=1, source_target_pairs={{0,96},{32,0},{64,32},{96,64},{1,97},{33,1},{65,33},{97,65},{2,98}... | collective-permute-start | bytes 983048 | tf_op jit(solution)/shard_map/ppermute | solution.py:156
  148.9 19.9 %collective-permute-start = (f32[1024,128]{1,0:T(8,128)}, f32[1024,128]{1,0:T(8,128)S(1)}, u32[]{:S(2)}, u32[]{:S(2)}) collective-permute-start(f32[1024,128]{1,0:T(8,128)} %sum_by_row.5), channel_id=1, source_target_pairs={{0,1},{1,0},{2,3},{3,2},{4,5},{5,4},{6,7},{7,6},{8,9},{9,8},{10,11... | collective-permute-start | bytes 1572872 | tf_op jit(solution)/shard_map/ppermute | solution.py:334
  150.8 4.2 %collective-permute-start.17 = (s16[4,64,640]{2,1,0:T(8,128)(2,1)S(1)}, s16[4,64,640]{2,1,0:T(8,128)(2,1)S(1)}, u32[]{:S(2)}, u32[]{:S(2)}) collective-permute-start(s16[4,64,640]{2,1,0:T(8,128)(2,1)S(1)} %pad_add_fusion.refs_0_), channel_id=1, source_target_pairs={{0,2},{2,0},{1,3},{3,1},{4,6},{6,4},{5,7},{7,5},{8,10},{10,8},{9,1... | collective-permute-start | bytes 983048 | tf_op jit(solution)/shard_map/ppermute | solution.py:273
  153.7 1.7 %collective-permute-start.18 = (s16[4,64,640]{2,1,0:T(8,128)(2,1)S(1)}, s16[4,64,640]{2,1,0:T(8,128)(2,1)S(1)}, u32[]{:S(2)}, u32[]{:S(2)}) collective-permute-start(s16[4,64,640]{2,1,0:T(8,128)(2,1)S(1)} %collective-permute-done.14.refs_1_), channel_id=1, source_target_pairs={{0,2},{2,0},{1,3},{3,1},{4,6},{6,4},{5,7},{7,5},{8,10},{10,8},{9,1... | collective-permute-start | bytes 983048 | tf_op jit(solution)/shard_map/ppermute | solution.py:273
  153.7 2.2 %collective-permute-start.19 = (s16[4,64,640]{2,1,0:T(8,128)(2,1)S(1)}, s16[4,64,640]{2,1,0:T(8,128)(2,1)S(1)}, u32[]{:S(2)}, u32[]{:S(2)}) collective-permute-start(s16[4,64,640]{2,1,0:T(8,128)(2,1)S(1)} %collective-permute-done.15.refs_2_), channel_id=1, source_target_pairs={{0,2},{2,0},{1,3},{3,1},{4,6},{6,4},{5,7},{7,5},{8,10},{10,8},{9,1... | collective-permute-start | bytes 983048 | tf_op jit(solution)/shard_map/ppermute | solution.py:273
  154.3 2.1 %collective-permute-start.20 = (s16[4,64,640]{2,1,0:T(8,128)(2,1)S(1)}, s16[4,64,640]{2,1,0:T(8,128)(2,1)S(1)}, u32[]{:S(2)}, u32[]{:S(2)}) collective-permute-start(s16[4,64,640]{2,1,0:T(8,128)(2,1)S(1)} %collective-permute-done.16.refs_3_), channel_id=1, source_target_pairs={{0,2},{2,0},{1,3},{3,1},{4,6},{6,4},{5,7},{7,5},{8,10},{10,8},{9,1... | collective-permute-start | bytes 983048 | tf_op jit(solution)/shard_map/ppermute | solution.py:273
  160.1 6.3 %copy-start = (f32[2,1024,128]{2,1,0:T(8,128)S(1)}, f32[2,1024,128]{2,1,0:T(8,128)}, u32[]{:S(2)}) copy-start(f32[2,1024,128]{2,1,0:T(8,128)} %table_ref.3) | copy-start | bytes 3145732
  160.2 6.3 %copy-start.2 = (f32[2,1024]{1,0:T(2,128)S(1)}, f32[2,1024]{1,0:T(2,128)}, u32[]{:S(2)}) copy-start(f32[2,1024]{1,0:T(2,128)} %accum_ref.3) | copy-start | bytes 24580
  166.5 1.0 copy-start.1

commit v7 on v6

--- a/solution.py
+++ b/solution.py
@@ -21,7 +21,7 @@
     return jnp.where(row >= 1024, -size, size)
 
 
-def codes_kernel(row_ref, count_ref, out_ref):
+def slot_codes(row_ref, count_ref, out_ref):
     samples, slots, tables = row_ref.shape
     row = [row_ref[:, j, :] for j in range(slots)]
     active = [count_ref[...] > j for j in range(slots)]
@@ -47,52 +47,49 @@
         out_ref[top : top + 16] = turned.reshape(16, len(kinds), samples).astype(bf16)
 
 
-def slot_codes(lengths, looked):
-    samples, tables, slots = looked.shape
-    return pl.pallas_call(
-        codes_kernel,
-        out_shape=jax.ShapeDtypeStruct((tables, 2 * slots, samples), bf16),
-        cost_estimate=pl.CostEstimate(flops=1 << 20, bytes_accessed=1 << 20, transcendentals=0),
-        name="slot_codes",
-    )(jnp.transpose(looked, (0, 2, 1)), lengths)
-
-
-def pack_kernel(*refs):
-    grad_ref, out_ref, swap_ref = refs[0], refs[-2], refs[-1]
+def pack_kernel(grad_ref, *refs):
+    lookups = refs[:2] if len(refs) == 5 else ()
+    out_ref, swap_ref, *code_refs = refs[len(lookups) :]
     samples, tables, width = grad_ref.shape
-
-    @pl.when(pl.program_id(0) == 0)
+    at = pl.program_id(0)
+
+    @pl.when(at == 0)
     def _():
         to = lax.broadcasted_iota(jnp.int32, swap_ref.shape, 0)
         of = lax.broadcasted_iota(jnp.int32, swap_ref.shape, 1)
         hit = ((to & 15) == (of >> 4)) & ((to >> 4) == (of & 15))
         swap_ref[...] = jnp.where(hit, 1.0, 0.0).astype(bf16)
+        for code_ref in code_refs:
+            slot_codes(*lookups, code_ref)
 
     for first in range(0, samples, 16):
         for top in range(0, tables, 16):
             block = grad_ref[first : first + 16, top : top + 16].reshape(256, width)
             turned = jnp.dot(swap_ref[...], block, preferred_element_type=f32)
             out_ref[top : top + 16, first : first + 16, :] = turned.astype(bf16).reshape(16, 16, width)
-    if len(refs) == 4:
-        out_ref[:, samples : samples + 8, :] = refs[1][...]
-
-
-def packed(grads, part, codes=()):
+    for code_ref in code_refs:
+        out_ref[:, samples : samples + 8, :] = code_ref[pl.ds(pl.multiple_of(at * tables, tables), tables)]
+
+
+def packed(grads, part, lookups=()):
     start, stop = cut[part : part + 2]
-    _, tables, width = grads.shape
+    samples, tables, width = grads.shape
     count = stop - start
-    height = count + 8 * len(codes)
+    height = count + (8 if lookups else 0)
+    codes = [pltpu.VMEM((tables, 8, samples), bf16)] if lookups else []
     return pl.pallas_call(
         pack_kernel,
         grid=(tables // 64,),
-        in_specs=[pl.BlockSpec((pl.Element(count), pl.Element(64), pl.Element(width)), lambda i: (start, i * 64, 0))]
-        + [pl.BlockSpec((64, 8, width), lambda i: (i, 0, 0))] * len(codes),
+        in_specs=[
+            pl.BlockSpec((pl.Element(count), pl.Element(64), pl.Element(width)), lambda i: (start, i * 64, 0))
+        ]
+        + [pl.BlockSpec(a.shape, lambda i, n=a.ndim: (0,) * n) for a in lookups],
         out_specs=pl.BlockSpec((64, height, width), lambda i: (i, 0, 0)),
         out_shape=jax.ShapeDtypeStruct((tables, height, width), bf16),
-        scratch_shapes=[pltpu.VMEM((256, 256), bf16)],
+        scratch_shapes=[pltpu.VMEM((256, 256), bf16)] + codes,
         cost_estimate=pl.CostEstimate(flops=2 * 256 * count * tables * width, bytes_accessed=4 << 20, transcendentals=0),
         name="pack",
-    )(grads, *codes)
+    )(grads, *lookups)
 
 
 cut = (0, 80, 128)
@@ -319,12 +316,12 @@
 ):
     tables, rows = row_accum.shape
     dense_grad = dense_sum(dense_input, dense_cotangent)
-    codes = slot_codes(bag_lengths, bag_rows)
+    looked = jnp.transpose(bag_rows, (0, 2, 1))
 
     def exchanged(value):
         return lax.all_to_all(value, every, split_axis=0, concat_axis=0, tiled=True)
 
-    near = packed(pooled_grad, 0, (codes,))
+    near = packed(pooled_grad, 0, (looked, bag_lengths))
     late = packed(pooled_grad, 1)
     first = exchanged(near)
     second = exchanged(late)

time: 171 us -> 169 us (0.988)
    pallas_call x1 -> x0, Pallas kernels: 3.54 us -> none  [slot_codes(): pl.pallas_call(codes_kernel, out_shape=jax.ShapeDtypeStruct((tables, 2 *...]
    pallas_call x2, Pallas kernels: 7.39 us -> 9.33 us  [packed(): pl.pallas_call(pack_kernel, grid=(tables // 64,), in_specs=[pl.BlockSpec(...]
where the time goes in v7:
time: 169 us
  waiting for transfers between devices  65 us (38%)
  starting transfers between devices  46.3 us (27%)
  Pallas kernels  44.8 us (27%)
  local copies, waits for them, and re-layouts  7.57 us (4%)
  other arithmetic  2.46 us (1%)
    ppermute x15, waiting for transfers between devices, to_next(): lax.ppermute(value, axis, [(i, (i + step) % ring) for i in range(ring)])  63.2 us
    pallas_call x3, Pallas kernels, summed(): pl.pallas_call(functools.partial(sum_kernel, part), grid_spec=pltpu.Prefe...  26.9 us
    ppermute x15, starting transfers between devices, to_next(): lax.ppermute(value, axis, [(i, (i + step) % ring) for i in range(ring)])  20.8 us
    all_to_all x2, starting transfers between devices, exchanged(): return lax.all_to_all(value, every, split_axis=0, concat_axis=0, tiled=True)  18.8 us
    pallas_call x2, Pallas kernels, packed(): pl.pallas_call(pack_kernel, grid=(tables // 64,), in_specs=[pl.BlockSpec(...  9.33 us
    unnamed x13, local copies, waits for them, and re-layouts  6.08 us
    ppermute x4, starting transfers between devices, dense_sum(): theirs = [lax.ppermute(p, 'c', swap) for p in mine]  3.78 us
    pallas_call x1, Pallas kernels, placed(): pl.pallas_call(place_kernel, in_specs=[pl.BlockSpec(memory_space=pltpu.SM...  3.73 us
  transfers between devices with their start and end apart: 23, of which 14 were waited for; matrix products, arithmetic and copies ran while one was open for 6% of the time, Pallas kernels for 22%

profile of v7, /device:TPU:1, one launch (start us, length us, event | category | flops | bytes accessed | tf_op | source)
XLA Modules:
  0.0 168.6 jit_solution(8448026332297534400)
XLA Ops:
  0.6 6.1 %pack.2 = bf16[128,88,128]{2,1,0:T(8,128)(2,1)} custom-call(bf16[128,128,128]{2,1,0:T(8,128)(2,1)} %grad_ref.3, s32[128,4,128]{2,1,0:T(4,128)} %bitcast.35, s32[128,128]{1,0:T(8,128)} %refs_1_.1), custom_call_target="tpu_custom_call" | custom-call | flops 671088640 | bytes 4194304 | tf_op jit(solution)/shard_map/pack/pallas_call | solution.py:80
  6.7 11.5 %all-to-all-start = ((bf16[128,88,128]{2,1,0:T(8,128)(2,1)}), bf16[128,88,128]{2,1,0:T(8,128)(2,1)S(1)}, u32[]{:S(2)}, u32[]{:S(2)}) async-start(bf16[128,88,128]{2,1,0:T(8,128)(2,1)} %pack.2), calls=%async_computation | async-start | bytes 5767168 | tf_op jit(solution)/shard_map/all_to_all | solution.py:322
  18.2 2.1 %share.1 = (bf16[128,1024]{1,0:T(8,128)(2,1)}, bf16[128,1024]{1,0:T(8,128)(2,1)}, bf16[128,1024]{1,0:T(8,128)(2,1)}, bf16[128,1024]{1,0:T(8,128)(2,1)}) custom-call(s32[1]{0:T(128)} %bitcast.6.at_ref, bf16[128,1024]{1,0:T(8,128)(2,1)} %left_ref.1, bf16[128,1024]{1,0:T(8,128)(2,1)} %right_ref.1), custom_call_target="tpu_custom_call" | custom-call | flops 524288 | bytes 2097152 | tf_op jit(solution)/shard_map/share/pallas_call | solution.py:242
  20.3 1.4 collective-permute-start.1
  21.7 2.4 %collective-permute-start.2 = (bf16[128,1024]{1,0:T(8,128)(2,1)}, bf16[128,1024]{1,0:T(8,128)(2,1)S(1)}, u32[]{:S(2)}, u32[]{:S(2)}) collective-permute-start(bf16[128,1024]{1,0:T(8,128)(2,1)} %get-tuple-element.17), channel_id=1, source_target_pairs={{0,16},{8,24},{16,0},{24,8},{1,17},{9,25},{17,1},{25,9},{2,18},{10... | collective-permute-start | bytes 786440 | tf_op jit(solution)/shard_map/ppermute | solution.py:153
  24.1 1.2 collective-permute-start.3
  25.3 1.7 constant_dynamic-update-slice_fusion.3
  26.9 30.7 %collective-permute-done.1 = bf16[128,1024]{1,0:T(8,128)(2,1)} collective-permute-done((bf16[128,1024]{1,0:T(8,128)(2,1)}, bf16[128,1024]{1,0:T(8,128)(2,1)}, u32[]{:S(2)}, u32[]{:S(2)}) %collective-permute-start.1) | collective-permute-done | bytes 262176 | tf_op jit(solution)/shard_map/ppermute | solution.py:153
  57.6 1.7 constant_dynamic-update-slice_fusion.2
  59.3 4.0 %collective-permute-done.2 = bf16[128,1024]{1,0:T(8,128)(2,1)S(1)} collective-permute-done((bf16[128,1024]{1,0:T(8,128)(2,1)}, bf16[128,1024]{1,0:T(8,128)(2,1)S(1)}, u32[]{:S(2)}, u32[]{:S(2)}) %collective-permute-start.2) | collective-permute-done | bytes 262176 | tf_op jit(solution)/shard_map/ppermute | solution.py:153
  63.2 0.7 constant_dynamic-update-slice_fusion.1
  63.9 0.0 collective-permute-done.3
  64.0 0.7 constant_dynamic-update-slice_fusion
  64.7 1.7 fusion
  66.3 0.0 copy-start.4
  66.3 1.0 copy-done.4
  67.3 1.1 collective-permute-start.4
  68.4 3.2 %pack.3 = bf16[128,48,128]{2,1,0:T(8,128)(2,1)} custom-call(bf16[128,128,128]{2,1,0:T(8,128)(2,1)} %grad_ref.3), custom_call_target="tpu_custom_call" | custom-call | flops 402653184 | bytes 4194304 | tf_op jit(solution)/shard_map/pack/pallas_call | solution.py:80
  71.6 7.3 %all-to-all-start.1 = ((bf16[128,48,128]{2,1,0:T(8,128)(2,1)}), bf16[128,48,128]{2,1,0:T(8,128)(2,1)}, u32[]{:S(2)}, u32[]{:S(2)}) async-start(bf16[128,48,128]{2,1,0:T(8,128)(2,1)} %pack.3), calls=%async_computation.1 | async-start | bytes 3145728 | tf_op jit(solution)/shard_map/all_to_all | solution.py:322
  79.0 1.3 bitcast_add_fusion
  80.3 0.7 dynamic-slice_bitcast_fusion.3
  81.0 2.6 %collective-permute-start.7 = (f32[64,512]{1,0:T(8,128)}, f32[64,512]{1,0:T(8,128)}, u32[]{:S(2)}, u32[]{:S(2)}) collective-permute-start(f32[64,512]{1,0:T(8,128)} %get-tuple-element.20), channel_id=1, source_target_pairs={{0,96},{32,0},{64,32},{96,64},{1,97},{33,1},{65,33},{97,65},{2,98}... | collective-permute-start | bytes 393224 | tf_op jit(solution)/shard_map/ppermute | solution.py:153
  83.6 0.5 collective-permute-start.6
  84.1 0.6 collective-permute-start.5
  84.7 14.8 %collective-permute-done.7 = f32[64,512]{1,0:T(8,128)} collective-permute-done((f32[64,512]{1,0:T(8,128)}, f32[64,512]{1,0:T(8,128)}, u32[]{:S(2)}, u32[]{:S(2)}) %collective-permute-start.7) | collective-permute-done | bytes 131104 | tf_op jit(solution)/shard_map/ppermute | solution.py:153
  99.5 1.6 collective-permute-done.6
  101.2 2.9 %collective-permute-done.5 = f32[64,512]{1,0:T(8,128)} collective-permute-done((f32[64,512]{1,0:T(8,128)S(1)}, f32[64,512]{1,0:T(8,128)}, u32[]{:S(2)}, u32[]{:S(2)}) %collective-permute-start.5) | collective-permute-done | bytes 131104 | tf_op jit(solution)/shard_map/ppermute | solution.py:153
  104.1 1.1 fusion.4.refs_0_
  105.1 1.4 collective-permute-start.8
  106.5 3.2 %collective-permute-start.9 = (f32[64,512]{1,0:T(8,128)S(1)}, f32[64,512]{1,0:T(8,128)S(1)}, u32[]{:S(2)}, u32[]{:S(2)}) collective-permute-start(f32[64,512]{1,0:T(8,128)S(1)} %fusion.4.refs_0_), channel_id=1, source_target_pairs={{0,4},{1,5},{4,0},{5,1},{2,6},{3,7},{6,2},{7,3},{8,12},{9,13},{12,... | collective-permute-start | bytes 393224 | tf_op jit(solution)/shard_map/ppermute | solution.py:153
  109.7 0.8 collective-permute-start.10
  110.5 1.3 collective-permute-done.8.refs_1_
  111.7 3.7 %collective-permute-done.9.refs_2_ = f32[64,512]{1,0:T(8,128)S(1)} collective-permute-done((f32[64,512]{1,0:T(8,128)S(1)}, f32[64,512]{1,0:T(8,128)S(1)}, u32[]{:S(2)}, u32[]{:S(2)}) %collective-permute-start.9) | collective-permute-done | bytes 131104 | tf_op jit(solution)/shard_map/ppermute | solution.py:153
  115.4 0.0 collective-permute-done.10.refs_3_
  115.4 0.2 code_sum.1
  115.6 2.1 %collective-permute-start.13 = (s16[64,640]{1,0:T(8,128)(2,1)S(1)}, s16[64,640]{1,0:T(8,128)(2,1)S(1)}, u32[]{:S(2)}, u32[]{:S(2)}) collective-permute-start(s16[64,640]{1,0:T(8,128)(2,1)S(1)} %code_sum.1), channel_id=1, source_target_pairs={{0,24},{8,0},{16,8},{24,16},{1,25},{9,1},{17,9},{25,17},{2,26},{10... | collective-permute-start | bytes 245768 | tf_op jit(solution)/shard_map/ppermute | solution.py:153
  117.7 0.7 collective-permute-start.12
  118.5 0.6 collective-permute-start.11
  119.1 0.1 collective-permute-done.13
  119.2 3.4 %collective-permute-done.12 = s16[64,640]{1,0:T(8,128)(2,1)S(1)} collective-permute-done((s16[64,640]{1,0:T(8,128)(2,1)S(1)}, s16[64,640]{1,0:T(8,128)(2,1)S(1)}, u32[]{:S(2)}, u32[]{:S(2)}) %collective-permute-start.12) | collective-permute-done | bytes 81952 | tf_op jit(solution)/shard_map/ppermute | solution.py:153
  122.6 0.8 collective-permute-done.11
  123.4 0.9 collective-permute-start.14
  124.3 1.7 collective-permute-start.15
  125.9 0.8 collective-permute-start.16
  126.8 14.3 %sum_by_row.3.refs_0_ = f32[2048,128]{1,0:T(8,128)} custom-call(s32[1]{0:T(128)} %constant.37.clone.1.base_ref, bf16[128,88,128]{2,1,0:T(8,128)(2,1)} %copy-done.3, bf16[128,88,128]{2,1,0:T(8,128)(2,1)} %copy-done.3), custom_call_target="tpu_custom_call" | custom-call | flops 5368709120 | bytes 3145728 | tf_op jit(solution)/shard_map/sum_by_row/pallas_call | solution.py:133
  141.1 6.2 %sum_by_row.5 = f32[1024,128]{1,0:T(8,128)} custom-call(s32[1]{0:T(128)} %bitcast.4.base_ref, bf16[128,88,128]{2,1,0:T(8,128)(2,1)} %copy-done.3, bf16[128,48,128]{2,1,0:T(8,128)(2,1)} %all-to-all-done.1.data_ref, f32[2048,128]{1,0:T(8,128)} %sum_by_row.3.refs_0_), custom_call_target="tpu_custom_call" | custom-call | flops 1610612736 | bytes 3145728 | tf_op jit(solution)/shard_map/sum_by_row/pallas_call | solution.py:133
  147.3 1.8 %collective-permute-start = (f32[1024,128]{1,0:T(8,128)}, f32[1024,128]{1,0:T(8,128)S(1)}, u32[]{:S(2)}, u32[]{:S(2)}) collective-permute-start(f32[1024,128]{1,0:T(8,128)} %sum_by_row.5), channel_id=1, source_target_pairs={{0,1},{1,0},{2,3},{3,2},{4,5},{5,4},{6,7},{7,6},{8,9},{9,8},{10,11... | collective-permute-start | bytes 1572872 | tf_op jit(solution)/shard_map/ppermute | solution.py:331
  149.2 3.0 %collective-permute-start.17 = (s16[4,64,640]{2,1,0:T(8,128)(2,1)S(1)}, s16[4,64,640]{2,1,0:T(8,128)(2,1)S(1)}, u32[]{:S(2)}, u32[]{:S(2)}) collective-permute-start(s16[4,64,640]{2,1,0:T(8,128)(2,1)S(1)} %pad_add_fusion.refs_0_), channel_id=1, source_target_pairs={{0,2},{2,0},{1,3},{3,1},{4,6},{6,4},{5,7},{7,5},{8,10},{10,8},{9,1... | collective-permute-start | bytes 983048 | tf_op jit(solution)/shard_map/ppermute | solution.py:270
  152.1 0.0 collective-permute-done.14.refs_1_
  152.1 0.0 collective-permute-start.18
  152.1 0.5 collective-permute-start.19
  152.6 0.3 collective-permute-start.20
  153.0 0.1 pad_add_fusion.1.at_ref
  153.0 0.4 collective-permute-done.17.refs_4_
  153.4 0.5 collective-permute-done.18.refs_5_
  153.9 0.5 collective-permute-done.19.refs_6_
  154.3 0.5 collective-permute-done.20.refs_7_
  154.8 3.7 %place.1 = f32[1024,1024]{1,0:T(8,128)} custom-call(s32[3]{0:T(128)S(1)} %pad_add_fusion.1.at_ref, s16[4,64,640]{2,1,0:T(8,128)(2,1)S(1)} %pad_add_fusion.refs_0_, s16[4,64,640]{2,1,0:T(8,128)(2,1)S(1)} %collective-permute-done.14.refs_1_, s16[4,64,640]{2,1,0:T(8,128)(2,1)S(1)} %collective-permute-done.15.refs_2_, ...), custom_call_target="tpu_custom_call" | custom-call | flops 3145728 | bytes 8388608 | tf_op jit(solution)/shard_map/place/pallas_call | solution.py:219
  158.5 0.0 copy-start
  158.5 0.0 copy-start.2
  158.6 6.3 %sum_by_row.4.grad_ref = f32[1024,128]{1,0:T(8,128)} custom-call(s32[1]{0:T(128)} %bitcast.2.base_ref, bf16[128,88,128]{2,1,0:T(8,128)(2,1)} %copy-done.3, bf16[128,48,128]{2,1,0:T(8,128)(2,1)} %all-to-all-done.1.data_ref, f32[2048,128]{1,0:T(8,128)} %sum_by_row.3.refs_0_), custom_call_target="tpu_custom_call" | custom-call | flops 1610612736 | bytes 3145728 | tf_op jit(solution)/shard_map/sum_by_row/pallas_call | solution.py:133
  164.9 1.0 copy-done.1
  165.9 1.3 update.2
  167.2 1.3 update.3
  (13 shorter events, 0.1 us)
Async XLA Ops:
  6.7 64.9 %all-to-all-start = ((bf16[128,88,128]{2,1,0:T(8,128)(2,1)}), bf16[128,88,128]{2,1,0:T(8,128)(2,1)S(1)}, u32[]{:S(2)}, u32[]{:S(2)}) async-start(bf16[128,88,128]{2,1,0:T(8,128)(2,1)} %pack.2), calls=%async_computation | async-start | bytes 5767168 | tf_op jit(solution)/shard_map/all_to_all | solution.py:322
  20.3 37.3 %collective-permute-start.1 = (bf16[128,1024]{1,0:T(8,128)(2,1)}, bf16[128,1024]{1,0:T(8,128)(2,1)}, u32[]{:S(2)}, u32[]{:S(2)}) collective-permute-start(bf16[128,1024]{1,0:T(8,128)(2,1)} %get-tuple-element.16), channel_id=1, source_target_pairs={{0,8},{8,16},{16,24},{24,0},{1,9},{9,17},{17,25},{25,1},{2,10},{10... | collective-permute-start | bytes 786440 | tf_op jit(solution)/shard_map/ppermute | solution.py:153
  21.7 41.5 %collective-permute-start.2 = (bf16[128,1024]{1,0:T(8,128)(2,1)}, bf16[128,1024]{1,0:T(8,128)(2,1)S(1)}, u32[]{:S(2)}, u32[]{:S(2)}) collective-permute-start(bf16[128,1024]{1,0:T(8,128)(2,1)} %get-tuple-element.17), channel_id=1, source_target_pairs={{0,16},{8,24},{16,0},{24,8},{1,17},{9,25},{17,1},{25,9},{2,18},{10... | collective-permute-start | bytes 786440 | tf_op jit(solution)/shard_map/ppermute | solution.py:153
  24.1 39.9 %collective-permute-start.3 = (bf16[128,1024]{1,0:T(8,128)(2,1)}, bf16[128,1024]{1,0:T(8,128)(2,1)S(1)}, u32[]{:S(2)}, u32[]{:S(2)}) collective-permute-start(bf16[128,1024]{1,0:T(8,128)(2,1)} %get-tuple-element.18), channel_id=1, source_target_pairs={{0,24},{8,0},{16,8},{24,16},{1,25},{9,1},{17,9},{25,17},{2,26},{10... | collective-permute-start | bytes 786440 | tf_op jit(solution)/shard_map/ppermute | solution.py:153
  66.3 1.0 copy-start.4
  67.3 11.6 %collective-permute-start.4 = (f32[256,512]{1,0:T(8,128)S(1)}, f32[256,512]{1,0:T(8,128)}, u32[]{:S(2)}, u32[]{:S(2)}) collective-permute-start(f32[256,512]{1,0:T(8,128)S(1)} %dynamic-slice_bitcast_fusion), channel_id=1, source_target_pairs={{0,2},{2,0},{1,3},{3,1},{4,6},{6,4},{5,7},{7,5},{8,10},{10,8},{9,1... | collective-permute-start | bytes 1572872 | tf_op jit(solution)/shard_map/ppermute | solution.py:264
  71.6 33.5 %copy-start.3 = (bf16[128,88,128]{2,1,0:T(8,128)(2,1)}, bf16[128,88,128]{2,1,0:T(8,128)(2,1)S(1)}, u32[]{:S(2)}) copy-start(bf16[128,88,128]{2,1,0:T(8,128)(2,1)S(1)} %all-to-all-done.info_ref.data_ref) | copy-start | bytes 8650756
  71.6 69.5 %all-to-all-start.1 = ((bf16[128,48,128]{2,1,0:T(8,128)(2,1)}), bf16[128,48,128]{2,1,0:T(8,128)(2,1)}, u32[]{:S(2)}, u32[]{:S(2)}) async-start(bf16[128,48,128]{2,1,0:T(8,128)(2,1)} %pack.3), calls=%async_computation.1 | async-start | bytes 3145728 | tf_op jit(solution)/shard_map/all_to_all | solution.py:322
  81.0 18.6 %collective-permute-start.7 = (f32[64,512]{1,0:T(8,128)}, f32[64,512]{1,0:T(8,128)}, u32[]{:S(2)}, u32[]{:S(2)}) collective-permute-start(f32[64,512]{1,0:T(8,128)} %get-tuple-element.20), channel_id=1, source_target_pairs={{0,96},{32,0},{64,32},{96,64},{1,97},{33,1},{65,33},{97,65},{2,98}... | collective-permute-start | bytes 393224 | tf_op jit(solution)/shard_map/ppermute | solution.py:153
  83.6 17.6 %collective-permute-start.6 = (f32[64,512]{1,0:T(8,128)}, f32[64,512]{1,0:T(8,128)}, u32[]{:S(2)}, u32[]{:S(2)}) collective-permute-start(f32[64,512]{1,0:T(8,128)} %get-tuple-element.21), channel_id=1, source_target_pairs={{0,64},{32,96},{64,0},{96,32},{1,65},{33,97},{65,1},{97,33},{2,66}... | collective-permute-start | bytes 393224 | tf_op jit(solution)/shard_map/ppermute | solution.py:153
  84.1 19.9 %collective-permute-start.5 = (f32[64,512]{1,0:T(8,128)S(1)}, f32[64,512]{1,0:T(8,128)}, u32[]{:S(2)}, u32[]{:S(2)}) collective-permute-start(f32[64,512]{1,0:T(8,128)S(1)} %get-tuple-element.19), channel_id=1, source_target_pairs={{0,32},{32,64},{64,96},{96,0},{1,33},{33,65},{65,97},{97,1},{2,34}... | collective-permute-start | bytes 393224 | tf_op jit(solution)/shard_map/ppermute | solution.py:153
  105.1 6.6 %collective-permute-start.8 = (f32[64,512]{1,0:T(8,128)S(1)}, f32[64,512]{1,0:T(8,128)S(1)}, u32[]{:S(2)}, u32[]{:S(2)}) collective-permute-start(f32[64,512]{1,0:T(8,128)S(1)} %fusion.4.refs_0_), channel_id=1, source_target_pairs={{0,1},{1,4},{4,5},{5,0},{2,3},{3,6},{6,7},{7,2},{8,9},{9,12},{12,1... | collective-permute-start | bytes 393224 | tf_op jit(solution)/shard_map/ppermute | solution.py:153
  106.5 8.9 %collective-permute-start.9 = (f32[64,512]{1,0:T(8,128)S(1)}, f32[64,512]{1,0:T(8,128)S(1)}, u32[]{:S(2)}, u32[]{:S(2)}) collective-permute-start(f32[64,512]{1,0:T(8,128)S(1)} %fusion.4.refs_0_), channel_id=1, source_target_pairs={{0,4},{1,5},{4,0},{5,1},{2,6},{3,7},{6,2},{7,3},{8,12},{9,13},{12,... | collective-permute-start | bytes 393224 | tf_op jit(solution)/shard_map/ppermute | solution.py:153
  109.7 5.7 %collective-permute-start.10 = (f32[64,512]{1,0:T(8,128)S(1)}, f32[64,512]{1,0:T(8,128)S(1)}, u32[]{:S(2)}, u32[]{:S(2)}) collective-permute-start(f32[64,512]{1,0:T(8,128)S(1)} %fusion.4.refs_0_), channel_id=1, source_target_pairs={{0,5},{1,0},{4,1},{5,4},{2,7},{3,2},{6,3},{7,6},{8,13},{9,8},{12,9... | collective-permute-start | bytes 393224 | tf_op jit(solution)/shard_map/ppermute | solution.py:153
  115.6 3.6 %collective-permute-start.13 = (s16[64,640]{1,0:T(8,128)(2,1)S(1)}, s16[64,640]{1,0:T(8,128)(2,1)S(1)}, u32[]{:S(2)}, u32[]{:S(2)}) collective-permute-start(s16[64,640]{1,0:T(8,128)(2,1)S(1)} %code_sum.1), channel_id=1, source_target_pairs={{0,24},{8,0},{16,8},{24,16},{1,25},{9,1},{17,9},{25,17},{2,26},{10... | collective-permute-start | bytes 245768 | tf_op jit(solution)/shard_map/ppermute | solution.py:153
  117.7 4.8 %collective-permute-start.12 = (s16[64,640]{1,0:T(8,128)(2,1)S(1)}, s16[64,640]{1,0:T(8,128)(2,1)S(1)}, u32[]{:S(2)}, u32[]{:S(2)}) collective-permute-start(s16[64,640]{1,0:T(8,128)(2,1)S(1)} %code_sum.1), channel_id=1, source_target_pairs={{0,16},{8,24},{16,0},{24,8},{1,17},{9,25},{17,1},{25,9},{2,18},{10... | collective-permute-start | bytes 245768 | tf_op jit(solution)/shard_map/ppermute | solution.py:153
  118.5 4.9 %collective-permute-start.11 = (s16[64,640]{1,0:T(8,128)(2,1)S(1)}, s16[64,640]{1,0:T(8,128)(2,1)S(1)}, u32[]{:S(2)}, u32[]{:S(2)}) collective-permute-start(s16[64,640]{1,0:T(8,128)(2,1)S(1)} %code_sum.1), channel_id=1, source_target_pairs={{0,8},{8,16},{16,24},{24,0},{1,9},{9,17},{17,25},{25,1},{2,10},{10... | collective-permute-start | bytes 245768 | tf_op jit(solution)/shard_map/ppermute | solution.py:153
  123.4 28.7 %collective-permute-start.14 = (s16[4,64,640]{2,1,0:T(8,128)(2,1)S(1)}, s16[4,64,640]{2,1,0:T(8,128)(2,1)S(1)}, u32[]{:S(2)}, u32[]{:S(2)}) collective-permute-start(s16[4,64,640]{2,1,0:T(8,128)(2,1)S(1)} %pad_add_fusion.refs_0_), channel_id=1, source_target_pairs={{0,32},{32,64},{64,96},{96,0},{1,33},{33,65},{65,97},{97,1},{2,34}... | collective-permute-start | bytes 983048 | tf_op jit(solution)/shard_map/ppermute | solution.py:153
  124.3 27.9 %collective-permute-start.15 = (s16[4,64,640]{2,1,0:T(8,128)(2,1)S(1)}, s16[4,64,640]{2,1,0:T(8,128)(2,1)S(1)}, u32[]{:S(2)}, u32[]{:S(2)}) collective-permute-start(s16[4,64,640]{2,1,0:T(8,128)(2,1)S(1)} %pad_add_fusion.refs_0_), channel_id=1, source_target_pairs={{0,64},{32,96},{64,0},{96,32},{1,65},{33,97},{65,1},{97,33},{2,66}... | collective-permute-start | bytes 983048 | tf_op jit(solution)/shard_map/ppermute | solution.py:153
  125.9 26.7 %collective-permute-start.16 = (s16[4,64,640]{2,1,0:T(8,128)(2,1)S(1)}, s16[4,64,640]{2,1,0:T(8,128)(2,1)S(1)}, u32[]{:S(2)}, u32[]{:S(2)}) collective-permute-start(s16[4,64,640]{2,1,0:T(8,128)(2,1)S(1)} %pad_add_fusion.refs_0_), channel_id=1, source_target_pairs={{0,96},{32,0},{64,32},{96,64},{1,97},{33,1},{65,33},{97,65},{2,98}... | collective-permute-start | bytes 983048 | tf_op jit(solution)/shard_map/ppermute | solution.py:153
  147.3 19.9 %collective-permute-start = (f32[1024,128]{1,0:T(8,128)}, f32[1024,128]{1,0:T(8,128)S(1)}, u32[]{:S(2)}, u32[]{:S(2)}) collective-permute-start(f32[1024,128]{1,0:T(8,128)} %sum_by_row.5), channel_id=1, source_target_pairs={{0,1},{1,0},{2,3},{3,2},{4,5},{5,4},{6,7},{7,6},{8,9},{9,8},{10,11... | collective-permute-start | bytes 1572872 | tf_op jit(solution)/shard_map/ppermute | solution.py:331
  149.2 4.2 %collective-permute-start.17 = (s16[4,64,640]{2,1,0:T(8,128)(2,1)S(1)}, s16[4,64,640]{2,1,0:T(8,128)(2,1)S(1)}, u32[]{:S(2)}, u32[]{:S(2)}) collective-permute-start(s16[4,64,640]{2,1,0:T(8,128)(2,1)S(1)} %pad_add_fusion.refs_0_), channel_id=1, source_target_pairs={{0,2},{2,0},{1,3},{3,1},{4,6},{6,4},{5,7},{7,5},{8,10},{10,8},{9,1... | collective-permute-start | bytes 983048 | tf_op jit(solution)/shard_map/ppermute | solution.py:270
  152.1 1.7 %collective-permute-start.18 = (s16[4,64,640]{2,1,0:T(8,128)(2,1)S(1)}, s16[4,64,640]{2,1,0:T(8,128)(2,1)S(1)}, u32[]{:S(2)}, u32[]{:S(2)}) collective-permute-start(s16[4,64,640]{2,1,0:T(8,128)(2,1)S(1)} %collective-permute-done.14.refs_1_), channel_id=1, source_target_pairs={{0,2},{2,0},{1,3},{3,1},{4,6},{6,4},{5,7},{7,5},{8,10},{10,8},{9,1... | collective-permute-start | bytes 983048 | tf_op jit(solution)/shard_map/ppermute | solution.py:270
  152.1 2.2 %collective-permute-start.19 = (s16[4,64,640]{2,1,0:T(8,128)(2,1)S(1)}, s16[4,64,640]{2,1,0:T(8,128)(2,1)S(1)}, u32[]{:S(2)}, u32[]{:S(2)}) collective-permute-start(s16[4,64,640]{2,1,0:T(8,128)(2,1)S(1)} %collective-permute-done.15.refs_2_), channel_id=1, source_target_pairs={{0,2},{2,0},{1,3},{3,1},{4,6},{6,4},{5,7},{7,5},{8,10},{10,8},{9,1... | collective-permute-start | bytes 983048 | tf_op jit(solution)/shard_map/ppermute | solution.py:270
  152.6 2.1 %collective-permute-start.20 = (s16[4,64,640]{2,1,0:T(8,128)(2,1)S(1)}, s16[4,64,640]{2,1,0:T(8,128)(2,1)S(1)}, u32[]{:S(2)}, u32[]{:S(2)}) collective-permute-start(s16[4,64,640]{2,1,0:T(8,128)(2,1)S(1)} %collective-permute-done.16.refs_3_), channel_id=1, source_target_pairs={{0,2},{2,0},{1,3},{3,1},{4,6},{6,4},{5,7},{7,5},{8,10},{10,8},{9,1... | collective-permute-start | bytes 983048 | tf_op jit(solution)/shard_map/ppermute | solution.py:270
  158.5 6.3 %copy-start = (f32[2,1024,128]{2,1,0:T(8,128)S(1)}, f32[2,1024,128]{2,1,0:T(8,128)}, u32[]{:S(2)}) copy-start(f32[2,1024,128]{2,1,0:T(8,128)} %table_ref.3) | copy-start | bytes 3145732
  158.5 6.3 %copy-start.2 = (f32[2,1024]{1,0:T(2,128)S(1)}, f32[2,1024]{1,0:T(2,128)}, u32[]{:S(2)}) copy-start(f32[2,1024]{1,0:T(2,128)} %accum_ref.3) | copy-start | bytes 24580
  164.9 1.0 copy-start.1
